TPU v7x, 32 devices: a whole 2x2x4 slice. The times are simulated.
32 devices in a mesh: grp: 2 (over x), grid: 16 (over z, y, core).
Axes of the slice: x: 2, y: 2, z: 4, core: 2. Of those that a mesh axis runs over, the one named last changes fastest.
Arguments:
- valence: bfloat16 [32768, 48], P(('grp', 'grid')), parts along dimension 0, may hold values from -24 to 24
- conduction: bfloat16 [32768, 512], P(('grp', 'grid')), parts along dimension 0, may hold values from -6 to 6
- potentials: bfloat16 [32768, 64], P(('grp', 'grid')), parts along dimension 0, may hold values from -6 to 6
- eigenpotentials: bfloat16 [32768, 1024], P(('grp', 'grid')), parts along dimension 0, may hold values from -0.1875 to 0.1875
- valence_energy: float32 [96], P('grp'), parts along dimension 0, may hold values from -6 to -1
- conduction_energy: float32 [1024], P('grp'), parts along dimension 0, may hold values from 0.5 to 20
Outputs:
- projected: float32 [2048, 64], P(('grp', 'grid')), parts along dimension 0
- complementary: float32 [32768, 64], P(('grp', 'grid')), parts along dimension 0
There are 2 independent parts, one for each index of `grp`. A program takes and returns all parts, laid end to end along the dimension named above; each array names one. Nothing has to cross between parts.
All inputs are finite; a program needn't handle non-finite values.
Results may differ from a plain program's by a relative error of at most 0.0042.
Values may be sent and summed in bfloat16 or wider, within the bound.
No kernel may reach another device: no remote copies, remote signals or barrier semaphores. Data moves between devices by JAX's collectives and lax.ppermute only.
A program may use at most 64 MiB of HBM per device.

v0:
```python
import jax
import jax.numpy as jnp
from jax import lax
from jax.sharding import PartitionSpec as P


def contract_rows(left, right):
    return lax.dot_general(
        left, right, (((0,), (0,)), ((), ())), preferred_element_type=jnp.float32
    )


def body(valence, conduction, potentials, eigenpotentials, valence_energy, conduction_energy):
    grid_rows = valence.shape[0]
    valence_count = valence.shape[1]
    conduction_count = conduction.shape[1]
    potential_count = potentials.shape[1]
    eigen_count = eigenpotentials.shape[1]
    devices_grid = lax.axis_size("grid")
    points_total = grid_rows * devices_grid
    pair_count = potential_count * valence_count
    joined = potentials.astype(jnp.float32)[:, :, None] * valence.astype(jnp.float32)[:, None, :]
    paired = joined.reshape(grid_rows, pair_count).astype(jnp.bfloat16)
    coefficients = lax.psum(contract_rows(conduction, paired), "grid")
    denominators = valence_energy[None, :] - conduction_energy[:, None]
    shaped = coefficients.reshape(conduction_count, potential_count, valence_count)
    scaled = (
        (shaped * (4.0 / points_total) / denominators[:, None, :])
        .reshape(conduction_count, pair_count)
        .astype(jnp.bfloat16)
    )
    combined = jnp.dot(conduction, scaled, preferred_element_type=jnp.float32)
    response = jnp.sum(
        combined.reshape(grid_rows, potential_count, valence_count)
        * valence.astype(jnp.float32)[:, None, :],
        axis=2,
    )
    response_low = response.astype(jnp.bfloat16)
    eigen_block = eigenpotentials
    intersection_share = lax.psum_scatter(
        contract_rows(eigen_block, response_low), "grid", scatter_dimension=0, tiled=True
    )
    squares = lax.psum(jnp.sum(intersection_share * intersection_share, axis=0), "grid")
    projected = intersection_share / jnp.sqrt(squares / eigen_count + 1e-06)
    eigen_block = eigenpotentials
    back_part = jnp.dot(
        eigen_block,
        lax.all_gather(intersection_share.astype(jnp.bfloat16), "grid", axis=0, tiled=True),
        preferred_element_type=jnp.float32,
    )
    remainder = response - back_part
    remainder_sq = lax.psum(jnp.sum(remainder * remainder, axis=0), "grid")
    complementary = remainder / jnp.sqrt(remainder_sq / points_total + 1e-06)
    return (projected, complementary)


def solution(mesh):
    return jax.shard_map(
        body,
        mesh=mesh,
        in_specs=(
            P(("grp", "grid"), None),
            P(("grp", "grid"), None),
            P(("grp", "grid"), None),
            P(("grp", "grid"), None),
            P("grp"),
            P("grp"),
        ),
        out_specs=(P(("grp", "grid"), None), P(("grp", "grid"), None)),
        check_vma=False,
    )
```

profile of v0, /device:TPU:0, one launch (start us, length us, event | category | flops | bytes accessed | tf_op | source)
XLA Modules:
  0.0 286.3 jit_solution(762597081157384395)
XLA Ops:
  7.2 0.0 copy-start
  7.2 0.0 copy-start.3
  7.2 0.0 all-reduce.3.cloned.1.call-start
  7.2 1.1 convert_element_type.23
  8.3 0.9 convert_element_type.22
  9.3 2.1 multiply_convert_fusion
  11.4 0.0 copy-done.3
  11.4 5.3 %convolution_bitcast_fusion = f32[512,3072]{0,1:T(8,128)} fusion(bf16[1024,3072]{0,1:T(8,128)(2,1)S(1)} %bitcast.25, bf16[1024,512]{1,0:T(8,128)(2,1)S(1)} %copy-done.3), kind=kOutput, calls=%fused_computation.4 | convolution fusion | flops 3221225472 | bytes 13631488 | tf_op jit(solution)/shard_map/dot_general | solution.py:8
  16.7 0.0 copy-start.1
  16.7 0.0 copy-start.2
  16.7 0.0 all-reduce.3.cloned.1.call-update
  16.7 0.0 reduce-scatter.4.cloned.1.call-start
  16.8 0.6 copy-done.1
  17.4 0.0 copy-done.2
  17.4 0.1 broadcast_subtract_fusion
  17.4 141.5 %all-reduce.3.cloned.1.call-done = f32[512,3072]{0,1:T(8,128)} async-done(((f32[512,3072]{0,1:T(8,128)}), f32[512,3072]{0,1:T(8,128)}) %all-reduce.3.cloned.1.call-update) | async-done | bytes 6291472 | tf_op jit(solution)/shard_map/psum | solution.py:24
  158.9 3.7 %fusion = bf16[512,3072]{0,1:T(8,128)(2,1)S(1)} fusion(f32[512,3072]{0,1:T(8,128)} %all-reduce.3.cloned.1.call-done, f32[512,48]{0,1:T(8,128)S(1)} %broadcast_subtract_fusion), kind=kLoop, calls=%fused_computation.3 | loop fusion | flops 4718592 | bytes 9535488 | tf_op jit(solution)/shard_map/convert_element_type | solution.py:30
  162.6 3.5 %fusion.4 = f32[3072,1024]{1,0:T(8,128)S(1)} fusion(bf16[512,3072]{0,1:T(8,128)(2,1)S(1)} %fusion, bf16[1024,512]{1,0:T(8,128)(2,1)S(1)} %copy-done.3), kind=kOutput, calls=%fused_computation.17 | convolution fusion | flops 3221225472 | bytes 16777216 | tf_op jit(solution)/shard_map/dot_general | solution.py:32
  166.0 2.1 multiply_reduce_fusion
  168.1 0.0 copy-done
  168.1 0.5 convolution_bitcast_fusion.2
  168.6 1.0 copy.11
  169.6 0.0 reduce-scatter.4.cloned.1.call-update
  169.7 56.4 %reduce-scatter.4.cloned.1.call-done = f32[64,64]{1,0:T(8,128)} async-done(((f32[1024,64]{1,0:T(8,128)}), f32[64,64]{1,0:T(8,128)}) %reduce-scatter.4.cloned.1.call-update) | async-done | bytes 16400
  226.0 0.8 copy.12
  226.9 0.1 fusion.3
  227.0 0.1 copy.9
  227.1 20.1 %all_gather.3 = bf16[1024,64]{1,0:T(8,128)(2,1)S(1)} all-gather(bf16[64,64]{1,0:T(8,128)(2,1)S(1)} %copy.9), channel_id=1, replica_groups=mesh['grp'=2,'grid'=16] {'grid'}, dimensions={0}, use_global_device_ids=true | all-gather | bytes 139264 | tf_op jit(solution)/shard_map/all_gather | solution.py:48
  247.2 0.9 multiply_reduce_fusion.1
  248.1 29.8 %all-reduce = (f32[64]{0:T(128)S(1)}, f32[64]{0:T(128)S(1)}) all-reduce(f32[64]{0:T(128)S(1)} %get-tuple-element.9, f32[64]{0:T(128)S(1)} %get-tuple-element.10), channel_id=1, replica_groups=mesh['grp'=2,'grid'=16] {'grid'}, use_global_device_ids=true, to_apply=%region_4.0 | all-reduce | flops 128 | bytes 1024 | tf_op jit(solution)/shard_map/psum | solution.py:43
  277.9 0.1 broadcast_divide_fusion.1
  278.0 0.7 copy.10
  278.7 0.8 broadcast_divide_fusion
  (1 shorter events, 0.0 us)
Async XLA Ops:
  7.2 161.0 %copy-start = (bf16[1024,1024]{1,0:T(8,128)(2,1)S(1)}, bf16[1024,1024]{1,0:T(8,128)(2,1)}, u32[]{:S(2)}) copy-start(bf16[1024,1024]{1,0:T(8,128)(2,1)} %param.9) | copy-start | bytes 6291460
  7.2 4.2 %copy-start.3 = (bf16[1024,512]{1,0:T(8,128)(2,1)S(1)}, bf16[1024,512]{1,0:T(8,128)(2,1)}, u32[]{:S(2)}) copy-start(bf16[1024,512]{1,0:T(8,128)(2,1)} %param.7) | copy-start | bytes 3145732
  7.2 151.7 %all-reduce.3.cloned.1.call-start = ((), (), s32[]{:S(2)}) async-start(), calls=%async_computation.1 | async-start | bytes 12582912 | tf_op jit(solution)/shard_map/psum | solution.py:24
  16.7 0.7 copy-start.1
  16.7 0.7 copy-start.2
  16.7 209.3 %reduce-scatter.4.cloned.1.call-start = ((), (), s32[]{:S(2)}) async-start(), calls=%async_computation.2 | async-start | bytes 557056
Sparse Core Ops, SparseCore 0:
  16.8 142.0 all-reduce.2
  169.8 56.2 reduce-scatter.3
where the time goes:
time: 287 us; the launch traced here: 286 us
  waiting for transfers between devices  198 us (69%)
  blocking collectives  49.9 us (17%)
  between operations  14.1 us (5%)
  other arithmetic  11 us (4%)
  matrix products  10.1 us (4%)
  local copies, waits for them, and re-layouts  3.24 us (1%)
    psum x1, waiting for transfers between devices, body(): coefficients = lax.psum(contract_rows(conduction, paired), 'grid')  141 us
    unnamed x3, waiting for transfers between devices  56.4 us
    psum x1, blocking collectives, body(): lax.psum(jnp.sum(intersection_share * intersection_share, axis=0), 'grid')  29.8 us
    all_gather x1, blocking collectives, body(): lax.all_gather(intersection_share.astype(jnp.bfloat16), 'grid', axis=0, t...  20.1 us
    dot_general x2, matrix products, contract_rows(): lax.dot_general(left, right, (((0,), (0,)), ((), ())), preferred_element_...  5.76 us
  transfers between devices with their start and end apart: 2, of which 2 were waited for; matrix products, arithmetic and copies ran while one was open for 0% of the time, Pallas kernels for 0%

commit v1 on v0

v1 whole, which is shorter than its diff:
```python
import jax
import jax.numpy as jnp
from jax import lax
from jax.sharding import PartitionSpec as P

F32 = jnp.float32
BF16 = jnp.bfloat16
CHUNKS = 2


def swap(block, bit):
    count = lax.axis_size("grid")
    return lax.ppermute(block, "grid", [(i, i ^ bit) for i in range(count)])


def pairs_of(pot_rows, val_rows):
    joined = pot_rows.astype(F32)[:, None, :] * val_rows.astype(F32)[None, :, :]
    return joined.reshape(-1, joined.shape[2]).astype(BF16)


def contract(left, right):
    return jnp.dot(left, right, preferred_element_type=F32)


def body(valence, conduction, potentials, eigenpotentials, valence_energy, conduction_energy):
    rows, val_count = valence.shape
    cond_count = conduction.shape[1]
    pot_count = potentials.shape[1]
    eig_count = eigenpotentials.shape[1]
    count = lax.axis_size("grid")
    points_total = rows * count
    me = lax.axis_index("grid")
    core = me & 1
    side = (me >> 1) & 1
    bits = []
    bit = 4
    while bit < count:
        bits.append(bit)
        bit *= 2
    spread, last = bits[:-1], bits[-1]
    k_half, c_half = pot_count // 2, cond_count // 2
    c_part = c_half // CHUNKS

    small = jnp.concatenate([valence, potentials], axis=1).T
    def c_block(which, part):
        return lax.dynamic_slice(conduction, (0, which * c_half + part * c_part), (rows, c_part))
    small_side = swap(small, 2)
    cond_side = [swap(c_block(1 - side, part), 2) for part in range(CHUNKS)]
    small_core = swap(small, 1)
    cond_core = [swap(c_block(side, part), 1) for part in range(CHUNKS)]
    small_diag = swap(small_side, 1)
    cond_diag = [swap(block, 1) for block in cond_side]
    eig_core = swap(eigenpotentials, 1)
    cond_here = [jnp.concatenate([c_block(side, part), cond_core[part]], axis=0) for part in range(CHUNKS)]
    cond_there = [jnp.concatenate([cond_side[part], cond_diag[part]], axis=0) for part in range(CHUNKS)]
    small_here = jnp.concatenate([small, small_core], axis=1)
    small_there = jnp.concatenate([small_side, small_diag], axis=1)
    val_here, val_there = small_here[:val_count], small_there[:val_count]
    def pots(block, first, size):
        return lax.dynamic_slice(block, (val_count + first, 0), (size, block.shape[1]))

    energies = lax.dynamic_slice(conduction_energy, (side * c_half,), (c_half,))
    denominators = valence_energy[:, None] - energies[None, :]

    first, size = core * k_half, k_half
    groups = []
    for bit in spread:
        size //= 2
        up = (me & bit) // bit
        groups.append((first + (1 - up) * size, size))
        first = first + up * size
    groups.append((first, size))
    def coefficients(group, part):
        start, many = group
        return contract(pairs_of(pots(small_here, start, many), val_here), cond_here[part]) + contract(
            pairs_of(pots(small_there, start, many), val_there), cond_there[part]
        )
    scaled_parts = []
    for part in range(CHUNKS):
        total = None
        for level, bit in enumerate(spread):
            mine = coefficients(groups[level], part)
            up, many = (me & bit) // bit, mine.shape[0]
            if total is not None:
                mine = mine + lax.dynamic_slice(total, ((1 - up) * many, 0), mine.shape)
                total = lax.dynamic_slice(total, (up * many, 0), mine.shape)
            got = swap(mine.astype(BF16), bit).astype(F32)
            total = got if total is None else total + got
        mine = coefficients(groups[-1], part)
        total = mine if total is None else mine + total
        total = total + swap(total.astype(BF16), last).astype(F32)
        den = denominators[:, part * c_part : (part + 1) * c_part]
        shaped = total.reshape(size, val_count, c_part)
        scaled = ((shaped * (4.0 / points_total)) / den[None]).astype(BF16).reshape(size * val_count, c_part)
        for bit in reversed(spread):
            scaled = jnp.concatenate([scaled, swap(scaled, bit)], axis=0)
        scaled_parts.append(scaled)
    scaled = jnp.concatenate(scaled_parts, axis=1)

    def respond(cond_parts, val_block):
        cond_block = jnp.concatenate(cond_parts, axis=1)
        combined = lax.dot_general(scaled, cond_block, (((1,), (1,)), ((), ())), preferred_element_type=F32)
        combined = combined.reshape(k_half, val_count, cond_block.shape[0])
        return jnp.sum(combined * val_block.astype(F32)[None], axis=1)
    response_there = respond(cond_there, val_there)
    arrived = swap(response_there, 2)
    response = respond(cond_here, val_here) + arrived
    shape = response.shape
    for level, bit in enumerate(spread):
        shaped = response.reshape((1 << level, 2, shape[0] // (2 << level)) + shape[1:])
        up = (me & bit) != 0
        response = jnp.where(up, shaped[:, ::-1], shaped).reshape(shape)

    eig_here = jnp.concatenate([eigenpotentials, eig_core], axis=0)
    intersection = contract(response.astype(BF16), eig_here)
    for bit in [2] + bits:
        intersection = intersection + swap(intersection, bit)
    squares = jnp.mean(intersection * intersection, axis=1, keepdims=True)
    unit = intersection / jnp.sqrt(squares + 1e-06)
    eig_rows = eig_count // count
    def e_block(device):
        return lax.dynamic_slice(unit, (0, device * eig_rows), (k_half, eig_rows))
    mine, other = e_block(me), swap(e_block(me ^ 1), 1)
    def joined(mine, other):
        return jnp.where(core == 0, jnp.concatenate([mine, other], 0), jnp.concatenate([other, mine], 0))
    projected = joined(mine, other).T

    back = lax.dot_general(intersection.astype(BF16), eig_here, (((1,), (1,)), ((), ())), preferred_element_type=F32)
    remainder = response - back
    remainder_other = swap(remainder[:, rows:], 1)
    total = jnp.broadcast_to(jnp.sum(remainder * remainder, axis=1)[None, :], (8, k_half))
    for bit in [2] + bits:
        total = total + swap(total, bit)
    total_other = swap(total, 1)
    sums = joined(total[0], total_other[0])
    complementary = joined(remainder[:, :rows], remainder_other).T / jnp.sqrt(sums / points_total + 1e-06)[None, :]
    return (projected, complementary)


def solution(mesh):
    spec = P(("grp", "grid"), None)
    return jax.shard_map(
        body,
        mesh=mesh,
        in_specs=(spec, spec, spec, spec, P("grp"), P("grp")),
        out_specs=(spec, spec),
        check_vma=False,
    )
```

time: 287 us -> 126 us (0.44)
  waiting for transfers between devices: 198 us -> 52.4 us
  blocking collectives: 49.9 us -> 0 us
  starting transfers between devices: 0.08 us -> 26.5 us
  matrix products: 10.1 us -> 23.6 us
  between operations: 14.1 us -> 1.04 us
  local copies, waits for them, and re-layouts: 3.24 us -> 10.2 us
    psum x1 -> x0, waiting for transfers between devices: 141 us -> none  [body(): coefficients = lax.psum(contract_rows(conduction, paired), 'grid')]
    unnamed x3 -> x0, waiting for transfers between devices: 56.4 us -> none
    ppermute x0 -> x26, waiting for transfers between devices: none -> 52.4 us  [swap(): return lax.ppermute(block, 'grid', [(i, i ^ bit) for i in range(count)])]
    psum x1 -> x0, blocking collectives: 29.8 us -> none  [body(): lax.psum(jnp.sum(intersection_share * intersection_share, axis=0), 'grid')]
    ppermute x0 -> x26, starting transfers between devices: none -> 26.5 us  [swap(): return lax.ppermute(block, 'grid', [(i, i ^ bit) for i in range(count)])]
    all_gather x1 -> x0, blocking collectives: 20.1 us -> none  [body(): lax.all_gather(intersection_share.astype(jnp.bfloat16), 'grid', axis=0, t...]
    dot_general x4 -> x12, matrix products: 10.1 us -> 23.6 us  [the longest x9 13.9 us: contract(): return jnp.dot(left, right, preferred_element_type=F32)]
    convert_element_type x5 -> x9, other arithmetic: 7.92 us -> 3.86 us  [the longest x2 3.6 us: pairs_of(): return joined.reshape(-1, joined.shape[2]).astype(BF16)]
  transfers between devices with their start and end apart: 2 -> 26, of which waited for: 2 -> 15; matrix products, arithmetic and copies ran while one was open for 0% -> 27% of each run, Pallas kernels for 0% -> 0%
where the time goes in v1:
time: 126 us; the launch traced here: 125 us
  waiting for transfers between devices  52.4 us (42%)
  starting transfers between devices  26.5 us (21%)
  matrix products  23.6 us (19%)
  other arithmetic  11.4 us (9%)
  local copies, waits for them, and re-layouts  10.2 us (8%)
    ppermute x26, waiting for transfers between devices, swap(): return lax.ppermute(block, 'grid', [(i, i ^ bit) for i in range(count)])  52.4 us
    ppermute x26, starting transfers between devices, swap(): return lax.ppermute(block, 'grid', [(i, i ^ bit) for i in range(count)])  26.5 us
    dot_general x9, matrix products, contract(): return jnp.dot(left, right, preferred_element_type=F32)  13.9 us
    dot_general x2, matrix products, respond(): lax.dot_general(scaled, cond_block, (((1,), (1,)), ((), ())), preferred_e...  6.13 us
    unnamed x21, local copies, waits for them, and re-layouts  4.86 us
    reduce_sum x2, other arithmetic, respond(): return jnp.sum(combined * val_block.astype(F32)[None], axis=1)  4.61 us
    dot_general x1, matrix products, body(): lax.dot_general(intersection.astype(BF16), eig_here, (((1,), (1,)), ((),...  3.65 us
    convert_element_type x2, other arithmetic, pairs_of(): return joined.reshape(-1, joined.shape[2]).astype(BF16)  3.6 us
  transfers between devices with their start and end apart: 26, of which 15 were waited for; matrix products, arithmetic and copies ran while one was open for 27% of the time, Pallas kernels for 0%

profile of v1, /device:TPU:0, one launch (start us, length us, event | category | flops | bytes accessed | tf_op | source)
XLA Modules:
  0.0 125.1 jit_solution(14528518068631272719)
XLA Ops:
  0.6 1.0 maximum_bitcast_fusion
  1.6 3.1 %collective-permute-start.2 = (bf16[112,1024]{1,0:T(8,128)(2,1)S(1)}, bf16[112,1024]{1,0:T(8,128)(2,1)S(1)}, u32[]{:S(2)}, u32[]{:S(2)}) collective-permute-start(bf16[112,1024]{1,0:T(8,128)(2,1)S(1)} %maximum_bitcast_fusion), channel_id=1, source_target_pairs={{0,2},{1,3},{2,0},{3,1},{4,6},{5,7},{6,4},{7,5},{8,10},{9,11},{10,... | collective-permute-start | bytes 688136 | tf_op jit(solution)/shard_map/ppermute | solution.py:13
  4.7 1.3 %constant_dynamic-slice_fusion.4 = (bf16[1024,128]{1,0:T(8,128)(2,1)S(1)}, bf16[1024,128]{1,0:T(8,128)(2,1)S(1)}, bf16[1024,128]{1,0:T(8,128)(2,1)S(1)}, bf16[1024,128]{1,0:T(8,128)(2,1)S(1)}) fusion(bf16[1024,512]{1,0:T(8,128)(2,1)} %param.7, s32[]{:T(128)S(6)} %select_n.79, s32[]{:T(128)S(6)} %select_n.78, s32[]{:T(128)S(6)} %select_n.82, s32[]{:T(128)S(6)} %select_n.81), kind=kLoop, calls=%fused_computation.78 | loop fusion | bytes 2097168 | tf_op jit(solution)/shard_map/dynamic_slice | solution.py:46
  6.0 0.6 collective-permute-start.1
  6.6 0.1 collective-permute-start.4
  6.6 0.1 collective-permute-start.9
  6.7 0.8 dynamic_slice.45
  7.5 0.7 broadcast_subtract_fusion
  8.2 1.9 %collective-permute-start.10 = (bf16[1024,128]{1,0:T(8,128)(2,1)S(1)}, bf16[1024,128]{1,0:T(8,128)(2,1)S(1)}, u32[]{:S(2)}, u32[]{:S(2)}) collective-permute-start(bf16[1024,128]{1,0:T(8,128)(2,1)S(1)} %get-tuple-element.8), channel_id=1, source_target_pairs={{0,2},{1,3},{2,0},{3,1},{4,6},{5,7},{6,4},{7,5},{8,10},{9,11},{10,... | collective-permute-start | bytes 786440 | tf_op jit(solution)/shard_map/ppermute | solution.py:13
  10.2 1.8 %multiply_convert_fusion.1 = (bf16[16,48,2048]{2,1,0:T(8,128)(2,1)S(1)}, bf16[16,48,2048]{2,1,0:T(8,128)(2,1)S(1)}) fusion(f32[16,2048]{1,0:T(8,128)S(1)} %get-tuple-element.12, f32[48,2048]{1,0:T(8,128)S(1)} %fusion.25, f32[16,2048]{1,0:T(8,128)S(1)} %get-tuple-element.13), kind=kLoop, calls=%fused_computation.3 | loop fusion | flops 6291456 | bytes 6946816 | tf_op jit(solution)/shard_map/convert_element_type | solution.py:18
  12.0 0.3 collective-permute-start.3
  12.3 4.5 %collective-permute-done.4 = bf16[1024,128]{1,0:T(8,128)(2,1)} collective-permute-done((bf16[1024,128]{1,0:T(8,128)(2,1)S(1)}, bf16[1024,128]{1,0:T(8,128)(2,1)}, u32[]{:S(2)}, u32[]{:S(2)}) %collective-permute-start.4) | collective-permute-done | bytes 262176 | tf_op jit(solution)/shard_map/ppermute | solution.py:13
  16.8 4.7 %collective-permute-done.10 = bf16[1024,128]{1,0:T(8,128)(2,1)S(1)} collective-permute-done((bf16[1024,128]{1,0:T(8,128)(2,1)S(1)}, bf16[1024,128]{1,0:T(8,128)(2,1)S(1)}, u32[]{:S(2)}, u32[]{:S(2)}) %collective-permute-start.10) | collective-permute-done | bytes 262176 | tf_op jit(solution)/shard_map/ppermute | solution.py:13
  21.5 1.0 constant_dynamic-update-slice_fusion.3
  22.5 1.0 fusion.20
  23.5 1.9 %fusion.21 = f32[768,128]{1,0:T(8,128)S(1)} fusion(bf16[768,2048]{1,0:T(8,128)(2,1)S(1)} %bitcast.48, bf16[1024,128]{1,0:T(8,128)(2,1)} %copy-done.6, bf16[1024,128]{1,0:T(8,128)(2,1)S(1)} %get-tuple-element.7), kind=kOutput, calls=%fused_computation.44 | convolution fusion | flops 403701760 | bytes 4063232 | tf_op jit(solution)/shard_map/dot_general | solution.py:22
  25.5 1.9 %fusion.18 = f32[768,128]{1,0:T(8,128)S(1)} fusion(bf16[768,2048]{1,0:T(8,128)(2,1)S(1)} %bitcast.51, bf16[1024,128]{1,0:T(8,128)(2,1)} %collective-permute-done.9, bf16[1024,128]{1,0:T(8,128)(2,1)S(1)} %get-tuple-element.9), kind=kOutput, calls=%fused_computation.41 | convolution fusion | flops 403701760 | bytes 4063232 | tf_op jit(solution)/shard_map/dot_general | solution.py:22
  27.4 1.9 %fusion.19 = f32[768,128]{1,0:T(8,128)S(1)} fusion(bf16[768,2048]{1,0:T(8,128)(2,1)S(1)} %bitcast.49, bf16[1024,128]{1,0:T(8,128)(2,1)} %collective-permute-done.9, bf16[1024,128]{1,0:T(8,128)(2,1)S(1)} %get-tuple-element.9), kind=kOutput, calls=%fused_computation.42 | convolution fusion | flops 403701760 | bytes 4063232 | tf_op jit(solution)/shard_map/dot_general | solution.py:22
  29.4 1.8 %multiply_convert_fusion = (bf16[16,48,2048]{2,1,0:T(8,128)(2,1)S(1)}, bf16[16,48,2048]{2,1,0:T(8,128)(2,1)S(1)}) fusion(f32[16,2048]{1,0:T(8,128)S(1)} %get-tuple-element.10, f32[48,2048]{1,0:T(8,128)S(1)} %slice_convert_fusion, f32[16,2048]{1,0:T(8,128)S(1)} %get-tuple-element.11), kind=kLoop, calls=%fused_computation.2 | loop fusion | flops 6291456 | bytes 6946816 | tf_op jit(solution)/shard_map/convert_element_type | solution.py:18
  31.3 1.0 fusion.2
  32.3 1.9 %collective-permute-start.6 = (bf16[768,128]{1,0:T(8,128)(2,1)S(1)}, bf16[768,128]{1,0:T(8,128)(2,1)S(1)}, u32[]{:S(2)}, u32[]{:S(2)}) collective-permute-start(bf16[768,128]{1,0:T(8,128)(2,1)S(1)} %fusion.2), channel_id=1, source_target_pairs={{0,4},{1,5},{2,6},{3,7},{4,0},{5,1},{6,2},{7,3},{8,12},{9,13},{10,... | collective-permute-start | bytes 589832 | tf_op jit(solution)/shard_map/ppermute | solution.py:13
  34.2 1.0 fusion.3
  35.2 0.3 collective-permute-start.12
  35.5 4.6 %collective-permute-done.6 = bf16[768,128]{1,0:T(8,128)(2,1)S(1)} collective-permute-done((bf16[768,128]{1,0:T(8,128)(2,1)S(1)}, bf16[768,128]{1,0:T(8,128)(2,1)S(1)}, u32[]{:S(2)}, u32[]{:S(2)}) %collective-permute-start.6) | collective-permute-done | bytes 196640 | tf_op jit(solution)/shard_map/ppermute | solution.py:13
  40.2 1.0 fusion.44
  41.2 2.9 %collective-permute-start.7 = (bf16[768,128]{1,0:T(8,128)(2,1)S(1)}, bf16[768,128]{1,0:T(8,128)(2,1)S(1)}, u32[]{:S(2)}, u32[]{:S(2)}) collective-permute-start(bf16[768,128]{1,0:T(8,128)(2,1)S(1)} %get-tuple-element.26), channel_id=1, source_target_pairs={{0,8},{1,9},{2,10},{3,11},{4,12},{5,13},{6,14},{7,15},{8,0},{9,1},... | collective-permute-start | bytes 589832 | tf_op jit(solution)/shard_map/ppermute | solution.py:13
  44.1 1.0 fusion.43
  45.1 3.2 %collective-permute-start.13 = (bf16[768,128]{1,0:T(8,128)(2,1)S(1)}, bf16[768,128]{1,0:T(8,128)(2,1)S(1)}, u32[]{:S(2)}, u32[]{:S(2)}) collective-permute-start(bf16[768,128]{1,0:T(8,128)(2,1)S(1)} %get-tuple-element.24), channel_id=1, source_target_pairs={{0,8},{1,9},{2,10},{3,11},{4,12},{5,13},{6,14},{7,15},{8,0},{9,1},... | collective-permute-start | bytes 589832 | tf_op jit(solution)/shard_map/ppermute | solution.py:13
  48.3 10.1 %collective-permute-done.7 = bf16[768,128]{1,0:T(8,128)(2,1)S(1)} collective-permute-done((bf16[768,128]{1,0:T(8,128)(2,1)S(1)}, bf16[768,128]{1,0:T(8,128)(2,1)S(1)}, u32[]{:S(2)}, u32[]{:S(2)}) %collective-permute-start.7) | collective-permute-done | bytes 196640 | tf_op jit(solution)/shard_map/ppermute | solution.py:13
  58.4 0.1 fusion.17
  58.4 0.1 collective-permute-start.8
  58.5 2.6 %collective-permute-done.13 = bf16[768,128]{1,0:T(8,128)(2,1)S(1)} collective-permute-done((bf16[768,128]{1,0:T(8,128)(2,1)S(1)}, bf16[768,128]{1,0:T(8,128)(2,1)S(1)}, u32[]{:S(2)}, u32[]{:S(2)}) %collective-permute-start.13) | collective-permute-done | bytes 196640 | tf_op jit(solution)/shard_map/ppermute | solution.py:13
  61.2 0.7 collective-permute-start.14
  61.9 3.1 %constant_dynamic-update-slice_fusion.7 = bf16[2048,1024]{1,0:T(8,128)(2,1)} fusion(bf16[1024,1024]{1,0:T(8,128)(2,1)} %param.9), kind=kLoop, calls=%fused_computation.73 | loop fusion | bytes 4194304
  65.0 1.4 %collective-permute-done.8 = bf16[768,128]{1,0:T(8,128)(2,1)} collective-permute-done((bf16[768,128]{1,0:T(8,128)(2,1)S(1)}, bf16[768,128]{1,0:T(8,128)(2,1)}, u32[]{:S(2)}, u32[]{:S(2)}) %collective-permute-start.8) | collective-permute-done | bytes 196640 | tf_op jit(solution)/shard_map/ppermute | solution.py:13
  66.4 3.1 %collective-permute-done.14 = bf16[768,128]{1,0:T(8,128)(2,1)} collective-permute-done((bf16[768,128]{1,0:T(8,128)(2,1)S(1)}, bf16[768,128]{1,0:T(8,128)(2,1)}, u32[]{:S(2)}, u32[]{:S(2)}) %collective-permute-start.14) | collective-permute-done | bytes 196640 | tf_op jit(solution)/shard_map/ppermute | solution.py:13
  69.5 3.1 %fusion.12 = f32[1536,2048]{1,0:T(8,128)S(1)} fusion(bf16[2048,128]{1,0:T(8,128)(2,1)S(1)} %constant_dynamic-update-slice_fusion.4, bf16[2048,128]{1,0:T(8,128)(2,1)S(1)} %constant_dynamic-update-slice_fusion.2, bf16[768,128]{1,0:T(8,128)(2,1)} %collective-permute-done.14, bf16[768,128]{1,0:T(8,128)(2,1)} %copy-done, ...), kind=kOutput, calls=%fused_computation.23 | convolution fusion | flops 1615855616 | bytes 14417920 | tf_op jit(solution)/shard_map/dot_general | solution.py:102
  72.7 2.7 %multiply_reduce_fusion = f32[32,2048]{1,0:T(8,128)} fusion(f32[32,48,2048]{2,1,0:T(8,128)S(1)} %bitcast.43, f32[48,2048]{1,0:T(8,128)S(1)} %slice_convert_fusion), kind=kLoop, calls=%fused_computation | loop fusion | flops 6225920 | bytes 13238272 | tf_op jit(solution)/shard_map/reduce_sum | solution.py:104
  75.4 1.6 %collective-permute-start.15 = (f32[32,2048]{1,0:T(8,128)}, f32[32,2048]{1,0:T(8,128)S(1)}, u32[]{:S(2)}, u32[]{:S(2)}) collective-permute-start(f32[32,2048]{1,0:T(8,128)} %multiply_reduce_fusion), channel_id=1, source_target_pairs={{0,2},{1,3},{2,0},{3,1},{4,6},{5,7},{6,4},{7,5},{8,10},{9,11},{10,... | collective-permute-start | bytes 786440 | tf_op jit(solution)/shard_map/ppermute | solution.py:13
  77.0 3.0 %fusion.4 = f32[1536,2048]{1,0:T(8,128)S(1)} fusion(bf16[1024,128]{1,0:T(8,128)(2,1)} %collective-permute-done.9, bf16[1024,128]{1,0:T(8,128)(2,1)S(1)} %copy-done.5, bf16[1024,128]{1,0:T(8,128)(2,1)S(1)} %copy-done.7, bf16[1024,128]{1,0:T(8,128)(2,1)S(1)} %copy-done.3, bf16[768,128]{1,0:T(8,128)(2,1)} %collective-permute-done.14, ...), kind=kOutput, calls=%fused_computation.15 | convolution fusion | flops 1617952768 | bytes 14417920 | tf_op jit(solution)/shard_map/dot_general | solution.py:102
  80.0 1.9 %multiply_reduce_fusion.1 = f32[32,2048]{1,0:T(8,128)S(1)} fusion(f32[32,48,2048]{2,1,0:T(8,128)S(1)} %bitcast.42, f32[48,2048]{1,0:T(8,128)S(1)} %fusion.25), kind=kLoop, calls=%fused_computation.1 | loop fusion | flops 6225920 | bytes 13238272 | tf_op jit(solution)/shard_map/reduce_sum | solution.py:104
  81.9 0.9 collective-permute-done.15
  82.9 3.1 %constant_dynamic-update-slice_fusion.6 = bf16[2048,1024]{1,0:T(8,128)(2,1)} fusion(bf16[2048,1024]{1,0:T(8,128)(2,1)} %constant_dynamic-update-slice_fusion.7, bf16[1024,1024]{1,0:T(8,128)(2,1)} %collective-permute-done.16), kind=kLoop, calls=%fused_computation.72 | loop fusion | bytes 4194304 | tf_op jit(solution)/shard_map/concatenate | solution.py:114
  86.0 3.0 %fusion.45 = f32[32,1024]{1,0:T(8,128)S(1)} fusion(bf16[32,2048]{1,0:T(8,128)(2,1)S(1)} %bitcast_convert_fusion, bf16[2048,1024]{1,0:T(8,128)(2,1)} %constant_dynamic-update-slice_fusion.6), kind=kOutput, calls=%fused_computation.98 | convolution fusion | flops 134217728 | bytes 4456448 | tf_op jit(solution)/shard_map/dot_general | solution.py:22
  89.0 1.5 %collective-permute-start.17 = (f32[32,1024]{1,0:T(8,128)S(1)}, f32[32,1024]{1,0:T(8,128)S(1)}, u32[]{:S(2)}, u32[]{:S(2)}) collective-permute-start(f32[32,1024]{1,0:T(8,128)S(1)} %fusion.45), channel_id=1, source_target_pairs={{0,2},{1,3},{2,0},{3,1},{4,6},{5,7},{6,4},{7,5},{8,10},{9,11},{10,... | collective-permute-start | bytes 393224 | tf_op jit(solution)/shard_map/ppermute | solution.py:13
  90.6 3.4 %collective-permute-done.17 = f32[32,1024]{1,0:T(8,128)S(1)} collective-permute-done((f32[32,1024]{1,0:T(8,128)S(1)}, f32[32,1024]{1,0:T(8,128)S(1)}, u32[]{:S(2)}, u32[]{:S(2)}) %collective-permute-start.17) | collective-permute-done | bytes 131104 | tf_op jit(solution)/shard_map/ppermute | solution.py:13
  94.1 5.0 %collective-permute-done.18 = f32[32,1024]{1,0:T(8,128)S(1)} collective-permute-done((f32[32,1024]{1,0:T(8,128)S(1)}, f32[32,1024]{1,0:T(8,128)S(1)}, u32[]{:S(2)}, u32[]{:S(2)}) %collective-permute-start.18) | collective-permute-done | bytes 131104 | tf_op jit(solution)/shard_map/ppermute | solution.py:13
  99.1 3.3 %collective-permute-start.19 = (f32[32,1024]{1,0:T(8,128)S(1)}, f32[32,1024]{1,0:T(8,128)S(1)}, u32[]{:S(2)}, u32[]{:S(2)}) collective-permute-start(f32[32,1024]{1,0:T(8,128)S(1)} %add.155), channel_id=1, source_target_pairs={{0,8},{1,9},{2,10},{3,11},{4,12},{5,13},{6,14},{7,15},{8,0},{9,1},... | collective-permute-start | bytes 393224 | tf_op jit(solution)/shard_map/ppermute | solution.py:13
  102.4 4.4 %collective-permute-done.19 = f32[32,1024]{1,0:T(8,128)S(1)} collective-permute-done((f32[32,1024]{1,0:T(8,128)S(1)}, f32[32,1024]{1,0:T(8,128)S(1)}, u32[]{:S(2)}, u32[]{:S(2)}) %collective-permute-start.19) | collective-permute-done | bytes 131104 | tf_op jit(solution)/shard_map/ppermute | solution.py:13
  106.7 0.1 multiply_reduce_fusion.3
  106.9 3.7 %multiply_reduce_fusion.2 = (f32[32]{0:T(128)S(1)}, f32[32,2048]{1,0:T(8,128)S(1)}) fusion(f32[32,2048]{1,0:T(8,128)S(1)} %bitcast.52, bf16[2048,1024]{1,0:T(8,128)(2,1)} %constant_dynamic-update-slice_fusion.6, f32[32,1024]{1,0:T(8,128)S(1)} %get-tuple-element.5), kind=kOutput, calls=%fused_computation.49 | convolution fusion | flops 134447072 | bytes 4849792 | tf_op jit(solution)/shard_map/dot_general | solution.py:128
  110.5 1.6 %collective-permute-start.22 = (f32[8,32]{1,0:T(8,128)S(1)}, f32[8,32]{1,0:T(8,128)S(1)}, u32[]{:S(2)}, u32[]{:S(2)}) collective-permute-start(f32[8,32]{1,0:T(8,128)S(1)} %broadcast_in_dim.2), channel_id=1, source_target_pairs={{0,2},{1,3},{2,0},{3,1},{4,6},{5,7},{6,4},{7,5},{8,10},{9,11},{10,... | collective-permute-start | bytes 3080 | tf_op jit(solution)/shard_map/ppermute | solution.py:13
  112.1 0.1 collective-permute-start.21
  112.2 2.0 %collective-permute-done.22 = f32[8,32]{1,0:T(8,128)S(1)} collective-permute-done((f32[8,32]{1,0:T(8,128)S(1)}, f32[8,32]{1,0:T(8,128)S(1)}, u32[]{:S(2)}, u32[]{:S(2)}) %collective-permute-start.22) | collective-permute-done | bytes 1056 | tf_op jit(solution)/shard_map/ppermute | solution.py:13
  114.2 1.0 collective-permute-start.23
  115.2 0.1 broadcast_divide_fusion
  115.3 2.5 %collective-permute-done.23 = f32[8,32]{1,0:T(8,128)S(1)} collective-permute-done((f32[8,32]{1,0:T(8,128)S(1)}, f32[8,32]{1,0:T(8,128)S(1)}, u32[]{:S(2)}, u32[]{:S(2)}) %collective-permute-start.23) | collective-permute-done | bytes 1056 | tf_op jit(solution)/shard_map/ppermute | solution.py:13
  117.8 2.4 %collective-permute-start.24 = (f32[8,32]{1,0:T(8,128)S(1)}, f32[8,32]{1,0:T(8,128)S(1)}, u32[]{:S(2)}, u32[]{:S(2)}) collective-permute-start(f32[8,32]{1,0:T(8,128)S(1)} %fusion.61), channel_id=1, source_target_pairs={{0,8},{1,9},{2,10},{3,11},{4,12},{5,13},{6,14},{7,15},{8,0},{9,1},... | collective-permute-start | bytes 3080 | tf_op jit(solution)/shard_map/ppermute | solution.py:13
  120.2 0.1 constant_dynamic-slice_fusion.1
  120.3 2.0 %collective-permute-done.24 = f32[8,32]{1,0:T(8,128)S(1)} collective-permute-done((f32[8,32]{1,0:T(8,128)S(1)}, f32[8,32]{1,0:T(8,128)S(1)}, u32[]{:S(2)}, u32[]{:S(2)}) %collective-permute-start.24) | collective-permute-done | bytes 1056 | tf_op jit(solution)/shard_map/ppermute | solution.py:13
  122.3 1.2 collective-permute-done.25
  123.5 0.1 fusion.34
  123.6 0.7 copy.8
  124.3 0.8 fusion.23
  (59 shorter events, 0.6 us)
Async XLA Ops:
  1.6 10.4 %collective-permute-start.2 = (bf16[112,1024]{1,0:T(8,128)(2,1)S(1)}, bf16[112,1024]{1,0:T(8,128)(2,1)S(1)}, u32[]{:S(2)}, u32[]{:S(2)}) collective-permute-start(bf16[112,1024]{1,0:T(8,128)(2,1)S(1)} %maximum_bitcast_fusion), channel_id=1, source_target_pairs={{0,2},{1,3},{2,0},{3,1},{4,6},{5,7},{6,4},{7,5},{8,10},{9,11},{10,... | collective-permute-start | bytes 688136 | tf_op jit(solution)/shard_map/ppermute | solution.py:13
  4.7 3.5 %collective-permute-start = (bf16[112,1024]{1,0:T(8,128)(2,1)S(1)}, bf16[112,1024]{1,0:T(8,128)(2,1)S(1)}, u32[]{:S(2)}, u32[]{:S(2)}) collective-permute-start(bf16[112,1024]{1,0:T(8,128)(2,1)S(1)} %maximum_bitcast_fusion), channel_id=1, source_target_pairs={{0,1},{1,0},{2,3},{3,2},{4,5},{5,4},{6,7},{7,6},{8,9},{9,8},{10,11... | collective-permute-start | bytes 688136 | tf_op jit(solution)/shard_map/ppermute | solution.py:13
  6.0 17.6 %copy-start.2 = (bf16[1024,128]{1,0:T(8,128)(2,1)}, bf16[1024,128]{1,0:T(8,128)(2,1)S(1)}, u32[]{:S(2)}) copy-start(bf16[1024,128]{1,0:T(8,128)(2,1)S(1)} %get-tuple-element.7) | copy-start | bytes 786436
  6.0 21.4 %copy-start.4 = (bf16[1024,128]{1,0:T(8,128)(2,1)}, bf16[1024,128]{1,0:T(8,128)(2,1)S(1)}, u32[]{:S(2)}) copy-start(bf16[1024,128]{1,0:T(8,128)(2,1)S(1)} %get-tuple-element.9) | copy-start | bytes 786436
  6.0 16.5 %collective-permute-start.1 = (bf16[1024,128]{1,0:T(8,128)(2,1)S(1)}, bf16[1024,128]{1,0:T(8,128)(2,1)S(1)}, u32[]{:S(2)}, u32[]{:S(2)}) collective-permute-start(bf16[1024,128]{1,0:T(8,128)(2,1)S(1)} %get-tuple-element.7), channel_id=1, source_target_pairs={{0,1},{1,0},{2,3},{3,2},{4,5},{5,4},{6,7},{7,6},{8,9},{9,8},{10,11... | collective-permute-start | bytes 786440 | tf_op jit(solution)/shard_map/ppermute | solution.py:13
  6.6 10.3 %collective-permute-start.4 = (bf16[1024,128]{1,0:T(8,128)(2,1)S(1)}, bf16[1024,128]{1,0:T(8,128)(2,1)}, u32[]{:S(2)}, u32[]{:S(2)}) collective-permute-start(bf16[1024,128]{1,0:T(8,128)(2,1)S(1)} %get-tuple-element.6), channel_id=1, source_target_pairs={{0,2},{1,3},{2,0},{3,1},{4,6},{5,7},{6,4},{7,5},{8,10},{9,11},{10,... | collective-permute-start | bytes 786440 | tf_op jit(solution)/shard_map/ppermute | solution.py:13
  6.6 18.8 %collective-permute-start.9 = (bf16[1024,128]{1,0:T(8,128)(2,1)S(1)}, bf16[1024,128]{1,0:T(8,128)(2,1)}, u32[]{:S(2)}, u32[]{:S(2)}) collective-permute-start(bf16[1024,128]{1,0:T(8,128)(2,1)S(1)} %get-tuple-element.9), channel_id=1, source_target_pairs={{0,1},{1,0},{2,3},{3,2},{4,5},{5,4},{6,7},{7,6},{8,9},{9,8},{10,11... | collective-permute-start | bytes 786440 | tf_op jit(solution)/shard_map/ppermute | solution.py:13
  8.2 13.3 %collective-permute-start.10 = (bf16[1024,128]{1,0:T(8,128)(2,1)S(1)}, bf16[1024,128]{1,0:T(8,128)(2,1)S(1)}, u32[]{:S(2)}, u32[]{:S(2)}) collective-permute-start(bf16[1024,128]{1,0:T(8,128)(2,1)S(1)} %get-tuple-element.8), channel_id=1, source_target_pairs={{0,2},{1,3},{2,0},{3,1},{4,6},{5,7},{6,4},{7,5},{8,10},{9,11},{10,... | collective-permute-start | bytes 786440 | tf_op jit(solution)/shard_map/ppermute | solution.py:13
  12.0 17.3 %collective-permute-start.3 = (bf16[112,1024]{1,0:T(8,128)(2,1)S(1)}, bf16[112,1024]{1,0:T(8,128)(2,1)S(1)}, u32[]{:S(2)}, u32[]{:S(2)}) collective-permute-start(bf16[112,1024]{1,0:T(8,128)(2,1)S(1)} %collective-permute-done.2), channel_id=1, source_target_pairs={{0,1},{1,0},{2,3},{3,2},{4,5},{5,4},{6,7},{7,6},{8,9},{9,8},{10,11... | collective-permute-start | bytes 688136 | tf_op jit(solution)/shard_map/ppermute | solution.py:13
  16.8 14.4 %collective-permute-start.5 = (bf16[1024,128]{1,0:T(8,128)(2,1)}, bf16[1024,128]{1,0:T(8,128)(2,1)S(1)}, u32[]{:S(2)}, u32[]{:S(2)}) collective-permute-start(bf16[1024,128]{1,0:T(8,128)(2,1)} %collective-permute-done.4), channel_id=1, source_target_pairs={{0,1},{1,0},{2,3},{3,2},{4,5},{5,4},{6,7},{7,6},{8,9},{9,8},{10,11... | collective-permute-start | bytes 786440 | tf_op jit(solution)/shard_map/ppermute | solution.py:13
  21.5 12.7 %collective-permute-start.11 = (bf16[1024,128]{1,0:T(8,128)(2,1)S(1)}, bf16[1024,128]{1,0:T(8,128)(2,1)S(1)}, u32[]{:S(2)}, u32[]{:S(2)}) collective-permute-start(bf16[1024,128]{1,0:T(8,128)(2,1)S(1)} %collective-permute-done.10), channel_id=1, source_target_pairs={{0,1},{1,0},{2,3},{3,2},{4,5},{5,4},{6,7},{7,6},{8,9},{9,8},{10,11... | collective-permute-start | bytes 786440 | tf_op jit(solution)/shard_map/ppermute | solution.py:13
  22.5 1.0 copy-start.6
  32.3 7.8 %collective-permute-start.6 = (bf16[768,128]{1,0:T(8,128)(2,1)S(1)}, bf16[768,128]{1,0:T(8,128)(2,1)S(1)}, u32[]{:S(2)}, u32[]{:S(2)}) collective-permute-start(bf16[768,128]{1,0:T(8,128)(2,1)S(1)} %fusion.2), channel_id=1, source_target_pairs={{0,4},{1,5},{2,6},{3,7},{4,0},{5,1},{6,2},{7,3},{8,12},{9,13},{10,... | collective-permute-start | bytes 589832 | tf_op jit(solution)/shard_map/ppermute | solution.py:13
  35.2 8.8 %collective-permute-start.12 = (bf16[768,128]{1,0:T(8,128)(2,1)S(1)}, bf16[768,128]{1,0:T(8,128)(2,1)S(1)}, u32[]{:S(2)}, u32[]{:S(2)}) collective-permute-start(bf16[768,128]{1,0:T(8,128)(2,1)S(1)} %fusion.3), channel_id=1, source_target_pairs={{0,4},{1,5},{2,6},{3,7},{4,0},{5,1},{6,2},{7,3},{8,12},{9,13},{10,... | collective-permute-start | bytes 589832 | tf_op jit(solution)/shard_map/ppermute | solution.py:13
  41.2 17.2 %collective-permute-start.7 = (bf16[768,128]{1,0:T(8,128)(2,1)S(1)}, bf16[768,128]{1,0:T(8,128)(2,1)S(1)}, u32[]{:S(2)}, u32[]{:S(2)}) collective-permute-start(bf16[768,128]{1,0:T(8,128)(2,1)S(1)} %get-tuple-element.26), channel_id=1, source_target_pairs={{0,8},{1,9},{2,10},{3,11},{4,12},{5,13},{6,14},{7,15},{8,0},{9,1},... | collective-permute-start | bytes 589832 | tf_op jit(solution)/shard_map/ppermute | solution.py:13
  45.1 16.0 %collective-permute-start.13 = (bf16[768,128]{1,0:T(8,128)(2,1)S(1)}, bf16[768,128]{1,0:T(8,128)(2,1)S(1)}, u32[]{:S(2)}, u32[]{:S(2)}) collective-permute-start(bf16[768,128]{1,0:T(8,128)(2,1)S(1)} %get-tuple-element.24), channel_id=1, source_target_pairs={{0,8},{1,9},{2,10},{3,11},{4,12},{5,13},{6,14},{7,15},{8,0},{9,1},... | collective-permute-start | bytes 589832 | tf_op jit(solution)/shard_map/ppermute | solution.py:13
  58.4 7.9 %collective-permute-start.8 = (bf16[768,128]{1,0:T(8,128)(2,1)S(1)}, bf16[768,128]{1,0:T(8,128)(2,1)}, u32[]{:S(2)}, u32[]{:S(2)}) collective-permute-start(bf16[768,128]{1,0:T(8,128)(2,1)S(1)} %fusion.17), channel_id=1, source_target_pairs={{0,4},{1,5},{2,6},{3,7},{4,0},{5,1},{6,2},{7,3},{8,12},{9,13},{10,... | collective-permute-start | bytes 589832 | tf_op jit(solution)/shard_map/ppermute | solution.py:13
  61.2 5.2 %copy-start = (bf16[768,128]{1,0:T(8,128)(2,1)}, bf16[768,128]{1,0:T(8,128)(2,1)S(1)}, u32[]{:S(2)}) copy-start(bf16[768,128]{1,0:T(8,128)(2,1)S(1)} %fusion.16) | copy-start | bytes 589828
  61.2 8.4 %collective-permute-start.14 = (bf16[768,128]{1,0:T(8,128)(2,1)S(1)}, bf16[768,128]{1,0:T(8,128)(2,1)}, u32[]{:S(2)}, u32[]{:S(2)}) collective-permute-start(bf16[768,128]{1,0:T(8,128)(2,1)S(1)} %fusion.16), channel_id=1, source_target_pairs={{0,4},{1,5},{2,6},{3,7},{4,0},{5,1},{6,2},{7,3},{8,12},{9,13},{10,... | collective-permute-start | bytes 589832 | tf_op jit(solution)/shard_map/ppermute | solution.py:13
  61.9 21.1 %collective-permute-start.16 = (bf16[1024,1024]{1,0:T(8,128)(2,1)}, bf16[1024,1024]{1,0:T(8,128)(2,1)}, u32[]{:S(2)}, u32[]{:S(2)}) collective-permute-start(bf16[1024,1024]{1,0:T(8,128)(2,1)} %param.9), channel_id=1, source_target_pairs={{0,1},{1,0},{2,3},{3,2},{4,5},{5,4},{6,7},{7,6},{8,9},{9,8},{10,11... | collective-permute-start | bytes 6291464 | tf_op jit(solution)/shard_map/ppermute | solution.py:13
  72.7 4.3 %copy-start.1 = (bf16[768,128]{1,0:T(8,128)(2,1)S(1)}, bf16[768,128]{1,0:T(8,128)(2,1)}, u32[]{:S(2)}) copy-start(bf16[768,128]{1,0:T(8,128)(2,1)} %copy-done) | copy-start | bytes 589828
  72.7 4.3 %copy-start.3 = (bf16[1024,128]{1,0:T(8,128)(2,1)S(1)}, bf16[1024,128]{1,0:T(8,128)(2,1)}, u32[]{:S(2)}) copy-start(bf16[1024,128]{1,0:T(8,128)(2,1)} %copy-done.2) | copy-start | bytes 786436
  72.7 4.3 %copy-start.5 = (bf16[1024,128]{1,0:T(8,128)(2,1)S(1)}, bf16[1024,128]{1,0:T(8,128)(2,1)}, u32[]{:S(2)}) copy-start(bf16[1024,128]{1,0:T(8,128)(2,1)} %copy-done.4) | copy-start | bytes 786436
  72.7 4.3 %copy-start.7 = (bf16[1024,128]{1,0:T(8,128)(2,1)S(1)}, bf16[1024,128]{1,0:T(8,128)(2,1)}, u32[]{:S(2)}) copy-start(bf16[1024,128]{1,0:T(8,128)(2,1)} %copy-done.6) | copy-start | bytes 786436
  75.4 7.5 %collective-permute-start.15 = (f32[32,2048]{1,0:T(8,128)}, f32[32,2048]{1,0:T(8,128)S(1)}, u32[]{:S(2)}, u32[]{:S(2)}) collective-permute-start(f32[32,2048]{1,0:T(8,128)} %multiply_reduce_fusion), channel_id=1, source_target_pairs={{0,2},{1,3},{2,0},{3,1},{4,6},{5,7},{6,4},{7,5},{8,10},{9,11},{10,... | collective-permute-start | bytes 786440 | tf_op jit(solution)/shard_map/ppermute | solution.py:13
  89.0 5.0 %collective-permute-start.17 = (f32[32,1024]{1,0:T(8,128)S(1)}, f32[32,1024]{1,0:T(8,128)S(1)}, u32[]{:S(2)}, u32[]{:S(2)}) collective-permute-start(f32[32,1024]{1,0:T(8,128)S(1)} %fusion.45), channel_id=1, source_target_pairs={{0,2},{1,3},{2,0},{3,1},{4,6},{5,7},{6,4},{7,5},{8,10},{9,11},{10,... | collective-permute-start | bytes 393224 | tf_op jit(solution)/shard_map/ppermute | solution.py:13
  94.0 5.0 %collective-permute-start.18 = (f32[32,1024]{1,0:T(8,128)S(1)}, f32[32,1024]{1,0:T(8,128)S(1)}, u32[]{:S(2)}, u32[]{:S(2)}) collective-permute-start(f32[32,1024]{1,0:T(8,128)S(1)} %add.154), channel_id=1, source_target_pairs={{0,4},{1,5},{2,6},{3,7},{4,0},{5,1},{6,2},{7,3},{8,12},{9,13},{10,... | collective-permute-start | bytes 393224 | tf_op jit(solution)/shard_map/ppermute | solution.py:13
  99.1 7.7 %collective-permute-start.19 = (f32[32,1024]{1,0:T(8,128)S(1)}, f32[32,1024]{1,0:T(8,128)S(1)}, u32[]{:S(2)}, u32[]{:S(2)}) collective-permute-start(f32[32,1024]{1,0:T(8,128)S(1)} %add.155), channel_id=1, source_target_pairs={{0,8},{1,9},{2,10},{3,11},{4,12},{5,13},{6,14},{7,15},{8,0},{9,1},... | collective-permute-start | bytes 393224 | tf_op jit(solution)/shard_map/ppermute | solution.py:13
  110.5 3.7 %collective-permute-start.22 = (f32[8,32]{1,0:T(8,128)S(1)}, f32[8,32]{1,0:T(8,128)S(1)}, u32[]{:S(2)}, u32[]{:S(2)}) collective-permute-start(f32[8,32]{1,0:T(8,128)S(1)} %broadcast_in_dim.2), channel_id=1, source_target_pairs={{0,2},{1,3},{2,0},{3,1},{4,6},{5,7},{6,4},{7,5},{8,10},{9,11},{10,... | collective-permute-start | bytes 3080 | tf_op jit(solution)/shard_map/ppermute | solution.py:13
  112.1 12.2 %collective-permute-start.21 = (f32[32,1024]{1,0:T(8,128)S(1)}, f32[32,1024]{1,0:T(8,128)S(1)}, u32[]{:S(2)}, u32[]{:S(2)}) collective-permute-start(f32[32,1024]{1,0:T(8,128)S(1)} %get-tuple-element.19), channel_id=1, source_target_pairs={{0,1},{1,0},{2,3},{3,2},{4,5},{5,4},{6,7},{7,6},{8,9},{9,8},{10,11... | collective-permute-start | bytes 393224 | tf_op jit(solution)/shard_map/ppermute | solution.py:13
  114.2 3.6 %collective-permute-start.23 = (f32[8,32]{1,0:T(8,128)S(1)}, f32[8,32]{1,0:T(8,128)S(1)}, u32[]{:S(2)}, u32[]{:S(2)}) collective-permute-start(f32[8,32]{1,0:T(8,128)S(1)} %broadcast_add_fusion), channel_id=1, source_target_pairs={{0,4},{1,5},{2,6},{3,7},{4,0},{5,1},{6,2},{7,3},{8,12},{9,13},{10,... | collective-permute-start | bytes 3080 | tf_op jit(solution)/shard_map/ppermute | solution.py:13
  117.8 4.5 %collective-permute-start.24 = (f32[8,32]{1,0:T(8,128)S(1)}, f32[8,32]{1,0:T(8,128)S(1)}, u32[]{:S(2)}, u32[]{:S(2)}) collective-permute-start(f32[8,32]{1,0:T(8,128)S(1)} %fusion.61), channel_id=1, source_target_pairs={{0,8},{1,9},{2,10},{3,11},{4,12},{5,13},{6,14},{7,15},{8,0},{9,1},... | collective-permute-start | bytes 3080 | tf_op jit(solution)/shard_map/ppermute | solution.py:13
  120.3 3.3 %collective-permute-start.20 = (f32[32,64]{1,0:T(8,128)S(1)}, f32[32,64]{1,0:T(8,128)S(1)}, u32[]{:S(2)}, u32[]{:S(2)}) collective-permute-start(f32[32,64]{1,0:T(8,128)S(1)} %get-tuple-element.21), channel_id=1, source_target_pairs={{0,1},{1,0},{2,3},{3,2},{4,5},{5,4},{6,7},{7,6},{8,9},{9,8},{10,11... | collective-permute-start | bytes 24584 | tf_op jit(solution)/shard_map/ppermute | solution.py:13
  122.3 1.2 collective-permute-start.25

commit v2 on v1

v2 whole, which is shorter than its diff:
```python
import functools

import jax
import jax.numpy as jnp
from jax import lax
from jax.experimental import pallas as pl
from jax.experimental.pallas import tpu as pltpu

from jax.sharding import PartitionSpec as P

F32 = jnp.float32
BF16 = jnp.bfloat16
CHUNKS = 2
PIECES = 1


def swap(block, bit):
    count = lax.axis_size("grid")
    return lax.ppermute(block, "grid", [(i, i ^ bit) for i in range(count)])


def pairs_of(pot_rows, val_rows):
    joined = pot_rows[:, None, :] * val_rows[None, :, :]
    return joined.reshape(-1, joined.shape[2])


def contract(left, right):
    return jnp.dot(left, right, preferred_element_type=F32)


def contract_last(left, right):
    return lax.dot_general(left, right, (((1,), (1,)), ((), ())), preferred_element_type=F32)


def body(valence, conduction, potentials, eigenpotentials, valence_energy, conduction_energy):
    rows, val_count = valence.shape
    cond_count = conduction.shape[1]
    pot_count = potentials.shape[1]
    eig_count = eigenpotentials.shape[1]
    count = lax.axis_size("grid")
    points_total = rows * count
    me = lax.axis_index("grid")
    core = me & 1
    side = (me >> 1) & 1
    bits = []
    bit = 4
    while bit < count:
        bits.append(bit)
        bit *= 2
    spread, last = bits[:-1], bits[-1]
    k_half, c_half = pot_count // 2, cond_count // 2
    c_part = c_half // CHUNKS
    parts = range(CHUNKS)

    blocks = pl.pallas_call(
        functools.partial(prepare_kernel, CHUNKS),
        out_shape=[jax.ShapeDtypeStruct((rows, c_part), BF16)] * (2 * CHUNKS),
        in_specs=[pl.BlockSpec(memory_space=pltpu.SMEM), pl.BlockSpec(memory_space=pltpu.VMEM)],
        out_specs=[pl.BlockSpec(memory_space=pltpu.VMEM)] * (2 * CHUNKS),
        compiler_params=pltpu.CompilerParams(vmem_limit_bytes=6 * 2**20),
        cost_estimate=pl.CostEstimate(flops=10**6, bytes_accessed=2**21, transcendentals=0),
    )(side[None], conduction)
    vals, pots = [valence.T], [potentials.T]
    val_side, pot_side = swap(vals[0], 2), swap(pots[0], 2)
    cond_side = [swap(blocks[part], 2) for part in parts]
    cond_mine = blocks[CHUNKS:]
    vals += [swap(vals[0], 1), val_side, swap(val_side, 1)]
    pots += [swap(pots[0], 1), pot_side, swap(pot_side, 1)]
    cond_core = [swap(cond_mine[part], 1) for part in parts]
    cond_diag = [swap(cond_side[part], 1) for part in parts]
    eig_core = swap(eigenpotentials, 1)
    cond_all = [cond_mine, cond_core, cond_side, cond_diag]

    energies = lax.dynamic_slice(conduction_energy, (side * c_half,), (c_half,))
    factors = (4.0 / points_total) / (valence_energy[:, None] - energies[None, :])

    first, size = core * k_half, k_half
    groups = []
    for bit in spread:
        size //= 2
        up = (me & bit) // bit
        groups.append((first + (1 - up) * size, size))
        first = first + up * size
    groups.append((first, size))

    def pairs_for(place, group):
        block = pots[place]
        return pairs_of(lax.dynamic_slice(block, (group[0], 0), (group[1], block.shape[1])), vals[place])

    starts = jnp.stack([group[0] for group in groups])
    own = [cond_all[place][part] for place in (0, 1) for part in parts]
    own_terms = pl.pallas_call(
        functools.partial(own_kernel, CHUNKS),
        out_shape=[
            jax.ShapeDtypeStruct((group[1] * val_count, c_part), F32) for group in groups for part in parts
        ],
        in_specs=[pl.BlockSpec(memory_space=pltpu.SMEM)] + [pl.BlockSpec(memory_space=pltpu.VMEM)] * (4 + len(own)),
        out_specs=[pl.BlockSpec(memory_space=pltpu.VMEM)] * (len(groups) * CHUNKS),
        scratch_shapes=[
            pltpu.VMEM((groups[0][1] * val_count, 2 * rows), BF16),
            pltpu.VMEM((2 * rows, c_half), BF16),
            pltpu.VMEM((2, pot_count, rows), F32),
        ],
        compiler_params=pltpu.CompilerParams(vmem_limit_bytes=16 * 2**20),
        cost_estimate=pl.CostEstimate(
            flops=4 * rows * k_half * val_count * c_half, bytes_accessed=2**22, transcendentals=0
        ),
    )(starts, vals[0], vals[1], pots[0], pots[1], *own)
    pairs = {place: [pairs_for(place, group) for group in groups] for place in (2, 3)}

    def coefficients(index, part):
        total = own_terms[index * CHUNKS + part]
        for place in (2, 3):
            total = total + contract(pairs[place][index], cond_all[place][part])
        return total

    def cut(block):
        return jnp.split(block, PIECES, axis=0)

    scaled_mine, scaled_rest = [], []
    for part in parts:
        totals = [None] * PIECES
        for level, bit in enumerate(spread):
            mine = cut(coefficients(level, part))
            up = (me & bit) // bit
            for q in range(PIECES):
                send, many = mine[q], mine[q].shape[0]
                if totals[q] is not None:
                    send = send + lax.dynamic_slice(totals[q], ((1 - up) * many, 0), send.shape)
                    totals[q] = lax.dynamic_slice(totals[q], (up * many, 0), send.shape)
                got = swap(send.astype(BF16), bit).astype(F32)
                totals[q] = got if totals[q] is None else totals[q] + got
        mine = cut(coefficients(len(spread), part))
        factor = factors[:, part * c_part : (part + 1) * c_part]
        own, rest = [], []
        for q in range(PIECES):
            total = mine[q] if totals[q] is None else mine[q] + totals[q]
            total = total + swap(total.astype(BF16), last).astype(F32)
            many = total.shape[0] // val_count
            shaped = total.reshape(many, val_count, c_part)
            scaled = (shaped * factor[None]).astype(BF16).reshape(total.shape)
            own.append(scaled)
            others = []
            for level in reversed(range(len(spread))):
                known = jnp.concatenate([scaled] + others, axis=0)
                others.append(swap(known, spread[level]))
            if others:
                rest.append(jnp.concatenate(others, axis=0))
        scaled_mine.append(own)
        scaled_rest.append(rest)
    many = k_half // PIECES >> len(spread)

    def respond(blocks, places):
        kernel = functools.partial(respond_kernel, len(places), CHUNKS, len(blocks[0]))
        operands = [block for column in blocks for block in column]
        operands += [cond_all[place][part] for place in places for part in parts]
        operands += [vals[place] for place in places]
        height = sum(block.shape[0] for block in blocks[0])
        return pl.pallas_call(
            kernel,
            out_shape=jax.ShapeDtypeStruct((height // val_count, rows * len(places)), F32),
            in_specs=[pl.BlockSpec(memory_space=pltpu.VMEM)] * len(operands),
            out_specs=pl.BlockSpec(memory_space=pltpu.VMEM),
            scratch_shapes=[pltpu.VMEM((height, c_half), BF16)],
            compiler_params=pltpu.CompilerParams(vmem_limit_bytes=8 * 2**20),
            cost_estimate=pl.CostEstimate(
                flops=2 * height * c_half * rows * len(places), bytes_accessed=2**22, transcendentals=0
            ),
        )(*operands)

    here, there = (0, 1), (2, 3)
    kinds = [scaled_mine] + ([scaled_rest] if spread else [])
    sums = []
    for blocks in kinds:
        arrived = swap(respond(blocks, there), 2)
        sums.append(respond(blocks, here) + arrived)
    width = sums[0].shape[1]
    ordered = [block.reshape(PIECES, -1, many, width) for block in sums]
    response = jnp.concatenate(ordered, axis=1).swapaxes(0, 1).reshape(k_half, width)
    for level, bit in enumerate(spread):
        shaped = response.reshape(1 << level, 2, -1, width)
        response = jnp.where((me & bit) != 0, shaped[:, ::-1], shaped).reshape(k_half, width)

    low = response.astype(BF16)
    intersection = contract(low[:, :rows], eigenpotentials) + contract(low[:, rows:], eig_core)
    for bit in [2] + spread:
        intersection = intersection + swap(intersection, bit)
    intersection = intersection + swap(intersection.astype(BF16), last).astype(F32)
    squares = jnp.mean(intersection * intersection, axis=1, keepdims=True)
    unit = intersection / jnp.sqrt(squares + 1e-06)
    eig_rows = eig_count // count

    def e_block(device):
        return lax.dynamic_slice(unit, (0, device * eig_rows), (k_half, eig_rows))

    def joined(mine, other):
        return jnp.where(core == 0, jnp.concatenate([mine, other], 0), jnp.concatenate([other, mine], 0))

    projected = joined(e_block(me), swap(e_block(me ^ 1), 1)).T

    ilow = intersection.astype(BF16)
    remainder_core = response[:, rows:] - contract_last(ilow, eig_core)
    remainder_mine = response[:, :rows] - contract_last(ilow, eigenpotentials)
    remainder_other = swap(remainder_core, 1)
    share = jnp.sum(remainder_core * remainder_core, axis=1) + jnp.sum(remainder_mine * remainder_mine, axis=1)
    share = share[None, :]
    for low_bit, high_bit in zip(bits[::2], bits[1::2] + [0] * (len(bits) % 2)):
        steps = [step for step in (low_bit, high_bit, low_bit | high_bit) if step and (high_bit or step == low_bit)]
        share = share + sum(swap(share, step) for step in dict.fromkeys(steps))
    mine, other = share + swap(share, 2), swap(share, 1) + swap(share, 3)
    sums = joined(mine, other).reshape(pot_count)
    scale = jnp.sqrt(sums / points_total + 1e-06)
    turned = lax.optimization_barrier(joined(remainder_mine, remainder_other).T)
    return (projected, turned / scale[None, :])


def prepare_kernel(chunks, side_ref, cond_ref, *blocks):
    width = blocks[0].shape[1]
    side = side_ref[0]
    for index, block in enumerate(blocks):
        which = 1 - side if index < chunks else side
        begin = pl.multiple_of((which * chunks + index % chunks) * width, width)
        block[...] = cond_ref[:, pl.ds(begin, width)]


def own_kernel(chunks, starts_ref, val0, val1, pot0, pot1, *refs):
    conds, outs = refs[: 2 * chunks], refs[2 * chunks : -3]
    pairs, right, wide = refs[-3:]
    val_count, rows = val0.shape
    width = conds[0].shape[1]
    for place, (val, pot) in enumerate(((val0, pot0), (val1, pot1))):
        for part in range(chunks):
            right[pl.ds(place * rows, rows), pl.ds(part * width, width)] = conds[place * chunks + part][...]
        wide[place] = pot[...].astype(F32)
    for group in range(len(outs) // chunks):
        height = outs[group * chunks].shape[0]
        many = height // val_count
        start = starts_ref[group]
        for place, val in enumerate((val0, val1)):
            values = val[...].astype(F32)
            for k in range(many):
                row = wide[place, pl.ds(start + k, 1), :]
                pairs[pl.ds(k * val_count, val_count), pl.ds(place * rows, rows)] = (row * values).astype(BF16)
        total = contract(pairs[pl.ds(0, height), :], right[...])
        for part in range(chunks):
            outs[group * chunks + part][...] = total[:, part * width : (part + 1) * width]


def respond_kernel(places, chunks, pieces, *refs):
    scaled = refs[: chunks * pieces]
    conds = refs[chunks * pieces :][: places * chunks]
    vals = refs[chunks * pieces + places * chunks :][:places]
    out, left = refs[-2:]
    height, depth = left.shape
    width = depth // chunks
    for part in range(chunks):
        top = 0
        for q in range(pieces):
            block = scaled[part * pieces + q]
            left[pl.ds(top, block.shape[0]), pl.ds(part * width, width)] = block[...]
            top += block.shape[0]
    count = out.shape[0]
    val_count = height // count
    rows = out.shape[1] // places
    tile = min(rows, 256)
    for place in range(places):

        def step(index, carry):
            begin = pl.multiple_of(index * tile, tile)
            right = jnp.concatenate(
                [conds[place * chunks + part][pl.ds(begin, tile), :] for part in range(chunks)], axis=1
            )
            values = vals[place][:, pl.ds(begin, tile)].astype(F32)
            product = contract_last(left[...], right)
            summed = jnp.sum(product.reshape(count, val_count, tile) * values[None], axis=1)
            out[:, pl.ds(pl.multiple_of(place * rows + begin, tile), tile)] = summed
            return carry

        lax.fori_loop(0, rows // tile, step, 0)


def solution(mesh):
    spec = P(("grp", "grid"), None)

    return jax.shard_map(
        body,
        mesh=mesh,
        in_specs=(spec, spec, spec, spec, P("grp"), P("grp")),
        out_specs=(spec, spec),
        check_vma=False,
    )
```

time: 126 us -> 119 us (0.944)
  Pallas kernels: 0 us -> 12.9 us
  matrix products: 23.6 us -> 13.7 us
  other arithmetic: 11.4 us -> 2.56 us
  local copies, waits for them, and re-layouts: 10.2 us -> 2.87 us
  starting transfers between devices: 26.5 us -> 31.5 us
  waiting for transfers between devices: 52.4 us -> 53.8 us
    pallas_call x0 -> x6, Pallas kernels: none -> 12.9 us  [the longest x4 10.3 us: respond(): pl.pallas_call(kernel, out_shape=jax.ShapeDtypeStruct((height // val_coun...]
    dot_general x9 -> x10, matrix products: 13.9 us -> 8.8 us  [contract(): return jnp.dot(left, right, preferred_element_type=F32)]
    ppermute x26 -> x32, starting transfers between devices: 26.5 us -> 31.5 us  [swap(): return lax.ppermute(block, 'grid', [(i, i ^ bit) for i in range(count)])]
    dot_general x3 -> x2, matrix products: 9.78 us -> 4.86 us  [contract_last(): lax.dot_general(left, right, (((1,), (1,)), ((), ())), preferred_element_...]
    reduce_sum x2 -> x0, other arithmetic: 4.61 us -> none  [respond(): return jnp.sum(combined * val_block.astype(F32)[None], axis=1)]
    convert_element_type x9 -> x4, other arithmetic: 3.86 us -> 0.15 us  [the longest x2 0.12 us: body(): scaled = (shaped * factor[None]).astype(BF16).reshape(total.shape)]
    concatenate x6 -> x0, local copies, waits for them, and re-layouts: 3.19 us -> none  [the longest x1 3.1 us: body(): eig_here = jnp.concatenate([eigenpotentials, eig_core], axis=0)]
    unnamed x21 -> x7, local copies, waits for them, and re-layouts: 4.86 us -> 1.94 us
  transfers between devices with their start and end apart: 26 -> 32, of which waited for: 15 -> 18; matrix products, arithmetic and copies ran while one was open for 27% -> 9% of each run, Pallas kernels for 0% -> 11%
where the time goes in v2:
time: 119 us; the launch traced here: 118 us
  waiting for transfers between devices  53.8 us (45%)
  starting transfers between devices  31.5 us (26%)
  matrix products  13.7 us (12%)
  Pallas kernels  12.9 us (11%)
  local copies, waits for them, and re-layouts  2.87 us (2%)
  other arithmetic  2.56 us (2%)
    ppermute x32, waiting for transfers between devices, swap(): return lax.ppermute(block, 'grid', [(i, i ^ bit) for i in range(count)])  53.8 us
    ppermute x32, starting transfers between devices, swap(): return lax.ppermute(block, 'grid', [(i, i ^ bit) for i in range(count)])  31.5 us
    pallas_call x4, Pallas kernels, respond(): pl.pallas_call(kernel, out_shape=jax.ShapeDtypeStruct((height // val_coun...  10.3 us
    dot_general x10, matrix products, contract(): return jnp.dot(left, right, preferred_element_type=F32)  8.8 us
    dot_general x2, matrix products, contract_last(): lax.dot_general(left, right, (((1,), (1,)), ((), ())), preferred_element_...  4.86 us
    pallas_call x1, Pallas kernels, body(): pl.pallas_call(functools.partial(own_kernel, CHUNKS), out_shape=[jax.Shap...  2.48 us
  transfers between devices with their start and end apart: 32, of which 18 were waited for; matrix products, arithmetic and copies ran while one was open for 9% of the time, Pallas kernels for 11%

profile of v2, /device:TPU:0, one launch (start us, length us, event | category | flops | bytes accessed | tf_op | source)
XLA Modules:
  0.0 118.2 jit_solution(3353595048269844613)
XLA Ops:
  0.6 0.6 collective-permute-start.1
  1.2 2.6 %collective-permute-start.4 = (bf16[64,1024]{1,0:T(8,128)(2,1)}, bf16[64,1024]{1,0:T(8,128)(2,1)S(1)}, u32[]{:S(2)}, u32[]{:S(2)}) collective-permute-start(bf16[64,1024]{1,0:T(8,128)(2,1)} %bitcast.50), channel_id=1, source_target_pairs={{0,2},{1,3},{2,0},{3,1},{4,6},{5,7},{6,4},{7,5},{8,10},{9,11},{10,... | collective-permute-start | bytes 393224 | tf_op jit(solution)/shard_map/ppermute | solution.py:19
  3.9 0.3 collective-permute-start.5
  4.2 1.2 %copy-done = bf16[1024,512]{1,0:T(8,128)(2,1)S(1)} copy-done((bf16[1024,512]{1,0:T(8,128)(2,1)S(1)}, bf16[1024,512]{1,0:T(8,128)(2,1)}, u32[]{:S(2)}) %copy-start) | copy-done | bytes 1048600
  5.4 0.2 shard_map.77
  5.8 0.8 dynamic_slice.25
  6.5 0.7 subtract_divide_fusion
  7.4 1.0 collective-permute-done.4
  8.3 1.8 %collective-permute-done.5.refs_6_ = bf16[48,1024]{1,0:T(8,128)(2,1)S(1)} collective-permute-done((bf16[48,1024]{1,0:T(8,128)(2,1)}, bf16[48,1024]{1,0:T(8,128)(2,1)S(1)}, u32[]{:S(2)}, u32[]{:S(2)}) %collective-permute-start.5) | collective-permute-done | bytes 98336 | tf_op jit(solution)/shard_map/ppermute | solution.py:19
  10.2 1.7 %collective-permute-start.12 = (bf16[1024,128]{1,0:T(8,128)(2,1)S(1)}, bf16[1024,128]{1,0:T(8,128)(2,1)S(1)}, u32[]{:S(2)}, u32[]{:S(2)}) collective-permute-start(bf16[1024,128]{1,0:T(8,128)(2,1)S(1)} %get-tuple-element.16), channel_id=1, source_target_pairs={{0,2},{1,3},{2,0},{3,1},{4,6},{5,7},{6,4},{7,5},{8,10},{9,11},{10,... | collective-permute-start | bytes 786440 | tf_op jit(solution)/shard_map/ppermute | solution.py:19
  11.9 0.2 broadcast_multiply_fusion.3
  12.1 6.1 %collective-permute-done.12.refs_3_ = bf16[1024,128]{1,0:T(8,128)(2,1)S(1)} collective-permute-done((bf16[1024,128]{1,0:T(8,128)(2,1)S(1)}, bf16[1024,128]{1,0:T(8,128)(2,1)S(1)}, u32[]{:S(2)}, u32[]{:S(2)}) %collective-permute-start.12) | collective-permute-done | bytes 262176 | tf_op jit(solution)/shard_map/ppermute | solution.py:19
  18.2 0.6 fusion.24
  18.8 0.8 collective-permute-done.7
  19.7 1.1 collective-permute-done.8.refs_7_
  20.9 1.5 %collective-permute-start.6 = (bf16[1024,128]{1,0:T(8,128)(2,1)S(1)}, bf16[1024,128]{1,0:T(8,128)(2,1)S(1)}, u32[]{:S(2)}, u32[]{:S(2)}) collective-permute-start(bf16[1024,128]{1,0:T(8,128)(2,1)S(1)} %get-tuple-element.13), channel_id=1, source_target_pairs={{0,2},{1,3},{2,0},{3,1},{4,6},{5,7},{6,4},{7,5},{8,10},{9,11},{10,... | collective-permute-start | bytes 786440 | tf_op jit(solution)/shard_map/ppermute | solution.py:19
  22.4 0.2 broadcast_multiply_fusion
  22.6 0.6 fusion.23
  23.2 6.1 %collective-permute-done.6.refs_2_ = bf16[1024,128]{1,0:T(8,128)(2,1)S(1)} collective-permute-done((bf16[1024,128]{1,0:T(8,128)(2,1)S(1)}, bf16[1024,128]{1,0:T(8,128)(2,1)S(1)}, u32[]{:S(2)}, u32[]{:S(2)}) %collective-permute-start.6) | collective-permute-done | bytes 262176 | tf_op jit(solution)/shard_map/ppermute | solution.py:19
  29.3 0.6 fusion.22
  29.8 0.6 collective-permute-start.9
  30.4 2.5 %shard_map.78 = (f32[768,128]{1,0:T(8,128)S(1)}, f32[768,128]{1,0:T(8,128)S(1)}, f32[768,128]{1,0:T(8,128)S(1)}, f32[768,128]{1,0:T(8,128)S(1)}) custom-call(s32[2]{0:T(128)S(1)} %pad_add_fusion.starts_ref, bf16[48,1024]{1,0:T(8,128)(2,1)S(1)} %bitcast.54, bf16[48,1024]{1,0:T(8,128)(2,1)S(1)} %collective-permute-done.val1.refs_7_, ...), custom_call_target="tpu_custom_call" | custom-call | flops 1610612736 | bytes 4194304 | tf_op jit(solution)/shard_map/pallas_call | solution.py:92
  32.9 0.6 fusion.21
  33.5 0.6 fusion.3
  34.1 1.6 %collective-permute-start.14 = (bf16[768,128]{1,0:T(8,128)(2,1)S(1)}, bf16[768,128]{1,0:T(8,128)(2,1)S(1)}, u32[]{:S(2)}, u32[]{:S(2)}) collective-permute-start(bf16[768,128]{1,0:T(8,128)(2,1)S(1)} %fusion.3), channel_id=1, source_target_pairs={{0,4},{1,5},{2,6},{3,7},{4,0},{5,1},{6,2},{7,3},{8,12},{9,13},{10,... | collective-permute-start | bytes 589832 | tf_op jit(solution)/shard_map/ppermute | solution.py:19
  35.7 0.6 fusion.2
  36.3 0.6 collective-permute-start.10
  36.9 5.1 %collective-permute-done.14 = bf16[768,128]{1,0:T(8,128)(2,1)S(1)} collective-permute-done((bf16[768,128]{1,0:T(8,128)(2,1)S(1)}, bf16[768,128]{1,0:T(8,128)(2,1)S(1)}, u32[]{:S(2)}, u32[]{:S(2)}) %collective-permute-start.14) | collective-permute-done | bytes 196640 | tf_op jit(solution)/shard_map/ppermute | solution.py:19
  42.0 0.6 fusion.20
  42.6 2.6 %collective-permute-start.15 = (bf16[768,128]{1,0:T(8,128)(2,1)S(1)}, bf16[768,128]{1,0:T(8,128)(2,1)S(1)}, u32[]{:S(2)}, u32[]{:S(2)}) collective-permute-start(bf16[768,128]{1,0:T(8,128)(2,1)S(1)} %get-tuple-element.36), channel_id=1, source_target_pairs={{0,8},{1,9},{2,10},{3,11},{4,12},{5,13},{6,14},{7,15},{8,0},{9,1},... | collective-permute-start | bytes 589832 | tf_op jit(solution)/shard_map/ppermute | solution.py:19
  45.2 2.4 %collective-permute-done.10 = bf16[768,128]{1,0:T(8,128)(2,1)S(1)} collective-permute-done((bf16[768,128]{1,0:T(8,128)(2,1)S(1)}, bf16[768,128]{1,0:T(8,128)(2,1)S(1)}, u32[]{:S(2)}, u32[]{:S(2)}) %collective-permute-start.10) | collective-permute-done | bytes 196640 | tf_op jit(solution)/shard_map/ppermute | solution.py:19
  47.6 0.6 fusion.19
  48.2 1.2 %collective-permute-start.11 = (bf16[768,128]{1,0:T(8,128)(2,1)S(1)}, bf16[768,128]{1,0:T(8,128)(2,1)S(1)}, u32[]{:S(2)}, u32[]{:S(2)}) collective-permute-start(bf16[768,128]{1,0:T(8,128)(2,1)S(1)} %get-tuple-element.34), channel_id=1, source_target_pairs={{0,8},{1,9},{2,10},{3,11},{4,12},{5,13},{6,14},{7,15},{8,0},{9,1},... | collective-permute-start | bytes 589832 | tf_op jit(solution)/shard_map/ppermute | solution.py:19
  49.4 9.4 %collective-permute-done.15 = bf16[768,128]{1,0:T(8,128)(2,1)S(1)} collective-permute-done((bf16[768,128]{1,0:T(8,128)(2,1)S(1)}, bf16[768,128]{1,0:T(8,128)(2,1)S(1)}, u32[]{:S(2)}, u32[]{:S(2)}) %collective-permute-start.15) | collective-permute-done | bytes 196640 | tf_op jit(solution)/shard_map/ppermute | solution.py:19
  58.9 2.6 %collective-permute-done.11 = bf16[768,128]{1,0:T(8,128)(2,1)S(1)} collective-permute-done((bf16[768,128]{1,0:T(8,128)(2,1)S(1)}, bf16[768,128]{1,0:T(8,128)(2,1)S(1)}, u32[]{:S(2)}, u32[]{:S(2)}) %collective-permute-start.11) | collective-permute-done | bytes 196640 | tf_op jit(solution)/shard_map/ppermute | solution.py:19
  61.6 0.5 collective-permute-start.17
  62.1 2.7 %shard_map.80 = f32[16,2048]{1,0:T(8,128)S(1)} custom-call(bf16[768,128]{1,0:T(8,128)(2,1)S(1)} %fusion.5.refs_0_, bf16[768,128]{1,0:T(8,128)(2,1)S(1)} %fusion.4.refs_1_, bf16[1024,128]{1,0:T(8,128)(2,1)S(1)} %collective-permute-done.6.refs_2_, bf16[1024,128]{1,0:T(8,128)(2,1)S(1)} %collective-permute-done.12.refs_3_, ...), custom_call_target="tpu_custom_call" | custom-call | flops 805306368 | bytes 4194304 | tf_op jit(solution)/shard_map/pallas_call | solution.py:159
  64.8 1.6 %collective-permute-start.16 = (f32[16,2048]{1,0:T(8,128)S(1)}, f32[16,2048]{1,0:T(8,128)S(1)}, u32[]{:S(2)}, u32[]{:S(2)}) collective-permute-start(f32[16,2048]{1,0:T(8,128)S(1)} %shard_map.80), channel_id=1, source_target_pairs={{0,2},{1,3},{2,0},{3,1},{4,6},{5,7},{6,4},{7,5},{8,10},{9,11},{10,... | collective-permute-start | bytes 393224 | tf_op jit(solution)/shard_map/ppermute | solution.py:19
  66.3 2.5 %shard_map.79 = f32[16,2048]{1,0:T(8,128)S(1)} custom-call(bf16[768,128]{1,0:T(8,128)(2,1)S(1)} %fusion.5.refs_0_, bf16[768,128]{1,0:T(8,128)(2,1)S(1)} %fusion.4.refs_1_, bf16[1024,128]{1,0:T(8,128)(2,1)S(1)} %get-tuple-element.10.refs_0_.refs_2_, bf16[1024,128]{1,0:T(8,128)(2,1)S(1)} %get-tuple-element.11.refs_1_.refs_3_, ...), custom_call_target="tpu_custom_call" | custom-call | flops 805306368 | bytes 4194304 | tf_op jit(solution)/shard_map/pallas_call | solution.py:159
  68.9 1.0 collective-permute-done.17.refs_0_
  69.8 2.5 %shard_map.82 = f32[16,2048]{1,0:T(8,128)S(1)} custom-call(bf16[768,128]{1,0:T(8,128)(2,1)S(1)} %collective-permute-done.17.refs_0_, bf16[768,128]{1,0:T(8,128)(2,1)S(1)} %collective-permute-done.18.refs_1_, bf16[1024,128]{1,0:T(8,128)(2,1)S(1)} %collective-permute-done.6.refs_2_, bf16[1024,128]{1,0:T(8,128)(2,1)S(1)} %collective-permute-done.12.refs_3_, ...), custom_call_target="tpu_custom_call" | custom-call | flops 805306368 | bytes 4194304 | tf_op jit(solution)/shard_map/pallas_call | solution.py:159
  72.4 1.6 %collective-permute-start.19 = (f32[16,2048]{1,0:T(8,128)S(1)}, f32[16,2048]{1,0:T(8,128)S(1)}, u32[]{:S(2)}, u32[]{:S(2)}) collective-permute-start(f32[16,2048]{1,0:T(8,128)S(1)} %shard_map.82), channel_id=1, source_target_pairs={{0,2},{1,3},{2,0},{3,1},{4,6},{5,7},{6,4},{7,5},{8,10},{9,11},{10,... | collective-permute-start | bytes 393224 | tf_op jit(solution)/shard_map/ppermute | solution.py:19
  74.0 2.5 %shard_map.81 = f32[16,2048]{1,0:T(8,128)S(1)} custom-call(bf16[768,128]{1,0:T(8,128)(2,1)S(1)} %collective-permute-done.17.refs_0_, bf16[768,128]{1,0:T(8,128)(2,1)S(1)} %collective-permute-done.18.refs_1_, bf16[1024,128]{1,0:T(8,128)(2,1)S(1)} %get-tuple-element.10.refs_0_.refs_2_, bf16[1024,128]{1,0:T(8,128)(2,1)S(1)} %get-tuple-element.11.refs_1_.refs_3_, ...), custom_call_target="tpu_custom_call" | custom-call | flops 805306368 | bytes 4194304 | tf_op jit(solution)/shard_map/pallas_call | solution.py:159
  76.5 0.9 collective-permute-done.19
  77.5 2.1 %fusion.8 = f32[32,1024]{1,0:T(8,128)S(1)} fusion(bf16[1024,1024]{1,0:T(8,128)(2,1)} %param.9, bf16[32,2048]{1,0:T(8,128)(2,1)S(1)} %bitcast_convert_fusion), kind=kOutput, calls=%fused_computation.31 | convolution fusion | flops 67108864 | bytes 2293760 | tf_op jit(solution)/shard_map/dot_general | solution.py:28
  79.6 2.1 %convolution_add_fusion.4 = f32[32,1024]{1,0:T(8,128)S(1)} fusion(f32[32,1024]{1,0:T(8,128)S(1)} %fusion.8, bf16[1024,1024]{1,0:T(8,128)(2,1)} %collective-permute-done.20, bf16[32,2048]{1,0:T(8,128)(2,1)S(1)} %bitcast_convert_fusion), kind=kOutput, calls=%fused_computation.10 | convolution fusion | flops 67141632 | bytes 2424832 | tf_op jit(solution)/shard_map/dot_general | solution.py:28
  81.6 1.5 %collective-permute-start.21 = (f32[32,1024]{1,0:T(8,128)S(1)}, f32[32,1024]{1,0:T(8,128)S(1)}, u32[]{:S(2)}, u32[]{:S(2)}) collective-permute-start(f32[32,1024]{1,0:T(8,128)S(1)} %convolution_add_fusion.4), channel_id=1, source_target_pairs={{0,2},{1,3},{2,0},{3,1},{4,6},{5,7},{6,4},{7,5},{8,10},{9,11},{10,... | collective-permute-start | bytes 393224 | tf_op jit(solution)/shard_map/ppermute | solution.py:19
  83.2 3.5 %collective-permute-done.21 = f32[32,1024]{1,0:T(8,128)S(1)} collective-permute-done((f32[32,1024]{1,0:T(8,128)S(1)}, f32[32,1024]{1,0:T(8,128)S(1)}, u32[]{:S(2)}, u32[]{:S(2)}) %collective-permute-start.21) | collective-permute-done | bytes 131104 | tf_op jit(solution)/shard_map/ppermute | solution.py:19
  86.7 1.4 %collective-permute-start.22 = (f32[32,1024]{1,0:T(8,128)S(1)}, f32[32,1024]{1,0:T(8,128)S(1)}, u32[]{:S(2)}, u32[]{:S(2)}) collective-permute-start(f32[32,1024]{1,0:T(8,128)S(1)} %add.148), channel_id=1, source_target_pairs={{0,4},{1,5},{2,6},{3,7},{4,0},{5,1},{6,2},{7,3},{8,12},{9,13},{10,... | collective-permute-start | bytes 393224 | tf_op jit(solution)/shard_map/ppermute | solution.py:19
  88.1 3.7 %collective-permute-done.22 = f32[32,1024]{1,0:T(8,128)S(1)} collective-permute-done((f32[32,1024]{1,0:T(8,128)S(1)}, f32[32,1024]{1,0:T(8,128)S(1)}, u32[]{:S(2)}, u32[]{:S(2)}) %collective-permute-start.22) | collective-permute-done | bytes 131104 | tf_op jit(solution)/shard_map/ppermute | solution.py:19
  91.7 3.9 %collective-permute-start.23 = (bf16[32,1024]{1,0:T(8,128)(2,1)S(1)}, bf16[32,1024]{1,0:T(8,128)(2,1)S(1)}, u32[]{:S(2)}, u32[]{:S(2)}) collective-permute-start(bf16[32,1024]{1,0:T(8,128)(2,1)S(1)} %get-tuple-element.20), channel_id=1, source_target_pairs={{0,8},{1,9},{2,10},{3,11},{4,12},{5,13},{6,14},{7,15},{8,0},{9,1},... | collective-permute-start | bytes 196616 | tf_op jit(solution)/shard_map/ppermute | solution.py:19
  95.6 2.8 %collective-permute-done.23 = bf16[32,1024]{1,0:T(8,128)(2,1)S(1)} collective-permute-done((bf16[32,1024]{1,0:T(8,128)(2,1)S(1)}, bf16[32,1024]{1,0:T(8,128)(2,1)S(1)}, u32[]{:S(2)}, u32[]{:S(2)}) %collective-permute-start.23) | collective-permute-done | bytes 65568 | tf_op jit(solution)/shard_map/ppermute | solution.py:19
  98.4 2.4 %multiply_reduce_fusion = (f32[32]{0:T(128)S(1)}, f32[32,1024]{1,0:T(8,128)S(1)}) fusion(bf16[1024,1024]{1,0:T(8,128)(2,1)} %param.9, f32[32,1024]{1,0:T(8,128)S(1)} %get-tuple-element.21, bf16[32,1024]{1,0:T(8,128)(2,1)S(1)} %collective-permute-done.23, f32[32,2048]{1,0:T(8,128)S(1)} %bitcast.65), kind=kOutput, calls=%fused_computation.24 | convolution fusion | flops 67305440 | bytes 2556032 | tf_op jit(solution)/shard_map/dot_general | solution.py:32
  100.8 2.4 %multiply_reduce_fusion.1 = (f32[32]{0:T(128)S(1)}, f32[32,1024]{1,0:T(8,128)S(1)}) fusion(bf16[1024,1024]{1,0:T(8,128)(2,1)} %collective-permute-done.20, f32[32,1024]{1,0:T(8,128)S(1)} %get-tuple-element.21, bf16[32,1024]{1,0:T(8,128)(2,1)S(1)} %collective-permute-done.23, f32[32,2048]{1,0:T(8,128)S(1)} %bitcast.66), kind=kOutput, calls=%fused_computation.25 | convolution fusion | flops 67305440 | bytes 2556032 | tf_op jit(solution)/shard_map/dot_general | solution.py:32
  103.4 2.6 %collective-permute-start.27 = (f32[1,32]{1,0:T(1,128)S(1)}, f32[1,32]{1,0:T(1,128)S(1)}, u32[]{:S(2)}, u32[]{:S(2)}) collective-permute-start(f32[1,32]{1,0:T(1,128)S(1)} %add_bitcast_fusion.2), channel_id=1, source_target_pairs={{0,8},{1,9},{2,10},{3,11},{4,12},{5,13},{6,14},{7,15},{8,0},{9,1},... | collective-permute-start | bytes 392 | tf_op jit(solution)/shard_map/ppermute | solution.py:19
  106.0 1.7 %collective-permute-start.28 = (f32[1,32]{1,0:T(1,128)S(1)}, f32[1,32]{1,0:T(1,128)S(1)}, u32[]{:S(2)}, u32[]{:S(2)}) collective-permute-start(f32[1,32]{1,0:T(1,128)S(1)} %add_bitcast_fusion.2), channel_id=1, source_target_pairs={{0,12},{1,13},{2,14},{3,15},{4,8},{5,9},{6,10},{7,11},{8,4},{9,5},... | collective-permute-start | bytes 392 | tf_op jit(solution)/shard_map/ppermute | solution.py:19
  108.1 0.5 collective-permute-start.24
  108.6 2.8 %collective-permute-done.28 = f32[1,32]{1,0:T(1,128)S(1)} collective-permute-done((f32[1,32]{1,0:T(1,128)S(1)}, f32[1,32]{1,0:T(1,128)S(1)}, u32[]{:S(2)}, u32[]{:S(2)}) %collective-permute-start.28) | collective-permute-done | bytes 160 | tf_op jit(solution)/shard_map/ppermute | solution.py:19
  111.4 2.2 %collective-permute-start.29 = (f32[1,32]{1,0:T(1,128)S(1)}, f32[1,32]{1,0:T(1,128)S(1)}, u32[]{:S(2)}, u32[]{:S(2)}) collective-permute-start(f32[1,32]{1,0:T(1,128)S(1)} %add_add_fusion), channel_id=1, source_target_pairs={{0,2},{1,3},{2,0},{3,1},{4,6},{5,7},{6,4},{7,5},{8,10},{9,11},{10,... | collective-permute-start | bytes 392 | tf_op jit(solution)/shard_map/ppermute | solution.py:19
  113.6 0.2 collective-permute-start.31
  113.8 1.4 %collective-permute-done.29 = f32[1,32]{1,0:T(1,128)S(1)} collective-permute-done((f32[1,32]{1,0:T(1,128)S(1)}, f32[1,32]{1,0:T(1,128)S(1)}, u32[]{:S(2)}, u32[]{:S(2)}) %collective-permute-start.29) | collective-permute-done | bytes 160 | tf_op jit(solution)/shard_map/ppermute | solution.py:19
  115.1 1.4 %collective-permute-done.31 = f32[1,32]{1,0:T(1,128)S(1)} collective-permute-done((f32[1,32]{1,0:T(1,128)S(1)}, f32[1,32]{1,0:T(1,128)S(1)}, u32[]{:S(2)}, u32[]{:S(2)}) %collective-permute-start.31) | collective-permute-done | bytes 160 | tf_op jit(solution)/shard_map/ppermute | solution.py:19
  116.7 0.7 copy.8
  117.4 0.8 broadcast_divide_fusion
  (55 shorter events, 1.5 us)
Async XLA Ops:
  0.6 29.8 %collective-permute-start.1 = (bf16[64,1024]{1,0:T(8,128)(2,1)}, bf16[64,1024]{1,0:T(8,128)(2,1)S(1)}, u32[]{:S(2)}, u32[]{:S(2)}) collective-permute-start(bf16[64,1024]{1,0:T(8,128)(2,1)} %bitcast.49), channel_id=1, source_target_pairs={{0,1},{1,0},{2,3},{3,2},{4,5},{5,4},{6,7},{7,6},{8,9},{9,8},{10,11... | collective-permute-start | bytes 393224 | tf_op jit(solution)/shard_map/ppermute | solution.py:19
  1.2 7.1 %collective-permute-start.4 = (bf16[64,1024]{1,0:T(8,128)(2,1)}, bf16[64,1024]{1,0:T(8,128)(2,1)S(1)}, u32[]{:S(2)}, u32[]{:S(2)}) collective-permute-start(bf16[64,1024]{1,0:T(8,128)(2,1)} %bitcast.50), channel_id=1, source_target_pairs={{0,2},{1,3},{2,0},{3,1},{4,6},{5,7},{6,4},{7,5},{8,10},{9,11},{10,... | collective-permute-start | bytes 393224 | tf_op jit(solution)/shard_map/ppermute | solution.py:19
  3.8 26.1 %collective-permute-start = (bf16[48,1024]{1,0:T(8,128)(2,1)}, bf16[48,1024]{1,0:T(8,128)(2,1)S(1)}, u32[]{:S(2)}, u32[]{:S(2)}) collective-permute-start(bf16[48,1024]{1,0:T(8,128)(2,1)} %bitcast.52), channel_id=1, source_target_pairs={{0,1},{1,0},{2,3},{3,2},{4,5},{5,4},{6,7},{7,6},{8,9},{9,8},{10,11... | collective-permute-start | bytes 294920 | tf_op jit(solution)/shard_map/ppermute | solution.py:19
  3.9 6.3 %collective-permute-start.5 = (bf16[48,1024]{1,0:T(8,128)(2,1)}, bf16[48,1024]{1,0:T(8,128)(2,1)S(1)}, u32[]{:S(2)}, u32[]{:S(2)}) collective-permute-start(bf16[48,1024]{1,0:T(8,128)(2,1)} %bitcast.53), channel_id=1, source_target_pairs={{0,2},{1,3},{2,0},{3,1},{4,6},{5,7},{6,4},{7,5},{8,10},{9,11},{10,... | collective-permute-start | bytes 294920 | tf_op jit(solution)/shard_map/ppermute | solution.py:19
  4.2 1.2 %copy-start = (bf16[1024,512]{1,0:T(8,128)(2,1)S(1)}, bf16[1024,512]{1,0:T(8,128)(2,1)}, u32[]{:S(2)}) copy-start(bf16[1024,512]{1,0:T(8,128)(2,1)} %cond_ref.1) | copy-start | bytes 3145732
  5.6 24.8 %collective-permute-start.2 = (bf16[1024,128]{1,0:T(8,128)(2,1)S(1)}, bf16[1024,128]{1,0:T(8,128)(2,1)S(1)}, u32[]{:S(2)}, u32[]{:S(2)}) collective-permute-start(bf16[1024,128]{1,0:T(8,128)(2,1)S(1)} %get-tuple-element.10.refs_0_.refs_2_), channel_id=1, source_target_pairs={{0,1},{1,0},{2,3},{3,2},{4,5},{5,4},{6,7},{7,6},{8,9},{9,8},{10,11... | collective-permute-start | bytes 786440 | tf_op jit(solution)/shard_map/ppermute | solution.py:19
  8.3 22.1 %collective-permute-start.3 = (bf16[1024,128]{1,0:T(8,128)(2,1)S(1)}, bf16[1024,128]{1,0:T(8,128)(2,1)S(1)}, u32[]{:S(2)}, u32[]{:S(2)}) collective-permute-start(bf16[1024,128]{1,0:T(8,128)(2,1)S(1)} %get-tuple-element.11.refs_1_.refs_3_), channel_id=1, source_target_pairs={{0,1},{1,0},{2,3},{3,2},{4,5},{5,4},{6,7},{7,6},{8,9},{9,8},{10,11... | collective-permute-start | bytes 786440 | tf_op jit(solution)/shard_map/ppermute | solution.py:19
  10.2 8.1 %collective-permute-start.12 = (bf16[1024,128]{1,0:T(8,128)(2,1)S(1)}, bf16[1024,128]{1,0:T(8,128)(2,1)S(1)}, u32[]{:S(2)}, u32[]{:S(2)}) collective-permute-start(bf16[1024,128]{1,0:T(8,128)(2,1)S(1)} %get-tuple-element.16), channel_id=1, source_target_pairs={{0,2},{1,3},{2,0},{3,1},{4,6},{5,7},{6,4},{7,5},{8,10},{9,11},{10,... | collective-permute-start | bytes 786440 | tf_op jit(solution)/shard_map/ppermute | solution.py:19
  18.2 1.3 %collective-permute-start.7 = (bf16[64,1024]{1,0:T(8,128)(2,1)S(1)}, bf16[64,1024]{1,0:T(8,128)(2,1)S(1)}, u32[]{:S(2)}, u32[]{:S(2)}) collective-permute-start(bf16[64,1024]{1,0:T(8,128)(2,1)S(1)} %collective-permute-done.4), channel_id=1, source_target_pairs={{0,1},{1,0},{2,3},{3,2},{4,5},{5,4},{6,7},{7,6},{8,9},{9,8},{10,11... | collective-permute-start | bytes 393224 | tf_op jit(solution)/shard_map/ppermute | solution.py:19
  19.6 1.3 %collective-permute-start.8 = (bf16[48,1024]{1,0:T(8,128)(2,1)S(1)}, bf16[48,1024]{1,0:T(8,128)(2,1)S(1)}, u32[]{:S(2)}, u32[]{:S(2)}) collective-permute-start(bf16[48,1024]{1,0:T(8,128)(2,1)S(1)} %collective-permute-done.5.refs_6_), channel_id=1, source_target_pairs={{0,1},{1,0},{2,3},{3,2},{4,5},{5,4},{6,7},{7,6},{8,9},{9,8},{10,11... | collective-permute-start | bytes 294920 | tf_op jit(solution)/shard_map/ppermute | solution.py:19
  20.9 8.4 %collective-permute-start.6 = (bf16[1024,128]{1,0:T(8,128)(2,1)S(1)}, bf16[1024,128]{1,0:T(8,128)(2,1)S(1)}, u32[]{:S(2)}, u32[]{:S(2)}) collective-permute-start(bf16[1024,128]{1,0:T(8,128)(2,1)S(1)} %get-tuple-element.13), channel_id=1, source_target_pairs={{0,2},{1,3},{2,0},{3,1},{4,6},{5,7},{6,4},{7,5},{8,10},{9,11},{10,... | collective-permute-start | bytes 786440 | tf_op jit(solution)/shard_map/ppermute | solution.py:19
  23.1 7.3 %copy-start.1 = (bf16[1024,64]{0,1:T(8,128)(2,1)S(1)}, bf16[1024,64]{0,1:T(8,128)(2,1)}, u32[]{:S(2)}) copy-start(bf16[1024,64]{0,1:T(8,128)(2,1)} %param.8) | copy-start | bytes 393220
  23.2 7.3 %copy-start.2 = (bf16[1024,48]{0,1:T(8,128)(2,1)S(1)}, bf16[1024,48]{0,1:T(8,128)(2,1)}, u32[]{:S(2)}) copy-start(bf16[1024,48]{0,1:T(8,128)(2,1)} %param.6) | copy-start | bytes 294916
  29.3 4.3 %collective-permute-start.13 = (bf16[1024,128]{1,0:T(8,128)(2,1)S(1)}, bf16[1024,128]{1,0:T(8,128)(2,1)S(1)}, u32[]{:S(2)}, u32[]{:S(2)}) collective-permute-start(bf16[1024,128]{1,0:T(8,128)(2,1)S(1)} %collective-permute-done.12.refs_3_), channel_id=1, source_target_pairs={{0,1},{1,0},{2,3},{3,2},{4,5},{5,4},{6,7},{7,6},{8,9},{9,8},{10,11... | collective-permute-start | bytes 786440 | tf_op jit(solution)/shard_map/ppermute | solution.py:19
  29.8 5.9 %collective-permute-start.9 = (bf16[1024,128]{1,0:T(8,128)(2,1)S(1)}, bf16[1024,128]{1,0:T(8,128)(2,1)S(1)}, u32[]{:S(2)}, u32[]{:S(2)}) collective-permute-start(bf16[1024,128]{1,0:T(8,128)(2,1)S(1)} %collective-permute-done.6.refs_2_), channel_id=1, source_target_pairs={{0,1},{1,0},{2,3},{3,2},{4,5},{5,4},{6,7},{7,6},{8,9},{9,8},{10,11... | collective-permute-start | bytes 786440 | tf_op jit(solution)/shard_map/ppermute | solution.py:19
  34.1 7.8 %collective-permute-start.14 = (bf16[768,128]{1,0:T(8,128)(2,1)S(1)}, bf16[768,128]{1,0:T(8,128)(2,1)S(1)}, u32[]{:S(2)}, u32[]{:S(2)}) collective-permute-start(bf16[768,128]{1,0:T(8,128)(2,1)S(1)} %fusion.3), channel_id=1, source_target_pairs={{0,4},{1,5},{2,6},{3,7},{4,0},{5,1},{6,2},{7,3},{8,12},{9,13},{10,... | collective-permute-start | bytes 589832 | tf_op jit(solution)/shard_map/ppermute | solution.py:19
  36.3 11.3 %collective-permute-start.10 = (bf16[768,128]{1,0:T(8,128)(2,1)S(1)}, bf16[768,128]{1,0:T(8,128)(2,1)S(1)}, u32[]{:S(2)}, u32[]{:S(2)}) collective-permute-start(bf16[768,128]{1,0:T(8,128)(2,1)S(1)} %fusion.2), channel_id=1, source_target_pairs={{0,4},{1,5},{2,6},{3,7},{4,0},{5,1},{6,2},{7,3},{8,12},{9,13},{10,... | collective-permute-start | bytes 589832 | tf_op jit(solution)/shard_map/ppermute | solution.py:19
  42.6 16.2 %collective-permute-start.15 = (bf16[768,128]{1,0:T(8,128)(2,1)S(1)}, bf16[768,128]{1,0:T(8,128)(2,1)S(1)}, u32[]{:S(2)}, u32[]{:S(2)}) collective-permute-start(bf16[768,128]{1,0:T(8,128)(2,1)S(1)} %get-tuple-element.36), channel_id=1, source_target_pairs={{0,8},{1,9},{2,10},{3,11},{4,12},{5,13},{6,14},{7,15},{8,0},{9,1},... | collective-permute-start | bytes 589832 | tf_op jit(solution)/shard_map/ppermute | solution.py:19
  48.2 13.3 %collective-permute-start.11 = (bf16[768,128]{1,0:T(8,128)(2,1)S(1)}, bf16[768,128]{1,0:T(8,128)(2,1)S(1)}, u32[]{:S(2)}, u32[]{:S(2)}) collective-permute-start(bf16[768,128]{1,0:T(8,128)(2,1)S(1)} %get-tuple-element.34), channel_id=1, source_target_pairs={{0,8},{1,9},{2,10},{3,11},{4,12},{5,13},{6,14},{7,15},{8,0},{9,1},... | collective-permute-start | bytes 589832 | tf_op jit(solution)/shard_map/ppermute | solution.py:19
  58.8 10.0 %collective-permute-start.18 = (bf16[768,128]{1,0:T(8,128)(2,1)S(1)}, bf16[768,128]{1,0:T(8,128)(2,1)S(1)}, u32[]{:S(2)}, u32[]{:S(2)}) collective-permute-start(bf16[768,128]{1,0:T(8,128)(2,1)S(1)} %fusion.4.refs_1_), channel_id=1, source_target_pairs={{0,4},{1,5},{2,6},{3,7},{4,0},{5,1},{6,2},{7,3},{8,12},{9,13},{10,... | collective-permute-start | bytes 589832 | tf_op jit(solution)/shard_map/ppermute | solution.py:19
  61.6 8.3 %collective-permute-start.17 = (bf16[768,128]{1,0:T(8,128)(2,1)S(1)}, bf16[768,128]{1,0:T(8,128)(2,1)S(1)}, u32[]{:S(2)}, u32[]{:S(2)}) collective-permute-start(bf16[768,128]{1,0:T(8,128)(2,1)S(1)} %fusion.5.refs_0_), channel_id=1, source_target_pairs={{0,4},{1,5},{2,6},{3,7},{4,0},{5,1},{6,2},{7,3},{8,12},{9,13},{10,... | collective-permute-start | bytes 589832 | tf_op jit(solution)/shard_map/ppermute | solution.py:19
  62.1 17.5 %collective-permute-start.20 = (bf16[1024,1024]{1,0:T(8,128)(2,1)}, bf16[1024,1024]{1,0:T(8,128)(2,1)}, u32[]{:S(2)}, u32[]{:S(2)}) collective-permute-start(bf16[1024,1024]{1,0:T(8,128)(2,1)} %param.9), channel_id=1, source_target_pairs={{0,1},{1,0},{2,3},{3,2},{4,5},{5,4},{6,7},{7,6},{8,9},{9,8},{10,11... | collective-permute-start | bytes 6291464 | tf_op jit(solution)/shard_map/ppermute | solution.py:19
  64.8 9.2 %collective-permute-start.16 = (f32[16,2048]{1,0:T(8,128)S(1)}, f32[16,2048]{1,0:T(8,128)S(1)}, u32[]{:S(2)}, u32[]{:S(2)}) collective-permute-start(f32[16,2048]{1,0:T(8,128)S(1)} %shard_map.80), channel_id=1, source_target_pairs={{0,2},{1,3},{2,0},{3,1},{4,6},{5,7},{6,4},{7,5},{8,10},{9,11},{10,... | collective-permute-start | bytes 393224 | tf_op jit(solution)/shard_map/ppermute | solution.py:19
  72.4 5.0 %collective-permute-start.19 = (f32[16,2048]{1,0:T(8,128)S(1)}, f32[16,2048]{1,0:T(8,128)S(1)}, u32[]{:S(2)}, u32[]{:S(2)}) collective-permute-start(f32[16,2048]{1,0:T(8,128)S(1)} %shard_map.82), channel_id=1, source_target_pairs={{0,2},{1,3},{2,0},{3,1},{4,6},{5,7},{6,4},{7,5},{8,10},{9,11},{10,... | collective-permute-start | bytes 393224 | tf_op jit(solution)/shard_map/ppermute | solution.py:19
  81.6 5.0 %collective-permute-start.21 = (f32[32,1024]{1,0:T(8,128)S(1)}, f32[32,1024]{1,0:T(8,128)S(1)}, u32[]{:S(2)}, u32[]{:S(2)}) collective-permute-start(f32[32,1024]{1,0:T(8,128)S(1)} %convolution_add_fusion.4), channel_id=1, source_target_pairs={{0,2},{1,3},{2,0},{3,1},{4,6},{5,7},{6,4},{7,5},{8,10},{9,11},{10,... | collective-permute-start | bytes 393224 | tf_op jit(solution)/shard_map/ppermute | solution.py:19
  86.7 5.0 %collective-permute-start.22 = (f32[32,1024]{1,0:T(8,128)S(1)}, f32[32,1024]{1,0:T(8,128)S(1)}, u32[]{:S(2)}, u32[]{:S(2)}) collective-permute-start(f32[32,1024]{1,0:T(8,128)S(1)} %add.148), channel_id=1, source_target_pairs={{0,4},{1,5},{2,6},{3,7},{4,0},{5,1},{6,2},{7,3},{8,12},{9,13},{10,... | collective-permute-start | bytes 393224 | tf_op jit(solution)/shard_map/ppermute | solution.py:19
  91.7 6.7 %collective-permute-start.23 = (bf16[32,1024]{1,0:T(8,128)(2,1)S(1)}, bf16[32,1024]{1,0:T(8,128)(2,1)S(1)}, u32[]{:S(2)}, u32[]{:S(2)}) collective-permute-start(bf16[32,1024]{1,0:T(8,128)(2,1)S(1)} %get-tuple-element.20), channel_id=1, source_target_pairs={{0,8},{1,9},{2,10},{3,11},{4,12},{5,13},{6,14},{7,15},{8,0},{9,1},... | collective-permute-start | bytes 196616 | tf_op jit(solution)/shard_map/ppermute | solution.py:19
  103.3 5.3 %collective-permute-start.26 = (f32[1,32]{1,0:T(1,128)S(1)}, f32[1,32]{1,0:T(1,128)S(1)}, u32[]{:S(2)}, u32[]{:S(2)}) collective-permute-start(f32[1,32]{1,0:T(1,128)S(1)} %add_bitcast_fusion.2), channel_id=1, source_target_pairs={{0,4},{1,5},{2,6},{3,7},{4,0},{5,1},{6,2},{7,3},{8,12},{9,13},{10,... | collective-permute-start | bytes 392 | tf_op jit(solution)/shard_map/ppermute | solution.py:19
  103.4 5.2 %collective-permute-start.27 = (f32[1,32]{1,0:T(1,128)S(1)}, f32[1,32]{1,0:T(1,128)S(1)}, u32[]{:S(2)}, u32[]{:S(2)}) collective-permute-start(f32[1,32]{1,0:T(1,128)S(1)} %add_bitcast_fusion.2), channel_id=1, source_target_pairs={{0,8},{1,9},{2,10},{3,11},{4,12},{5,13},{6,14},{7,15},{8,0},{9,1},... | collective-permute-start | bytes 392 | tf_op jit(solution)/shard_map/ppermute | solution.py:19
  106.0 5.4 %collective-permute-start.28 = (f32[1,32]{1,0:T(1,128)S(1)}, f32[1,32]{1,0:T(1,128)S(1)}, u32[]{:S(2)}, u32[]{:S(2)}) collective-permute-start(f32[1,32]{1,0:T(1,128)S(1)} %add_bitcast_fusion.2), channel_id=1, source_target_pairs={{0,12},{1,13},{2,14},{3,15},{4,8},{5,9},{6,10},{7,11},{8,4},{9,5},... | collective-permute-start | bytes 392 | tf_op jit(solution)/shard_map/ppermute | solution.py:19
  107.7 9.7 %collective-permute-start.25 = (f32[32,1024]{1,0:T(8,128)S(1)}, f32[32,1024]{1,0:T(8,128)S(1)}, u32[]{:S(2)}, u32[]{:S(2)}) collective-permute-start(f32[32,1024]{1,0:T(8,128)S(1)} %get-tuple-element.39), channel_id=1, source_target_pairs={{0,1},{1,0},{2,3},{3,2},{4,5},{5,4},{6,7},{7,6},{8,9},{9,8},{10,11... | collective-permute-start | bytes 393224 | tf_op jit(solution)/shard_map/ppermute | solution.py:19
  108.1 8.6 %collective-permute-start.24 = (f32[32,64]{1,0:T(8,128)S(1)}, f32[32,64]{1,0:T(8,128)S(1)}, u32[]{:S(2)}, u32[]{:S(2)}) collective-permute-start(f32[32,64]{1,0:T(8,128)S(1)} %get-tuple-element.23), channel_id=1, source_target_pairs={{0,1},{1,0},{2,3},{3,2},{4,5},{5,4},{6,7},{7,6},{8,9},{9,8},{10,11... | collective-permute-start | bytes 24584 | tf_op jit(solution)/shard_map/ppermute | solution.py:19
  111.4 3.8 %collective-permute-start.29 = (f32[1,32]{1,0:T(1,128)S(1)}, f32[1,32]{1,0:T(1,128)S(1)}, u32[]{:S(2)}, u32[]{:S(2)}) collective-permute-start(f32[1,32]{1,0:T(1,128)S(1)} %add_add_fusion), channel_id=1, source_target_pairs={{0,2},{1,3},{2,0},{3,1},{4,6},{5,7},{6,4},{7,5},{8,10},{9,11},{10,... | collective-permute-start | bytes 392 | tf_op jit(solution)/shard_map/ppermute | solution.py:19
  113.6 1.6 %collective-permute-start.30 = (f32[1,32]{1,0:T(1,128)S(1)}, f32[1,32]{1,0:T(1,128)S(1)}, u32[]{:S(2)}, u32[]{:S(2)}) collective-permute-start(f32[1,32]{1,0:T(1,128)S(1)} %add_add_fusion), channel_id=1, source_target_pairs={{0,1},{1,0},{2,3},{3,2},{4,5},{5,4},{6,7},{7,6},{8,9},{9,8},{10,11... | collective-permute-start | bytes 392 | tf_op jit(solution)/shard_map/ppermute | solution.py:19
  113.6 3.0 %collective-permute-start.31 = (f32[1,32]{1,0:T(1,128)S(1)}, f32[1,32]{1,0:T(1,128)S(1)}, u32[]{:S(2)}, u32[]{:S(2)}) collective-permute-start(f32[1,32]{1,0:T(1,128)S(1)} %add_add_fusion), channel_id=1, source_target_pairs={{0,3},{1,2},{2,1},{3,0},{4,7},{5,6},{6,5},{7,4},{8,11},{9,10},{10,... | collective-permute-start | bytes 392 | tf_op jit(solution)/shard_map/ppermute | solution.py:19

commit v3 on v2

--- a/solution.py
+++ b/solution.py
@@ -11,7 +11,7 @@
 F32 = jnp.float32
 BF16 = jnp.bfloat16
 CHUNKS = 2
-PIECES = 1
+PIECES = 2
 
 
 def swap(block, bit):
@@ -117,7 +117,8 @@
     def cut(block):
         return jnp.split(block, PIECES, axis=0)
 
-    scaled_mine, scaled_rest = [], []
+    scaled_own = [[None] * CHUNKS for _ in range(PIECES)]
+    scaled_rest = [[None] * CHUNKS for _ in range(PIECES)]
     for part in parts:
         totals = [None] * PIECES
         for level, bit in enumerate(spread):
@@ -126,63 +127,51 @@
             for q in range(PIECES):
                 send, many = mine[q], mine[q].shape[0]
                 if totals[q] is not None:
+                    totals[q] = totals[q].astype(F32)
                     send = send + lax.dynamic_slice(totals[q], ((1 - up) * many, 0), send.shape)
                     totals[q] = lax.dynamic_slice(totals[q], (up * many, 0), send.shape)
-                got = swap(send.astype(BF16), bit).astype(F32)
-                totals[q] = got if totals[q] is None else totals[q] + got
-        mine = cut(coefficients(len(spread), part))
+                got = swap(send.astype(BF16), bit)
+                totals[q] = got if totals[q] is None else totals[q] + got.astype(F32)
+        mine = coefficients(len(spread), part)
         factor = factors[:, part * c_part : (part + 1) * c_part]
-        own, rest = [], []
         for q in range(PIECES):
-            total = mine[q] if totals[q] is None else mine[q] + totals[q]
-            total = total + swap(total.astype(BF16), last).astype(F32)
-            many = total.shape[0] // val_count
-            shaped = total.reshape(many, val_count, c_part)
-            scaled = (shaped * factor[None]).astype(BF16).reshape(total.shape)
-            own.append(scaled)
+            total, low = added(mine, totals[q], q)
+            scaled = rescaled(total, swap(low, last), factor)
+            scaled_own[q][part] = scaled
             others = []
             for level in reversed(range(len(spread))):
                 known = jnp.concatenate([scaled] + others, axis=0)
                 others.append(swap(known, spread[level]))
             if others:
-                rest.append(jnp.concatenate(others, axis=0))
-        scaled_mine.append(own)
-        scaled_rest.append(rest)
+                scaled_rest[q][part] = jnp.concatenate(others, axis=0)
+
     many = k_half // PIECES >> len(spread)
 
-    def respond(blocks, places):
-        kernel = functools.partial(respond_kernel, len(places), CHUNKS, len(blocks[0]))
-        operands = [block for column in blocks for block in column]
-        operands += [cond_all[place][part] for place in places for part in parts]
-        operands += [vals[place] for place in places]
-        height = sum(block.shape[0] for block in blocks[0])
-        return pl.pallas_call(
-            kernel,
-            out_shape=jax.ShapeDtypeStruct((height // val_count, rows * len(places)), F32),
-            in_specs=[pl.BlockSpec(memory_space=pltpu.VMEM)] * len(operands),
-            out_specs=pl.BlockSpec(memory_space=pltpu.VMEM),
-            scratch_shapes=[pltpu.VMEM((height, c_half), BF16)],
-            compiler_params=pltpu.CompilerParams(vmem_limit_bytes=8 * 2**20),
-            cost_estimate=pl.CostEstimate(
-                flops=2 * height * c_half * rows * len(places), bytes_accessed=2**22, transcendentals=0
-            ),
-        )(*operands)
+    cond_turned = turned([column for column in cond_all])
+    eig_turned = turned([[eigenpotentials], [eig_core]])
+
+    def respond(columns, places):
+        blocks = [block for column in columns for block in column]
+        height = sum(column[0].shape[0] for column in columns)
+        operands = [*blocks, cond_turned, *[vals[place] for place in places]]
+        kernel = functools.partial(respond_kernel, places, CHUNKS)
+        shape = jax.ShapeDtypeStruct((height // val_count, rows * len(places)), F32)
+        return in_vmem(kernel, shape, operands, 10**9, 8, [pltpu.VMEM((height, c_half), BF16)])
 
     here, there = (0, 1), (2, 3)
-    kinds = [scaled_mine] + ([scaled_rest] if spread else [])
     sums = []
-    for blocks in kinds:
-        arrived = swap(respond(blocks, there), 2)
-        sums.append(respond(blocks, here) + arrived)
-    width = sums[0].shape[1]
-    ordered = [block.reshape(PIECES, -1, many, width) for block in sums]
-    response = jnp.concatenate(ordered, axis=1).swapaxes(0, 1).reshape(k_half, width)
+    for columns in (scaled_own, scaled_rest):
+        if columns[0][0] is not None:
+            arrived = swap(respond(columns, there), 2)
+            total = respond(columns, here) + arrived
+            sums.append(total.reshape(PIECES, -1, many, total.shape[1]))
+    width = sums[0].shape[-1]
+    response = jnp.concatenate(sums, axis=1).swapaxes(0, 1).reshape(k_half, width)
     for level, bit in enumerate(spread):
         shaped = response.reshape(1 << level, 2, -1, width)
         response = jnp.where((me & bit) != 0, shaped[:, ::-1], shaped).reshape(k_half, width)
 
-    low = response.astype(BF16)
-    intersection = contract(low[:, :rows], eigenpotentials) + contract(low[:, rows:], eig_core)
+    intersection = intersect(response, eig_turned)
     for bit in [2] + spread:
         intersection = intersection + swap(intersection, bit)
     intersection = intersection + swap(intersection.astype(BF16), last).astype(F32)
@@ -196,22 +185,18 @@
     def joined(mine, other):
         return jnp.where(core == 0, jnp.concatenate([mine, other], 0), jnp.concatenate([other, mine], 0))
 
-    projected = joined(e_block(me), swap(e_block(me ^ 1), 1)).T
-
-    ilow = intersection.astype(BF16)
-    remainder_core = response[:, rows:] - contract_last(ilow, eig_core)
-    remainder_mine = response[:, :rows] - contract_last(ilow, eigenpotentials)
-    remainder_other = swap(remainder_core, 1)
-    share = jnp.sum(remainder_core * remainder_core, axis=1) + jnp.sum(remainder_mine * remainder_mine, axis=1)
-    share = share[None, :]
+    projected = finish(core, e_block(me), swap(e_block(me ^ 1), 1))
+    remainder, share = outside(response, intersection, [eigenpotentials, eig_core])
+    remainder_other = swap(remainder[:, rows:], 1)
+    share = share[:, :1].reshape(1, k_half)
     for low_bit, high_bit in zip(bits[::2], bits[1::2] + [0] * (len(bits) % 2)):
-        steps = [step for step in (low_bit, high_bit, low_bit | high_bit) if step and (high_bit or step == low_bit)]
-        share = share + sum(swap(share, step) for step in dict.fromkeys(steps))
+        steps = dict.fromkeys(step for step in (low_bit, high_bit, low_bit | high_bit) if step)
+        share = share + sum(swap(share, step) for step in steps)
     mine, other = share + swap(share, 2), swap(share, 1) + swap(share, 3)
     sums = joined(mine, other).reshape(pot_count)
     scale = jnp.sqrt(sums / points_total + 1e-06)
-    turned = lax.optimization_barrier(joined(remainder_mine, remainder_other).T)
-    return (projected, turned / scale[None, :])
+    final = lax.optimization_barrier(joined(remainder[:, :rows], remainder_other).T)
+    return (projected, final / scale[None, :])
 
 
 def prepare_kernel(chunks, side_ref, cond_ref, *blocks):
@@ -246,34 +231,126 @@
             outs[group * chunks + part][...] = total[:, part * width : (part + 1) * width]
 
 
-def respond_kernel(places, chunks, pieces, *refs):
-    scaled = refs[: chunks * pieces]
-    conds = refs[chunks * pieces :][: places * chunks]
-    vals = refs[chunks * pieces + places * chunks :][:places]
+def in_vmem(kernel, out_shape, operands, flops, megabytes, scratch=()):
+    return pl.pallas_call(
+        kernel,
+        out_shape=out_shape,
+        in_specs=[pl.BlockSpec(memory_space=pltpu.VMEM)] * len(operands),
+        out_specs=jax.tree.map(lambda _: pl.BlockSpec(memory_space=pltpu.VMEM), out_shape),
+        scratch_shapes=list(scratch),
+        compiler_params=pltpu.CompilerParams(vmem_limit_bytes=megabytes * 2**20),
+        cost_estimate=pl.CostEstimate(flops=flops, bytes_accessed=2**22, transcendentals=0),
+    )(*operands)
+
+
+def added(block, other, q):
+    height = block.shape[0] // PIECES
+
+    def kernel(block_ref, *refs):
+        total = block_ref[pl.ds(q * height, height), :]
+        for ref in refs[:-2]:
+            total = total + ref[...].astype(F32)
+        refs[-2][...] = total
+        refs[-1][...] = total.astype(BF16)
+
+    shapes = tuple(jax.ShapeDtypeStruct((height, block.shape[1]), kind) for kind in (F32, BF16))
+    operands = [block] if other is None else [block, other]
+    return in_vmem(kernel, shapes, operands, 10**6, 4)
+
+
+def rescaled(total, other, factor):
+    val_count = factor.shape[0]
+
+    def kernel(total_ref, other_ref, factor_ref, out_ref):
+        shaped = (total_ref[...] + other_ref[...].astype(F32)).reshape(-1, val_count, total_ref.shape[1])
+        out_ref[...] = (shaped * factor_ref[...][None]).reshape(total_ref.shape).astype(BF16)
+
+    shape = jax.ShapeDtypeStruct(total.shape, BF16)
+    return in_vmem(kernel, shape, [total, other, factor], 10**6, 4)
+
+
+def turned(columns):
+    rows = columns[0][0].shape[0]
+    depth = sum(block.shape[1] for block in columns[0])
+    blocks = [block for column in columns for block in column]
+
+    def kernel(*refs):
+        for index, ref in enumerate(refs[:-1]):
+            column, part = divmod(index, len(columns[0]))
+            size = ref.shape[1]
+            refs[-1][part * size : (part + 1) * size, column * rows : (column + 1) * rows] = ref[...].T
+
+    shape = jax.ShapeDtypeStruct((depth, rows * len(columns)), BF16)
+    return in_vmem(kernel, shape, blocks, 2 * 10**9, 12)
+
+
+def finish(core, mine, other):
+    def kernel(core_ref, mine_ref, other_ref, out_ref):
+        mine, other = mine_ref[...], other_ref[...]
+        first = core_ref[0] == 0
+        out_ref[...] = jnp.concatenate([jnp.where(first, mine, other), jnp.where(first, other, mine)], axis=0).T
+
+    return pl.pallas_call(
+        kernel,
+        out_shape=jax.ShapeDtypeStruct((mine.shape[1], 2 * mine.shape[0]), F32),
+        in_specs=[pl.BlockSpec(memory_space=pltpu.SMEM)] + [pl.BlockSpec(memory_space=pltpu.VMEM)] * 2,
+        out_specs=pl.BlockSpec(memory_space=pltpu.VMEM),
+        compiler_params=pltpu.CompilerParams(vmem_limit_bytes=2**21),
+        cost_estimate=pl.CostEstimate(flops=10**8, bytes_accessed=2**16, transcendentals=0),
+    )(core[None], mine, other)
+
+
+def intersect(response, eig_turned):
+    def kernel(response_ref, eig_ref, out_ref):
+        out_ref[...] = contract_last(eig_ref[...], response_ref[...].astype(BF16)).T
+
+    shape = jax.ShapeDtypeStruct((response.shape[0], eig_turned.shape[0]), F32)
+    return in_vmem(kernel, shape, [response, eig_turned], 10**9, 8)
+
+
+def outside(response, intersection, eig_blocks):
+    rows = eig_blocks[0].shape[0]
+
+    def kernel(response_ref, part_ref, *refs):
+        eigs, (out_ref, share_ref) = refs[:-2], refs[-2:]
+        low = part_ref[...].astype(BF16)
+        share = jnp.zeros((low.shape[0], 1), F32)
+        for index, eig in enumerate(eigs):
+            spot = slice(index * rows, (index + 1) * rows)
+            left = response_ref[:, spot] - contract_last(eig[...], low).T
+            out_ref[:, spot] = left
+            share = share + jnp.sum(left * left, axis=1, keepdims=True)
+        share_ref[...] = jnp.broadcast_to(share, share_ref.shape)
+
+    shapes = (
+        jax.ShapeDtypeStruct(response.shape, F32),
+        jax.ShapeDtypeStruct((response.shape[0], 128), F32),
+    )
+    return in_vmem(kernel, shapes, [response, intersection, *eig_blocks], 10**9, 12)
+
+
+def respond_kernel(places, chunks, *refs):
+    vals = refs[-2 - len(places) : -2]
+    right, scaled = refs[-3 - len(places)], refs[: -3 - len(places)]
     out, left = refs[-2:]
     height, depth = left.shape
     width = depth // chunks
-    for part in range(chunks):
-        top = 0
-        for q in range(pieces):
-            block = scaled[part * pieces + q]
-            left[pl.ds(top, block.shape[0]), pl.ds(part * width, width)] = block[...]
-            top += block.shape[0]
+    piece = height // (len(scaled) // chunks)
+    for index, block in enumerate(scaled):
+        q, part = divmod(index, chunks)
+        left[pl.ds(q * piece, piece), pl.ds(part * width, width)] = block[...]
     count = out.shape[0]
     val_count = height // count
-    rows = out.shape[1] // places
+    rows = out.shape[1] // len(places)
     tile = min(rows, 256)
-    for place in range(places):
-
-        def step(index, carry):
-            begin = pl.multiple_of(index * tile, tile)
-            right = jnp.concatenate(
-                [conds[place * chunks + part][pl.ds(begin, tile), :] for part in range(chunks)], axis=1
-            )
-            values = vals[place][:, pl.ds(begin, tile)].astype(F32)
-            product = contract_last(left[...], right)
+    for index, place in enumerate(places):
+
+        def step(number, carry):
+            begin = pl.multiple_of(number * tile, tile)
+            values = vals[index][:, pl.ds(begin, tile)].astype(F32)
+            product = contract(left[...], right[:, pl.ds(pl.multiple_of(place * rows + begin, tile), tile)])
             summed = jnp.sum(product.reshape(count, val_count, tile) * values[None], axis=1)
-            out[:, pl.ds(pl.multiple_of(place * rows + begin, tile), tile)] = summed
+            out[:, pl.ds(pl.multiple_of(index * rows + begin, tile), tile)] = summed
             return carry
 
         lax.fori_loop(0, rows // tile, step, 0)

time: 119 us -> 113 us (0.950)
  matrix products: 13.7 us -> 4.63 us
  waiting for transfers between devices: 53.8 us -> 45.8 us
  starting transfers between devices: 31.5 us -> 37.4 us
  Pallas kernels: 12.9 us -> 17.3 us
  local copies, waits for them, and re-layouts: 2.87 us -> 4.1 us
    ppermute x32 -> x38, waiting for transfers between devices: 53.8 us -> 45.8 us  [swap(): return lax.ppermute(block, 'grid', [(i, i ^ bit) for i in range(count)])]
    ppermute x32 -> x38, starting transfers between devices: 31.5 us -> 37.4 us  [swap(): return lax.ppermute(block, 'grid', [(i, i ^ bit) for i in range(count)])]
    dot_general x2 -> x0, matrix products: 4.86 us -> none  [contract_last(): lax.dot_general(left, right, (((1,), (1,)), ((), ())), preferred_element_...]
    pallas_call x4 -> x17, Pallas kernels: 10.3 us -> 14.7 us  [the longest x16 14 us: in_vmem(): pl.pallas_call(kernel, out_shape=out_shape, in_specs=[pl.BlockSpec(memory...]
    dot_general x10 -> x8, matrix products: 8.8 us -> 4.63 us  [contract(): return jnp.dot(left, right, preferred_element_type=F32)]
    unnamed x7 -> x12, local copies, waits for them, and re-layouts: 1.94 us -> 2.94 us
  transfers between devices with their start and end apart: 32 -> 38, of which waited for: 18 -> 19; matrix products, arithmetic and copies ran while one was open for 9% -> 6% of each run, Pallas kernels for 11% -> 12%
where the time goes in v3:
time: 113 us
  waiting for transfers between devices  45.8 us (41%)
  starting transfers between devices  37.4 us (33%)
  Pallas kernels  17.3 us (15%)
  matrix products  4.63 us (4%)
  local copies, waits for them, and re-layouts  4.1 us (4%)
  other arithmetic  2.4 us (2%)
    ppermute x38, waiting for transfers between devices, swap(): return lax.ppermute(block, 'grid', [(i, i ^ bit) for i in range(count)])  45.8 us
    ppermute x38, starting transfers between devices, swap(): return lax.ppermute(block, 'grid', [(i, i ^ bit) for i in range(count)])  37.4 us
    pallas_call x16, Pallas kernels, in_vmem(): pl.pallas_call(kernel, out_shape=out_shape, in_specs=[pl.BlockSpec(memory...  14 us
    dot_general x8, matrix products, contract(): return jnp.dot(left, right, preferred_element_type=F32)  4.63 us
    unnamed x12, local copies, waits for them, and re-layouts  2.94 us
    pallas_call x1, Pallas kernels, body(): pl.pallas_call(functools.partial(own_kernel, CHUNKS), out_shape=[jax.Shap...  2.48 us
  transfers between devices with their start and end apart: 38, of which 19 were waited for; matrix products, arithmetic and copies ran while one was open for 6% of the time, Pallas kernels for 12%

profile of v3, /device:TPU:0, one launch (start us, length us, event | category | flops | bytes accessed | tf_op | source)
XLA Modules:
  0.0 112.7 jit_solution(13297924557615884418)
XLA Ops:
  0.6 0.6 collective-permute-start.1
  1.2 2.6 %collective-permute-start.4 = (bf16[64,1024]{1,0:T(8,128)(2,1)}, bf16[64,1024]{1,0:T(8,128)(2,1)S(1)}, u32[]{:S(2)}, u32[]{:S(2)}) collective-permute-start(bf16[64,1024]{1,0:T(8,128)(2,1)} %bitcast.42), channel_id=1, source_target_pairs={{0,2},{1,3},{2,0},{3,1},{4,6},{5,7},{6,4},{7,5},{8,10},{9,11},{10,... | collective-permute-start | bytes 393224 | tf_op jit(solution)/shard_map/ppermute | solution.py:19
  4.2 1.2 %copy-done.3 = bf16[1024,512]{1,0:T(8,128)(2,1)S(1)} copy-done((bf16[1024,512]{1,0:T(8,128)(2,1)S(1)}, bf16[1024,512]{1,0:T(8,128)(2,1)}, u32[]{:S(2)}) %copy-start.3) | copy-done | bytes 1048600
  5.8 0.8 dynamic_slice.25
  6.5 0.7 subtract_divide_fusion
  7.4 1.0 collective-permute-done.4
  8.3 1.8 %collective-permute-done.5.refs_5_ = bf16[48,1024]{1,0:T(8,128)(2,1)S(1)} collective-permute-done((bf16[48,1024]{1,0:T(8,128)(2,1)}, bf16[48,1024]{1,0:T(8,128)(2,1)S(1)}, u32[]{:S(2)}, u32[]{:S(2)}) %collective-permute-start.5) | collective-permute-done | bytes 98336 | tf_op jit(solution)/shard_map/ppermute | solution.py:19
  10.2 1.7 %collective-permute-start.12 = (bf16[1024,128]{1,0:T(8,128)(2,1)S(1)}, bf16[1024,128]{1,0:T(8,128)(2,1)S(1)}, u32[]{:S(2)}, u32[]{:S(2)}) collective-permute-start(bf16[1024,128]{1,0:T(8,128)(2,1)S(1)} %get-tuple-element.28), channel_id=1, source_target_pairs={{0,2},{1,3},{2,0},{3,1},{4,6},{5,7},{6,4},{7,5},{8,10},{9,11},{10,... | collective-permute-start | bytes 786440 | tf_op jit(solution)/shard_map/ppermute | solution.py:19
  12.1 6.1 %collective-permute-done.12.refs_5_ = bf16[1024,128]{1,0:T(8,128)(2,1)S(1)} collective-permute-done((bf16[1024,128]{1,0:T(8,128)(2,1)S(1)}, bf16[1024,128]{1,0:T(8,128)(2,1)S(1)}, u32[]{:S(2)}, u32[]{:S(2)}) %collective-permute-start.12) | collective-permute-done | bytes 262176 | tf_op jit(solution)/shard_map/ppermute | solution.py:19
  18.2 0.6 fusion.14
  18.8 0.8 collective-permute-done.7
  19.7 1.1 %collective-permute-done.8.refs_6_ = bf16[48,1024]{1,0:T(8,128)(2,1)S(1)} collective-permute-done((bf16[48,1024]{1,0:T(8,128)(2,1)S(1)}, bf16[48,1024]{1,0:T(8,128)(2,1)S(1)}, u32[]{:S(2)}, u32[]{:S(2)}) %collective-permute-start.8) | collective-permute-done | bytes 98336 | tf_op jit(solution)/shard_map/ppermute | solution.py:19
  20.9 1.5 %collective-permute-start.6 = (bf16[1024,128]{1,0:T(8,128)(2,1)S(1)}, bf16[1024,128]{1,0:T(8,128)(2,1)S(1)}, u32[]{:S(2)}, u32[]{:S(2)}) collective-permute-start(bf16[1024,128]{1,0:T(8,128)(2,1)S(1)} %get-tuple-element.23), channel_id=1, source_target_pairs={{0,2},{1,3},{2,0},{3,1},{4,6},{5,7},{6,4},{7,5},{8,10},{9,11},{10,... | collective-permute-start | bytes 786440 | tf_op jit(solution)/shard_map/ppermute | solution.py:19
  22.6 0.6 fusion.13
  23.2 6.1 %collective-permute-done.6.refs_4_ = bf16[1024,128]{1,0:T(8,128)(2,1)S(1)} collective-permute-done((bf16[1024,128]{1,0:T(8,128)(2,1)S(1)}, bf16[1024,128]{1,0:T(8,128)(2,1)S(1)}, u32[]{:S(2)}, u32[]{:S(2)}) %collective-permute-start.6) | collective-permute-done | bytes 262176 | tf_op jit(solution)/shard_map/ppermute | solution.py:19
  29.3 0.6 fusion.12
  29.8 0.6 collective-permute-start.13
  30.5 2.5 %shard_map.78 = (f32[768,128]{1,0:T(8,128)S(1)}, f32[768,128]{1,0:T(8,128)S(1)}, f32[768,128]{1,0:T(8,128)S(1)}, f32[768,128]{1,0:T(8,128)S(1)}) custom-call(s32[2]{0:T(128)S(1)} %pad_add_fusion.starts_ref, bf16[48,1024]{1,0:T(8,128)(2,1)S(1)} %bitcast.46, bf16[48,1024]{1,0:T(8,128)(2,1)S(1)} %collective-permute-done.val1.refs_6_, ...), custom_call_target="tpu_custom_call" | custom-call | flops 1610612736 | bytes 4194304 | tf_op jit(solution)/shard_map/pallas_call | solution.py:92
  33.0 0.6 fusion.11
  33.8 0.6 fusion.1
  34.4 1.6 %collective-permute-start.18 = (bf16[384,128]{1,0:T(8,128)(2,1)S(1)}, bf16[384,128]{1,0:T(8,128)(2,1)S(1)}, u32[]{:S(2)}, u32[]{:S(2)}) collective-permute-start(bf16[384,128]{1,0:T(8,128)(2,1)S(1)} %get-tuple-element.44), channel_id=1, source_target_pairs={{0,4},{1,5},{2,6},{3,7},{4,0},{5,1},{6,2},{7,3},{8,12},{9,13},{10,... | collective-permute-start | bytes 294920 | tf_op jit(solution)/shard_map/ppermute | solution.py:19
  36.0 0.6 fusion
  36.6 0.6 collective-permute-start.16
  37.2 1.5 %collective-permute-start.14 = (bf16[384,128]{1,0:T(8,128)(2,1)S(1)}, bf16[384,128]{1,0:T(8,128)(2,1)S(1)}, u32[]{:S(2)}, u32[]{:S(2)}) collective-permute-start(bf16[384,128]{1,0:T(8,128)(2,1)S(1)} %get-tuple-element.45), channel_id=1, source_target_pairs={{0,4},{1,5},{2,6},{3,7},{4,0},{5,1},{6,2},{7,3},{8,12},{9,13},{10,... | collective-permute-start | bytes 294920 | tf_op jit(solution)/shard_map/ppermute | solution.py:19
  39.2 0.6 convolution_add_fusion.1.block_ref
  39.8 0.6 convolution_add_fusion.3.block_ref
  40.4 2.6 %collective-permute-start.19 = (bf16[384,128]{1,0:T(8,128)(2,1)S(1)}, bf16[384,128]{1,0:T(8,128)(2,1)S(1)}, u32[]{:S(2)}, u32[]{:S(2)}) collective-permute-start(bf16[384,128]{1,0:T(8,128)(2,1)S(1)} %get-tuple-element.35), channel_id=1, source_target_pairs={{0,8},{1,9},{2,10},{3,11},{4,12},{5,13},{6,14},{7,15},{8,0},{9,1},... | collective-permute-start | bytes 294920 | tf_op jit(solution)/shard_map/ppermute | solution.py:19
  43.1 2.0 %collective-permute-start.17 = (bf16[384,128]{1,0:T(8,128)(2,1)S(1)}, bf16[384,128]{1,0:T(8,128)(2,1)S(1)}, u32[]{:S(2)}, u32[]{:S(2)}) collective-permute-start(bf16[384,128]{1,0:T(8,128)(2,1)S(1)} %get-tuple-element.33), channel_id=1, source_target_pairs={{0,8},{1,9},{2,10},{3,11},{4,12},{5,13},{6,14},{7,15},{8,0},{9,1},... | collective-permute-start | bytes 294920 | tf_op jit(solution)/shard_map/ppermute | solution.py:19
  45.0 2.7 %collective-permute-done.14.refs_0_ = bf16[384,128]{1,0:T(8,128)(2,1)S(1)} collective-permute-done((bf16[384,128]{1,0:T(8,128)(2,1)S(1)}, bf16[384,128]{1,0:T(8,128)(2,1)S(1)}, u32[]{:S(2)}, u32[]{:S(2)}) %collective-permute-start.14) | collective-permute-done | bytes 98336 | tf_op jit(solution)/shard_map/ppermute | solution.py:19
  47.9 1.7 %collective-permute-done.10.refs_0_ = bf16[384,128]{1,0:T(8,128)(2,1)S(1)} collective-permute-done((bf16[384,128]{1,0:T(8,128)(2,1)S(1)}, bf16[384,128]{1,0:T(8,128)(2,1)S(1)}, u32[]{:S(2)}, u32[]{:S(2)}) %collective-permute-start.10) | collective-permute-done | bytes 98336 | tf_op jit(solution)/shard_map/ppermute | solution.py:19
  49.6 1.3 %collective-permute-start.11 = (bf16[384,128]{1,0:T(8,128)(2,1)S(1)}, bf16[384,128]{1,0:T(8,128)(2,1)S(1)}, u32[]{:S(2)}, u32[]{:S(2)}) collective-permute-start(bf16[384,128]{1,0:T(8,128)(2,1)S(1)} %get-tuple-element.26), channel_id=1, source_target_pairs={{0,8},{1,9},{2,10},{3,11},{4,12},{5,13},{6,14},{7,15},{8,0},{9,1},... | collective-permute-start | bytes 294920 | tf_op jit(solution)/shard_map/ppermute | solution.py:19
  50.9 0.6 shard_map.87.refs_4_
  51.5 4.5 %collective-permute-start.24 = (bf16[384,128]{1,0:T(8,128)(2,1)S(1)}, bf16[384,128]{1,0:T(8,128)(2,1)S(1)}, u32[]{:S(2)}, u32[]{:S(2)}) collective-permute-start(bf16[384,128]{1,0:T(8,128)(2,1)S(1)} %shard_map.86.refs_3_), channel_id=1, source_target_pairs={{0,4},{1,5},{2,6},{3,7},{4,0},{5,1},{6,2},{7,3},{8,12},{9,13},{10,... | collective-permute-start | bytes 294920 | tf_op jit(solution)/shard_map/ppermute | solution.py:19
  56.1 1.7 %collective-permute-done.17.other_ref = bf16[384,128]{1,0:T(8,128)(2,1)S(1)} collective-permute-done((bf16[384,128]{1,0:T(8,128)(2,1)S(1)}, bf16[384,128]{1,0:T(8,128)(2,1)S(1)}, u32[]{:S(2)}, u32[]{:S(2)}) %collective-permute-start.17) | collective-permute-done | bytes 98336 | tf_op jit(solution)/shard_map/ppermute | solution.py:19
  58.3 1.5 %collective-permute-done.15.other_ref = bf16[384,128]{1,0:T(8,128)(2,1)S(1)} collective-permute-done((bf16[384,128]{1,0:T(8,128)(2,1)S(1)}, bf16[384,128]{1,0:T(8,128)(2,1)S(1)}, u32[]{:S(2)}, u32[]{:S(2)}) %collective-permute-start.15) | collective-permute-done | bytes 98336 | tf_op jit(solution)/shard_map/ppermute | solution.py:19
  60.1 0.8 collective-permute-done.11.other_ref
  60.9 1.1 %collective-permute-start.21 = (bf16[384,128]{1,0:T(8,128)(2,1)S(1)}, bf16[384,128]{1,0:T(8,128)(2,1)S(1)}, u32[]{:S(2)}, u32[]{:S(2)}) collective-permute-start(bf16[384,128]{1,0:T(8,128)(2,1)S(1)} %shard_map.80.refs_0_), channel_id=1, source_target_pairs={{0,4},{1,5},{2,6},{3,7},{4,0},{5,1},{6,2},{7,3},{8,12},{9,13},{10,... | collective-permute-start | bytes 294920 | tf_op jit(solution)/shard_map/ppermute | solution.py:19
  62.1 2.5 %shard_map.89 = f32[16,2048]{1,0:T(8,128)S(1)} custom-call(bf16[384,128]{1,0:T(8,128)(2,1)S(1)} %shard_map.80.refs_0_, bf16[384,128]{1,0:T(8,128)(2,1)S(1)} %shard_map.82.refs_1_, bf16[384,128]{1,0:T(8,128)(2,1)S(1)} %shard_map.84.refs_2_, bf16[384,128]{1,0:T(8,128)(2,1)S(1)} %shard_map.86.refs_3_, bf16[256,4096]{1,0:T(8,128)(2,1)S(1)} %shard_map.87.refs_4_, ...), custom_call_target="tpu_custom_call" | custom-call | flops 1000000000 | bytes 4194304 | tf_op jit(solution)/shard_map/pallas_call | solution.py:235
  64.6 2.3 %shard_map.88 = f32[16,2048]{1,0:T(8,128)S(1)} custom-call(bf16[384,128]{1,0:T(8,128)(2,1)S(1)} %shard_map.80.refs_0_, bf16[384,128]{1,0:T(8,128)(2,1)S(1)} %shard_map.82.refs_1_, bf16[384,128]{1,0:T(8,128)(2,1)S(1)} %shard_map.84.refs_2_, bf16[384,128]{1,0:T(8,128)(2,1)S(1)} %shard_map.86.refs_3_, bf16[256,4096]{1,0:T(8,128)(2,1)S(1)} %shard_map.87.refs_4_, ...), custom_call_target="tpu_custom_call" | custom-call | flops 1000000000 | bytes 4194304 | tf_op jit(solution)/shard_map/pallas_call | solution.py:235
  66.9 1.5 %collective-permute-start.20 = (f32[16,2048]{1,0:T(8,128)S(1)}, f32[16,2048]{1,0:T(8,128)S(1)}, u32[]{:S(2)}, u32[]{:S(2)}) collective-permute-start(f32[16,2048]{1,0:T(8,128)S(1)} %shard_map.89), channel_id=1, source_target_pairs={{0,2},{1,3},{2,0},{3,1},{4,6},{5,7},{6,4},{7,5},{8,10},{9,11},{10,... | collective-permute-start | bytes 393224 | tf_op jit(solution)/shard_map/ppermute | solution.py:19
  68.4 2.3 %shard_map.91 = f32[16,2048]{1,0:T(8,128)S(1)} custom-call(bf16[384,128]{1,0:T(8,128)(2,1)S(1)} %collective-permute-done.21.refs_0_, bf16[384,128]{1,0:T(8,128)(2,1)S(1)} %collective-permute-done.22.refs_1_, bf16[384,128]{1,0:T(8,128)(2,1)S(1)} %collective-permute-done.23.refs_2_, bf16[384,128]{1,0:T(8,128)(2,1)S(1)} %collective-permute-done.24.refs_3_, ...), custom_call_target="tpu_custom_call" | custom-call | flops 1000000000 | bytes 4194304 | tf_op jit(solution)/shard_map/pallas_call | solution.py:235
  70.7 0.7 collective-permute-start.25
  71.4 2.3 %shard_map.90 = f32[16,2048]{1,0:T(8,128)S(1)} custom-call(bf16[384,128]{1,0:T(8,128)(2,1)S(1)} %collective-permute-done.21.refs_0_, bf16[384,128]{1,0:T(8,128)(2,1)S(1)} %collective-permute-done.22.refs_1_, bf16[384,128]{1,0:T(8,128)(2,1)S(1)} %collective-permute-done.23.refs_2_, bf16[384,128]{1,0:T(8,128)(2,1)S(1)} %collective-permute-done.24.refs_3_, ...), custom_call_target="tpu_custom_call" | custom-call | flops 1000000000 | bytes 4194304 | tf_op jit(solution)/shard_map/pallas_call | solution.py:235
  73.7 2.0 %collective-permute-done.25 = f32[16,2048]{1,0:T(8,128)S(1)} collective-permute-done((f32[16,2048]{1,0:T(8,128)S(1)}, f32[16,2048]{1,0:T(8,128)S(1)}, u32[]{:S(2)}, u32[]{:S(2)}) %collective-permute-start.25) | collective-permute-done | bytes 131104 | tf_op jit(solution)/shard_map/ppermute | solution.py:19
  75.8 1.2 %shard_map.92.eig_ref = bf16[1024,2048]{1,0:T(8,128)(2,1)S(1)} custom-call(bf16[1024,1024]{1,0:T(8,128)(2,1)S(1)} %copy-done, bf16[1024,1024]{1,0:T(8,128)(2,1)S(1)} %collective-permute-done.26.refs_1_), custom_call_target="tpu_custom_call" | custom-call | flops 2000000000 | bytes 4194304 | tf_op jit(solution)/shard_map/pallas_call | solution.py:235
  77.2 1.3 %shard_map.93 = f32[32,1024]{1,0:T(8,128)S(1)} custom-call(f32[32,2048]{1,0:T(8,128)S(1)} %bitcast.39, bf16[1024,2048]{1,0:T(8,128)(2,1)S(1)} %shard_map.92.eig_ref), custom_call_target="tpu_custom_call" | custom-call | flops 1000000000 | bytes 4194304 | tf_op jit(solution)/shard_map/pallas_call | solution.py:235
  78.4 0.7 collective-permute-start.27
  79.1 4.3 %collective-permute-done.27 = f32[32,1024]{1,0:T(8,128)S(1)} collective-permute-done((f32[32,1024]{1,0:T(8,128)S(1)}, f32[32,1024]{1,0:T(8,128)S(1)}, u32[]{:S(2)}, u32[]{:S(2)}) %collective-permute-start.27) | collective-permute-done | bytes 131104 | tf_op jit(solution)/shard_map/ppermute | solution.py:19
  83.4 1.1 %collective-permute-start.28 = (f32[32,1024]{1,0:T(8,128)S(1)}, f32[32,1024]{1,0:T(8,128)S(1)}, u32[]{:S(2)}, u32[]{:S(2)}) collective-permute-start(f32[32,1024]{1,0:T(8,128)S(1)} %add.115), channel_id=1, source_target_pairs={{0,4},{1,5},{2,6},{3,7},{4,0},{5,1},{6,2},{7,3},{8,12},{9,13},{10,... | collective-permute-start | bytes 393224 | tf_op jit(solution)/shard_map/ppermute | solution.py:19
  84.6 4.6 %collective-permute-done.28 = f32[32,1024]{1,0:T(8,128)S(1)} collective-permute-done((f32[32,1024]{1,0:T(8,128)S(1)}, f32[32,1024]{1,0:T(8,128)S(1)}, u32[]{:S(2)}, u32[]{:S(2)}) %collective-permute-start.28) | collective-permute-done | bytes 131104 | tf_op jit(solution)/shard_map/ppermute | solution.py:19
  89.2 2.0 %collective-permute-start.29 = (bf16[32,1024]{1,0:T(8,128)(2,1)S(1)}, bf16[32,1024]{1,0:T(8,128)(2,1)S(1)}, u32[]{:S(2)}, u32[]{:S(2)}) collective-permute-start(bf16[32,1024]{1,0:T(8,128)(2,1)S(1)} %get-tuple-element.40), channel_id=1, source_target_pairs={{0,8},{1,9},{2,10},{3,11},{4,12},{5,13},{6,14},{7,15},{8,0},{9,1},... | collective-permute-start | bytes 196616 | tf_op jit(solution)/shard_map/ppermute | solution.py:19
  91.2 3.9 %collective-permute-done.29 = bf16[32,1024]{1,0:T(8,128)(2,1)S(1)} collective-permute-done((bf16[32,1024]{1,0:T(8,128)(2,1)S(1)}, bf16[32,1024]{1,0:T(8,128)(2,1)S(1)}, u32[]{:S(2)}, u32[]{:S(2)}) %collective-permute-start.29) | collective-permute-done | bytes 65568 | tf_op jit(solution)/shard_map/ppermute | solution.py:19
  95.3 1.6 %copy-done.2 = bf16[1024,1024]{1,0:T(8,128)(2,1)S(1)} copy-done((bf16[1024,1024]{1,0:T(8,128)(2,1)S(1)}, bf16[1024,1024]{1,0:T(8,128)(2,1)}, u32[]{:S(2)}) %copy-start.2) | copy-done | bytes 2097176
  96.9 1.3 %shard_map.95 = (f32[32,2048]{1,0:T(8,128)S(1)}, f32[32,128]{1,0:T(8,128)S(1)}) custom-call(f32[32,2048]{1,0:T(8,128)S(1)} %bitcast.40, f32[32,1024]{1,0:T(8,128)S(1)} %get-tuple-element.39.part_ref, bf16[1024,1024]{1,0:T(8,128)(2,1)S(1)} %copy-done, bf16[1024,1024]{1,0:T(8,128)(2,1)S(1)} %copy-done.2), custom_call_target="tpu_custom_call" | custom-call | flops 1000000000 | bytes 4194304 | tf_op jit(solution)/shard_map/pallas_call | solution.py:235
  98.3 0.5 collective-permute-start.32
  98.9 2.9 %collective-permute-start.33 = (f32[1,32]{1,0:T(1,128)S(1)}, f32[1,32]{1,0:T(1,128)S(1)}, u32[]{:S(2)}, u32[]{:S(2)}) collective-permute-start(f32[1,32]{1,0:T(1,128)S(1)} %bitcast.58), channel_id=1, source_target_pairs={{0,8},{1,9},{2,10},{3,11},{4,12},{5,13},{6,14},{7,15},{8,0},{9,1},... | collective-permute-start | bytes 392 | tf_op jit(solution)/shard_map/ppermute | solution.py:19
  101.8 1.0 collective-permute-start.34
  103.1 0.5 collective-permute-start.30
  103.6 3.6 %collective-permute-done.34 = f32[1,32]{1,0:T(1,128)S(1)} collective-permute-done((f32[1,32]{1,0:T(1,128)S(1)}, f32[1,32]{1,0:T(1,128)S(1)}, u32[]{:S(2)}, u32[]{:S(2)}) %collective-permute-start.34) | collective-permute-done | bytes 160 | tf_op jit(solution)/shard_map/ppermute | solution.py:19
  107.2 0.8 collective-permute-start.35
  108.0 1.3 %collective-permute-start.37 = (f32[1,32]{1,0:T(1,128)S(1)}, f32[1,32]{1,0:T(1,128)S(1)}, u32[]{:S(2)}, u32[]{:S(2)}) collective-permute-start(f32[1,32]{1,0:T(1,128)S(1)} %add_add_fusion), channel_id=1, source_target_pairs={{0,3},{1,2},{2,1},{3,0},{4,7},{5,6},{6,5},{7,4},{8,11},{9,10},{10,... | collective-permute-start | bytes 392 | tf_op jit(solution)/shard_map/ppermute | solution.py:19
  109.3 1.4 %collective-permute-done.35 = f32[1,32]{1,0:T(1,128)S(1)} collective-permute-done((f32[1,32]{1,0:T(1,128)S(1)}, f32[1,32]{1,0:T(1,128)S(1)}, u32[]{:S(2)}, u32[]{:S(2)}) %collective-permute-start.35) | collective-permute-done | bytes 160 | tf_op jit(solution)/shard_map/ppermute | solution.py:19
  111.1 0.7 shard_map.94
  111.9 0.8 broadcast_divide_fusion
  (80 shorter events, 4.4 us)
Async XLA Ops:
  0.6 29.8 %collective-permute-start.1 = (bf16[64,1024]{1,0:T(8,128)(2,1)}, bf16[64,1024]{1,0:T(8,128)(2,1)S(1)}, u32[]{:S(2)}, u32[]{:S(2)}) collective-permute-start(bf16[64,1024]{1,0:T(8,128)(2,1)} %bitcast.41), channel_id=1, source_target_pairs={{0,1},{1,0},{2,3},{3,2},{4,5},{5,4},{6,7},{7,6},{8,9},{9,8},{10,11... | collective-permute-start | bytes 393224 | tf_op jit(solution)/shard_map/ppermute | solution.py:19
  1.2 7.1 %collective-permute-start.4 = (bf16[64,1024]{1,0:T(8,128)(2,1)}, bf16[64,1024]{1,0:T(8,128)(2,1)S(1)}, u32[]{:S(2)}, u32[]{:S(2)}) collective-permute-start(bf16[64,1024]{1,0:T(8,128)(2,1)} %bitcast.42), channel_id=1, source_target_pairs={{0,2},{1,3},{2,0},{3,1},{4,6},{5,7},{6,4},{7,5},{8,10},{9,11},{10,... | collective-permute-start | bytes 393224 | tf_op jit(solution)/shard_map/ppermute | solution.py:19
  3.8 26.1 %collective-permute-start = (bf16[48,1024]{1,0:T(8,128)(2,1)}, bf16[48,1024]{1,0:T(8,128)(2,1)S(1)}, u32[]{:S(2)}, u32[]{:S(2)}) collective-permute-start(bf16[48,1024]{1,0:T(8,128)(2,1)} %bitcast.44), channel_id=1, source_target_pairs={{0,1},{1,0},{2,3},{3,2},{4,5},{5,4},{6,7},{7,6},{8,9},{9,8},{10,11... | collective-permute-start | bytes 294920 | tf_op jit(solution)/shard_map/ppermute | solution.py:19
  3.9 6.3 %collective-permute-start.5 = (bf16[48,1024]{1,0:T(8,128)(2,1)}, bf16[48,1024]{1,0:T(8,128)(2,1)S(1)}, u32[]{:S(2)}, u32[]{:S(2)}) collective-permute-start(bf16[48,1024]{1,0:T(8,128)(2,1)} %bitcast.45), channel_id=1, source_target_pairs={{0,2},{1,3},{2,0},{3,1},{4,6},{5,7},{6,4},{7,5},{8,10},{9,11},{10,... | collective-permute-start | bytes 294920 | tf_op jit(solution)/shard_map/ppermute | solution.py:19
  4.2 1.2 %copy-start.3 = (bf16[1024,512]{1,0:T(8,128)(2,1)S(1)}, bf16[1024,512]{1,0:T(8,128)(2,1)}, u32[]{:S(2)}) copy-start(bf16[1024,512]{1,0:T(8,128)(2,1)} %cond_ref.1) | copy-start | bytes 3145732
  5.6 24.9 %collective-permute-start.2 = (bf16[1024,128]{1,0:T(8,128)(2,1)S(1)}, bf16[1024,128]{1,0:T(8,128)(2,1)S(1)}, u32[]{:S(2)}, u32[]{:S(2)}) collective-permute-start(bf16[1024,128]{1,0:T(8,128)(2,1)S(1)} %get-tuple-element.20.refs_0_), channel_id=1, source_target_pairs={{0,1},{1,0},{2,3},{3,2},{4,5},{5,4},{6,7},{7,6},{8,9},{9,8},{10,11... | collective-permute-start | bytes 786440 | tf_op jit(solution)/shard_map/ppermute | solution.py:19
  8.3 22.2 %collective-permute-start.3 = (bf16[1024,128]{1,0:T(8,128)(2,1)S(1)}, bf16[1024,128]{1,0:T(8,128)(2,1)S(1)}, u32[]{:S(2)}, u32[]{:S(2)}) collective-permute-start(bf16[1024,128]{1,0:T(8,128)(2,1)S(1)} %get-tuple-element.21.refs_1_), channel_id=1, source_target_pairs={{0,1},{1,0},{2,3},{3,2},{4,5},{5,4},{6,7},{7,6},{8,9},{9,8},{10,11... | collective-permute-start | bytes 786440 | tf_op jit(solution)/shard_map/ppermute | solution.py:19
  10.2 8.1 %collective-permute-start.12 = (bf16[1024,128]{1,0:T(8,128)(2,1)S(1)}, bf16[1024,128]{1,0:T(8,128)(2,1)S(1)}, u32[]{:S(2)}, u32[]{:S(2)}) collective-permute-start(bf16[1024,128]{1,0:T(8,128)(2,1)S(1)} %get-tuple-element.28), channel_id=1, source_target_pairs={{0,2},{1,3},{2,0},{3,1},{4,6},{5,7},{6,4},{7,5},{8,10},{9,11},{10,... | collective-permute-start | bytes 786440 | tf_op jit(solution)/shard_map/ppermute | solution.py:19
  18.2 1.3 %collective-permute-start.7 = (bf16[64,1024]{1,0:T(8,128)(2,1)S(1)}, bf16[64,1024]{1,0:T(8,128)(2,1)S(1)}, u32[]{:S(2)}, u32[]{:S(2)}) collective-permute-start(bf16[64,1024]{1,0:T(8,128)(2,1)S(1)} %collective-permute-done.4), channel_id=1, source_target_pairs={{0,1},{1,0},{2,3},{3,2},{4,5},{5,4},{6,7},{7,6},{8,9},{9,8},{10,11... | collective-permute-start | bytes 393224 | tf_op jit(solution)/shard_map/ppermute | solution.py:19
  19.6 1.3 %collective-permute-start.8 = (bf16[48,1024]{1,0:T(8,128)(2,1)S(1)}, bf16[48,1024]{1,0:T(8,128)(2,1)S(1)}, u32[]{:S(2)}, u32[]{:S(2)}) collective-permute-start(bf16[48,1024]{1,0:T(8,128)(2,1)S(1)} %collective-permute-done.5.refs_5_), channel_id=1, source_target_pairs={{0,1},{1,0},{2,3},{3,2},{4,5},{5,4},{6,7},{7,6},{8,9},{9,8},{10,11... | collective-permute-start | bytes 294920 | tf_op jit(solution)/shard_map/ppermute | solution.py:19
  20.9 8.4 %collective-permute-start.6 = (bf16[1024,128]{1,0:T(8,128)(2,1)S(1)}, bf16[1024,128]{1,0:T(8,128)(2,1)S(1)}, u32[]{:S(2)}, u32[]{:S(2)}) collective-permute-start(bf16[1024,128]{1,0:T(8,128)(2,1)S(1)} %get-tuple-element.23), channel_id=1, source_target_pairs={{0,2},{1,3},{2,0},{3,1},{4,6},{5,7},{6,4},{7,5},{8,10},{9,11},{10,... | collective-permute-start | bytes 786440 | tf_op jit(solution)/shard_map/ppermute | solution.py:19
  22.6 6.7 %copy-start = (bf16[1024,1024]{1,0:T(8,128)(2,1)S(1)}, bf16[1024,1024]{1,0:T(8,128)(2,1)}, u32[]{:S(2)}) copy-start(bf16[1024,1024]{1,0:T(8,128)(2,1)} %refs_0_.3) | copy-start | bytes 6291460
  23.2 7.4 %copy-start.4 = (bf16[1024,64]{0,1:T(8,128)(2,1)S(1)}, bf16[1024,64]{0,1:T(8,128)(2,1)}, u32[]{:S(2)}) copy-start(bf16[1024,64]{0,1:T(8,128)(2,1)} %param.8) | copy-start | bytes 393220
  23.2 7.3 %copy-start.5 = (bf16[1024,48]{0,1:T(8,128)(2,1)S(1)}, bf16[1024,48]{0,1:T(8,128)(2,1)}, u32[]{:S(2)}) copy-start(bf16[1024,48]{0,1:T(8,128)(2,1)} %param.6) | copy-start | bytes 294916
  29.3 46.5 %collective-permute-start.26 = (bf16[1024,1024]{1,0:T(8,128)(2,1)S(1)}, bf16[1024,1024]{1,0:T(8,128)(2,1)S(1)}, u32[]{:S(2)}, u32[]{:S(2)}) collective-permute-start(bf16[1024,1024]{1,0:T(8,128)(2,1)S(1)} %copy-done), channel_id=1, source_target_pairs={{0,1},{1,0},{2,3},{3,2},{4,5},{5,4},{6,7},{7,6},{8,9},{9,8},{10,11... | collective-permute-start | bytes 6291464 | tf_op jit(solution)/shard_map/ppermute | solution.py:19
  29.8 3.9 %collective-permute-start.13 = (bf16[1024,128]{1,0:T(8,128)(2,1)S(1)}, bf16[1024,128]{1,0:T(8,128)(2,1)S(1)}, u32[]{:S(2)}, u32[]{:S(2)}) collective-permute-start(bf16[1024,128]{1,0:T(8,128)(2,1)S(1)} %collective-permute-done.12.refs_5_), channel_id=1, source_target_pairs={{0,1},{1,0},{2,3},{3,2},{4,5},{5,4},{6,7},{7,6},{8,9},{9,8},{10,11... | collective-permute-start | bytes 786440 | tf_op jit(solution)/shard_map/ppermute | solution.py:19
  30.4 5.6 %collective-permute-start.9 = (bf16[1024,128]{1,0:T(8,128)(2,1)S(1)}, bf16[1024,128]{1,0:T(8,128)(2,1)S(1)}, u32[]{:S(2)}, u32[]{:S(2)}) collective-permute-start(bf16[1024,128]{1,0:T(8,128)(2,1)S(1)} %collective-permute-done.6.refs_4_), channel_id=1, source_target_pairs={{0,1},{1,0},{2,3},{3,2},{4,5},{5,4},{6,7},{7,6},{8,9},{9,8},{10,11... | collective-permute-start | bytes 786440 | tf_op jit(solution)/shard_map/ppermute | solution.py:19
  34.4 6.0 %collective-permute-start.18 = (bf16[384,128]{1,0:T(8,128)(2,1)S(1)}, bf16[384,128]{1,0:T(8,128)(2,1)S(1)}, u32[]{:S(2)}, u32[]{:S(2)}) collective-permute-start(bf16[384,128]{1,0:T(8,128)(2,1)S(1)} %get-tuple-element.44), channel_id=1, source_target_pairs={{0,4},{1,5},{2,6},{3,7},{4,0},{5,1},{6,2},{7,3},{8,12},{9,13},{10,... | collective-permute-start | bytes 294920 | tf_op jit(solution)/shard_map/ppermute | solution.py:19
  36.6 6.4 %collective-permute-start.16 = (bf16[384,128]{1,0:T(8,128)(2,1)S(1)}, bf16[384,128]{1,0:T(8,128)(2,1)S(1)}, u32[]{:S(2)}, u32[]{:S(2)}) collective-permute-start(bf16[384,128]{1,0:T(8,128)(2,1)S(1)} %get-tuple-element.46), channel_id=1, source_target_pairs={{0,4},{1,5},{2,6},{3,7},{4,0},{5,1},{6,2},{7,3},{8,12},{9,13},{10,... | collective-permute-start | bytes 294920 | tf_op jit(solution)/shard_map/ppermute | solution.py:19
  37.2 10.6 %collective-permute-start.14 = (bf16[384,128]{1,0:T(8,128)(2,1)S(1)}, bf16[384,128]{1,0:T(8,128)(2,1)S(1)}, u32[]{:S(2)}, u32[]{:S(2)}) collective-permute-start(bf16[384,128]{1,0:T(8,128)(2,1)S(1)} %get-tuple-element.45), channel_id=1, source_target_pairs={{0,4},{1,5},{2,6},{3,7},{4,0},{5,1},{6,2},{7,3},{8,12},{9,13},{10,... | collective-permute-start | bytes 294920 | tf_op jit(solution)/shard_map/ppermute | solution.py:19
  38.7 10.8 %collective-permute-start.10 = (bf16[384,128]{1,0:T(8,128)(2,1)S(1)}, bf16[384,128]{1,0:T(8,128)(2,1)S(1)}, u32[]{:S(2)}, u32[]{:S(2)}) collective-permute-start(bf16[384,128]{1,0:T(8,128)(2,1)S(1)} %get-tuple-element.47), channel_id=1, source_target_pairs={{0,4},{1,5},{2,6},{3,7},{4,0},{5,1},{6,2},{7,3},{8,12},{9,13},{10,... | collective-permute-start | bytes 294920 | tf_op jit(solution)/shard_map/ppermute | solution.py:19
  40.4 11.1 %collective-permute-start.19 = (bf16[384,128]{1,0:T(8,128)(2,1)S(1)}, bf16[384,128]{1,0:T(8,128)(2,1)S(1)}, u32[]{:S(2)}, u32[]{:S(2)}) collective-permute-start(bf16[384,128]{1,0:T(8,128)(2,1)S(1)} %get-tuple-element.35), channel_id=1, source_target_pairs={{0,8},{1,9},{2,10},{3,11},{4,12},{5,13},{6,14},{7,15},{8,0},{9,1},... | collective-permute-start | bytes 294920 | tf_op jit(solution)/shard_map/ppermute | solution.py:19
  43.1 14.7 %collective-permute-start.17 = (bf16[384,128]{1,0:T(8,128)(2,1)S(1)}, bf16[384,128]{1,0:T(8,128)(2,1)S(1)}, u32[]{:S(2)}, u32[]{:S(2)}) collective-permute-start(bf16[384,128]{1,0:T(8,128)(2,1)S(1)} %get-tuple-element.33), channel_id=1, source_target_pairs={{0,8},{1,9},{2,10},{3,11},{4,12},{5,13},{6,14},{7,15},{8,0},{9,1},... | collective-permute-start | bytes 294920 | tf_op jit(solution)/shard_map/ppermute | solution.py:19
  47.8 12.1 %collective-permute-start.15 = (bf16[384,128]{1,0:T(8,128)(2,1)S(1)}, bf16[384,128]{1,0:T(8,128)(2,1)S(1)}, u32[]{:S(2)}, u32[]{:S(2)}) collective-permute-start(bf16[384,128]{1,0:T(8,128)(2,1)S(1)} %get-tuple-element.31), channel_id=1, source_target_pairs={{0,8},{1,9},{2,10},{3,11},{4,12},{5,13},{6,14},{7,15},{8,0},{9,1},... | collective-permute-start | bytes 294920 | tf_op jit(solution)/shard_map/ppermute | solution.py:19
  49.6 11.3 %collective-permute-start.11 = (bf16[384,128]{1,0:T(8,128)(2,1)S(1)}, bf16[384,128]{1,0:T(8,128)(2,1)S(1)}, u32[]{:S(2)}, u32[]{:S(2)}) collective-permute-start(bf16[384,128]{1,0:T(8,128)(2,1)S(1)} %get-tuple-element.26), channel_id=1, source_target_pairs={{0,8},{1,9},{2,10},{3,11},{4,12},{5,13},{6,14},{7,15},{8,0},{9,1},... | collective-permute-start | bytes 294920 | tf_op jit(solution)/shard_map/ppermute | solution.py:19
  51.5 15.3 %collective-permute-start.24 = (bf16[384,128]{1,0:T(8,128)(2,1)S(1)}, bf16[384,128]{1,0:T(8,128)(2,1)S(1)}, u32[]{:S(2)}, u32[]{:S(2)}) collective-permute-start(bf16[384,128]{1,0:T(8,128)(2,1)S(1)} %shard_map.86.refs_3_), channel_id=1, source_target_pairs={{0,4},{1,5},{2,6},{3,7},{4,0},{5,1},{6,2},{7,3},{8,12},{9,13},{10,... | collective-permute-start | bytes 294920 | tf_op jit(solution)/shard_map/ppermute | solution.py:19
  57.9 10.5 %collective-permute-start.23 = (bf16[384,128]{1,0:T(8,128)(2,1)S(1)}, bf16[384,128]{1,0:T(8,128)(2,1)S(1)}, u32[]{:S(2)}, u32[]{:S(2)}) collective-permute-start(bf16[384,128]{1,0:T(8,128)(2,1)S(1)} %shard_map.84.refs_2_), channel_id=1, source_target_pairs={{0,4},{1,5},{2,6},{3,7},{4,0},{5,1},{6,2},{7,3},{8,12},{9,13},{10,... | collective-permute-start | bytes 294920 | tf_op jit(solution)/shard_map/ppermute | solution.py:19
  59.9 8.5 %collective-permute-start.22 = (bf16[384,128]{1,0:T(8,128)(2,1)S(1)}, bf16[384,128]{1,0:T(8,128)(2,1)S(1)}, u32[]{:S(2)}, u32[]{:S(2)}) collective-permute-start(bf16[384,128]{1,0:T(8,128)(2,1)S(1)} %shard_map.82.refs_1_), channel_id=1, source_target_pairs={{0,4},{1,5},{2,6},{3,7},{4,0},{5,1},{6,2},{7,3},{8,12},{9,13},{10,... | collective-permute-start | bytes 294920 | tf_op jit(solution)/shard_map/ppermute | solution.py:19
  60.9 7.5 %collective-permute-start.21 = (bf16[384,128]{1,0:T(8,128)(2,1)S(1)}, bf16[384,128]{1,0:T(8,128)(2,1)S(1)}, u32[]{:S(2)}, u32[]{:S(2)}) collective-permute-start(bf16[384,128]{1,0:T(8,128)(2,1)S(1)} %shard_map.80.refs_0_), channel_id=1, source_target_pairs={{0,4},{1,5},{2,6},{3,7},{4,0},{5,1},{6,2},{7,3},{8,12},{9,13},{10,... | collective-permute-start | bytes 294920 | tf_op jit(solution)/shard_map/ppermute | solution.py:19
  66.9 6.8 %collective-permute-start.20 = (f32[16,2048]{1,0:T(8,128)S(1)}, f32[16,2048]{1,0:T(8,128)S(1)}, u32[]{:S(2)}, u32[]{:S(2)}) collective-permute-start(f32[16,2048]{1,0:T(8,128)S(1)} %shard_map.89), channel_id=1, source_target_pairs={{0,2},{1,3},{2,0},{3,1},{4,6},{5,7},{6,4},{7,5},{8,10},{9,11},{10,... | collective-permute-start | bytes 393224 | tf_op jit(solution)/shard_map/ppermute | solution.py:19
  70.7 5.0 %collective-permute-start.25 = (f32[16,2048]{1,0:T(8,128)S(1)}, f32[16,2048]{1,0:T(8,128)S(1)}, u32[]{:S(2)}, u32[]{:S(2)}) collective-permute-start(f32[16,2048]{1,0:T(8,128)S(1)} %shard_map.91), channel_id=1, source_target_pairs={{0,2},{1,3},{2,0},{3,1},{4,6},{5,7},{6,4},{7,5},{8,10},{9,11},{10,... | collective-permute-start | bytes 393224 | tf_op jit(solution)/shard_map/ppermute | solution.py:19
  75.8 1.4 %copy-start.1 = (bf16[1024,1024]{1,0:T(8,128)(2,1)}, bf16[1024,1024]{1,0:T(8,128)(2,1)S(1)}, u32[]{:S(2)}) copy-start(bf16[1024,1024]{1,0:T(8,128)(2,1)S(1)} %collective-permute-done.26.refs_1_) | copy-start | bytes 6291460
  78.4 5.0 %collective-permute-start.27 = (f32[32,1024]{1,0:T(8,128)S(1)}, f32[32,1024]{1,0:T(8,128)S(1)}, u32[]{:S(2)}, u32[]{:S(2)}) collective-permute-start(f32[32,1024]{1,0:T(8,128)S(1)} %shard_map.93), channel_id=1, source_target_pairs={{0,2},{1,3},{2,0},{3,1},{4,6},{5,7},{6,4},{7,5},{8,10},{9,11},{10,... | collective-permute-start | bytes 393224 | tf_op jit(solution)/shard_map/ppermute | solution.py:19
  83.4 5.7 %collective-permute-start.28 = (f32[32,1024]{1,0:T(8,128)S(1)}, f32[32,1024]{1,0:T(8,128)S(1)}, u32[]{:S(2)}, u32[]{:S(2)}) collective-permute-start(f32[32,1024]{1,0:T(8,128)S(1)} %add.115), channel_id=1, source_target_pairs={{0,4},{1,5},{2,6},{3,7},{4,0},{5,1},{6,2},{7,3},{8,12},{9,13},{10,... | collective-permute-start | bytes 393224 | tf_op jit(solution)/shard_map/ppermute | solution.py:19
  89.2 5.9 %collective-permute-start.29 = (bf16[32,1024]{1,0:T(8,128)(2,1)S(1)}, bf16[32,1024]{1,0:T(8,128)(2,1)S(1)}, u32[]{:S(2)}, u32[]{:S(2)}) collective-permute-start(bf16[32,1024]{1,0:T(8,128)(2,1)S(1)} %get-tuple-element.40), channel_id=1, source_target_pairs={{0,8},{1,9},{2,10},{3,11},{4,12},{5,13},{6,14},{7,15},{8,0},{9,1},... | collective-permute-start | bytes 196616 | tf_op jit(solution)/shard_map/ppermute | solution.py:19
  95.3 1.6 %copy-start.2 = (bf16[1024,1024]{1,0:T(8,128)(2,1)S(1)}, bf16[1024,1024]{1,0:T(8,128)(2,1)}, u32[]{:S(2)}) copy-start(bf16[1024,1024]{1,0:T(8,128)(2,1)} %copy-done.1) | copy-start | bytes 6291460
  98.3 5.3 %collective-permute-start.32 = (f32[1,32]{1,0:T(1,128)S(1)}, f32[1,32]{1,0:T(1,128)S(1)}, u32[]{:S(2)}, u32[]{:S(2)}) collective-permute-start(f32[1,32]{1,0:T(1,128)S(1)} %bitcast.57), channel_id=1, source_target_pairs={{0,4},{1,5},{2,6},{3,7},{4,0},{5,1},{6,2},{7,3},{8,12},{9,13},{10,... | collective-permute-start | bytes 392 | tf_op jit(solution)/shard_map/ppermute | solution.py:19
  98.9 4.7 %collective-permute-start.33 = (f32[1,32]{1,0:T(1,128)S(1)}, f32[1,32]{1,0:T(1,128)S(1)}, u32[]{:S(2)}, u32[]{:S(2)}) collective-permute-start(f32[1,32]{1,0:T(1,128)S(1)} %bitcast.58), channel_id=1, source_target_pairs={{0,8},{1,9},{2,10},{3,11},{4,12},{5,13},{6,14},{7,15},{8,0},{9,1},... | collective-permute-start | bytes 392 | tf_op jit(solution)/shard_map/ppermute | solution.py:19
  101.8 5.4 %collective-permute-start.34 = (f32[1,32]{1,0:T(1,128)S(1)}, f32[1,32]{1,0:T(1,128)S(1)}, u32[]{:S(2)}, u32[]{:S(2)}) collective-permute-start(f32[1,32]{1,0:T(1,128)S(1)} %bitcast.59), channel_id=1, source_target_pairs={{0,12},{1,13},{2,14},{3,15},{4,8},{5,9},{6,10},{7,11},{8,4},{9,5},... | collective-permute-start | bytes 392 | tf_op jit(solution)/shard_map/ppermute | solution.py:19
  102.8 9.0 %collective-permute-start.31 = (f32[32,1024]{1,0:T(8,128)S(1)}, f32[32,1024]{1,0:T(8,128)S(1)}, u32[]{:S(2)}, u32[]{:S(2)}) collective-permute-start(f32[32,1024]{1,0:T(8,128)S(1)} %get-tuple-element.43), channel_id=1, source_target_pairs={{0,1},{1,0},{2,3},{3,2},{4,5},{5,4},{6,7},{7,6},{8,9},{9,8},{10,11... | collective-permute-start | bytes 393224 | tf_op jit(solution)/shard_map/ppermute | solution.py:19
  103.1 8.0 %collective-permute-start.30 = (f32[32,64]{1,0:T(8,128)S(1)}, f32[32,64]{1,0:T(8,128)S(1)}, u32[]{:S(2)}, u32[]{:S(2)}) collective-permute-start(f32[32,64]{1,0:T(8,128)S(1)} %get-tuple-element.48), channel_id=1, source_target_pairs={{0,1},{1,0},{2,3},{3,2},{4,5},{5,4},{6,7},{7,6},{8,9},{9,8},{10,11... | collective-permute-start | bytes 24584 | tf_op jit(solution)/shard_map/ppermute | solution.py:19
  107.2 3.6 %collective-permute-start.35 = (f32[1,32]{1,0:T(1,128)S(1)}, f32[1,32]{1,0:T(1,128)S(1)}, u32[]{:S(2)}, u32[]{:S(2)}) collective-permute-start(f32[1,32]{1,0:T(1,128)S(1)} %add_add_fusion), channel_id=1, source_target_pairs={{0,2},{1,3},{2,0},{3,1},{4,6},{5,7},{6,4},{7,5},{8,10},{9,11},{10,... | collective-permute-start | bytes 392 | tf_op jit(solution)/shard_map/ppermute | solution.py:19
  108.0 2.7 %collective-permute-start.36 = (f32[1,32]{1,0:T(1,128)S(1)}, f32[1,32]{1,0:T(1,128)S(1)}, u32[]{:S(2)}, u32[]{:S(2)}) collective-permute-start(f32[1,32]{1,0:T(1,128)S(1)} %add_add_fusion), channel_id=1, source_target_pairs={{0,1},{1,0},{2,3},{3,2},{4,5},{5,4},{6,7},{7,6},{8,9},{9,8},{10,11... | collective-permute-start | bytes 392 | tf_op jit(solution)/shard_map/ppermute | solution.py:19
  108.0 3.0 %collective-permute-start.37 = (f32[1,32]{1,0:T(1,128)S(1)}, f32[1,32]{1,0:T(1,128)S(1)}, u32[]{:S(2)}, u32[]{:S(2)}) collective-permute-start(f32[1,32]{1,0:T(1,128)S(1)} %add_add_fusion), channel_id=1, source_target_pairs={{0,3},{1,2},{2,1},{3,0},{4,7},{5,6},{6,5},{7,4},{8,11},{9,10},{10,... | collective-permute-start | bytes 392 | tf_op jit(solution)/shard_map/ppermute | solution.py:19

commit v4 on v3

--- a/solution.py
+++ b/solution.py
@@ -87,7 +87,8 @@
         block = pots[place]
         return pairs_of(lax.dynamic_slice(block, (group[0], 0), (group[1], block.shape[1])), vals[place])
 
-    starts = jnp.stack([group[0] for group in groups])
+    mask = sum((me & bit) // bit << (len(spread) - 1 - level) for level, bit in enumerate(spread))
+    marks = jnp.stack([jnp.int32(core), jnp.int32(mask), jnp.int32(me >> 1)] + [group[0] for group in groups])
     own = [cond_all[place][part] for place in (0, 1) for part in parts]
     own_terms = pl.pallas_call(
         functools.partial(own_kernel, CHUNKS),
@@ -105,7 +106,7 @@
         cost_estimate=pl.CostEstimate(
             flops=4 * rows * k_half * val_count * c_half, bytes_accessed=2**22, transcendentals=0
         ),
-    )(starts, vals[0], vals[1], pots[0], pots[1], *own)
+    )(marks, vals[0], vals[1], pots[0], pots[1], *own)
     pairs = {place: [pairs_for(place, group) for group in groups] for place in (2, 3)}
 
     def coefficients(index, part):
@@ -148,7 +149,7 @@
     many = k_half // PIECES >> len(spread)
 
     cond_turned = turned([column for column in cond_all])
-    eig_turned = turned([[eigenpotentials], [eig_core]])
+    eig_turned = [turned([[eigenpotentials]]), turned([[eig_core]])]
 
     def respond(columns, places):
         blocks = [block for column in columns for block in column]
@@ -159,44 +160,43 @@
         return in_vmem(kernel, shape, operands, 10**9, 8, [pltpu.VMEM((height, c_half), BF16)])
 
     here, there = (0, 1), (2, 3)
-    sums = []
+    halves = []
     for columns in (scaled_own, scaled_rest):
         if columns[0][0] is not None:
             arrived = swap(respond(columns, there), 2)
-            total = respond(columns, here) + arrived
-            sums.append(total.reshape(PIECES, -1, many, total.shape[1]))
-    width = sums[0].shape[-1]
-    response = jnp.concatenate(sums, axis=1).swapaxes(0, 1).reshape(k_half, width)
-    for level, bit in enumerate(spread):
-        shaped = response.reshape(1 << level, 2, -1, width)
-        response = jnp.where((me & bit) != 0, shaped[:, ::-1], shaped).reshape(k_half, width)
-
-    intersection = intersect(response, eig_turned)
+            halves.append((respond(columns, here), arrived))
+
+    if many % 8:
+        sums = [(near + arrived).reshape(PIECES, -1, many, near.shape[1]) for near, arrived in halves]
+        width = sums[0].shape[-1]
+        response = jnp.concatenate(sums, axis=1).swapaxes(0, 1).reshape(k_half, width)
+        for level, bit in enumerate(spread):
+            shaped = response.reshape(1 << level, 2, -1, width)
+            response = jnp.where((me & bit) != 0, shaped[:, ::-1], shaped).reshape(k_half, width)
+        halves, marks_used = [(response, jnp.zeros_like(response))], jnp.zeros_like(marks)
+        response, intersection = intersect(marks_used, halves, eig_turned, k_half)
+    else:
+        response, intersection = intersect(marks, halves, eig_turned, many)
     for bit in [2] + spread:
         intersection = intersection + swap(intersection, bit)
     intersection = intersection + swap(intersection.astype(BF16), last).astype(F32)
-    squares = jnp.mean(intersection * intersection, axis=1, keepdims=True)
-    unit = intersection / jnp.sqrt(squares + 1e-06)
     eig_rows = eig_count // count
-
-    def e_block(device):
-        return lax.dynamic_slice(unit, (0, device * eig_rows), (k_half, eig_rows))
-
-    def joined(mine, other):
-        return jnp.where(core == 0, jnp.concatenate([mine, other], 0), jnp.concatenate([other, mine], 0))
-
-    projected = finish(core, e_block(me), swap(e_block(me ^ 1), 1))
-    remainder, share = outside(response, intersection, [eigenpotentials, eig_core])
-    remainder_other = swap(remainder[:, rows:], 1)
-    share = share[:, :1].reshape(1, k_half)
+    remainder, remainder_core, share, *blocks = outside(
+        marks, response, intersection, [eigenpotentials, eig_core], eig_rows
+    )
+    remainder_other = swap(remainder_core, 1)
+    if blocks:
+        mine, other = blocks
+    else:
+        unit = intersection / jnp.sqrt(jnp.mean(intersection * intersection, axis=1, keepdims=True) + 1e-06)
+        mine, other = [lax.dynamic_slice(unit, (0, at * eig_rows), (k_half, eig_rows)) for at in (me, me ^ 1)]
+    projected = finish(marks, mine, swap(other, 1))
     for low_bit, high_bit in zip(bits[::2], bits[1::2] + [0] * (len(bits) % 2)):
         steps = dict.fromkeys(step for step in (low_bit, high_bit, low_bit | high_bit) if step)
         share = share + sum(swap(share, step) for step in steps)
     mine, other = share + swap(share, 2), swap(share, 1) + swap(share, 3)
-    sums = joined(mine, other).reshape(pot_count)
-    scale = jnp.sqrt(sums / points_total + 1e-06)
-    final = lax.optimization_barrier(joined(remainder[:, :rows], remainder_other).T)
-    return (projected, final / scale[None, :])
+    complementary = normalised(marks, mine, other, remainder, remainder_other, points_total)
+    return (projected, complementary.T)
 
 
 def prepare_kernel(chunks, side_ref, cond_ref, *blocks):
@@ -208,7 +208,7 @@
         block[...] = cond_ref[:, pl.ds(begin, width)]
 
 
-def own_kernel(chunks, starts_ref, val0, val1, pot0, pot1, *refs):
+def own_kernel(chunks, marks_ref, val0, val1, pot0, pot1, *refs):
     conds, outs = refs[: 2 * chunks], refs[2 * chunks : -3]
     pairs, right, wide = refs[-3:]
     val_count, rows = val0.shape
@@ -220,7 +220,7 @@
     for group in range(len(outs) // chunks):
         height = outs[group * chunks].shape[0]
         many = height // val_count
-        start = starts_ref[group]
+        start = marks_ref[3 + group]
         for place, val in enumerate((val0, val1)):
             values = val[...].astype(F32)
             for k in range(many):
@@ -284,49 +284,105 @@
     return in_vmem(kernel, shape, blocks, 2 * 10**9, 12)
 
 
-def finish(core, mine, other):
-    def kernel(core_ref, mine_ref, other_ref, out_ref):
-        mine, other = mine_ref[...], other_ref[...]
-        first = core_ref[0] == 0
-        out_ref[...] = jnp.concatenate([jnp.where(first, mine, other), jnp.where(first, other, mine)], axis=0).T
-
+def with_marks(kernel, out_shape, operands, megabytes):
     return pl.pallas_call(
         kernel,
-        out_shape=jax.ShapeDtypeStruct((mine.shape[1], 2 * mine.shape[0]), F32),
-        in_specs=[pl.BlockSpec(memory_space=pltpu.SMEM)] + [pl.BlockSpec(memory_space=pltpu.VMEM)] * 2,
-        out_specs=pl.BlockSpec(memory_space=pltpu.VMEM),
-        compiler_params=pltpu.CompilerParams(vmem_limit_bytes=2**21),
-        cost_estimate=pl.CostEstimate(flops=10**8, bytes_accessed=2**16, transcendentals=0),
-    )(core[None], mine, other)
-
-
-def intersect(response, eig_turned):
-    def kernel(response_ref, eig_ref, out_ref):
-        out_ref[...] = contract_last(eig_ref[...], response_ref[...].astype(BF16)).T
-
-    shape = jax.ShapeDtypeStruct((response.shape[0], eig_turned.shape[0]), F32)
-    return in_vmem(kernel, shape, [response, eig_turned], 10**9, 8)
-
-
-def outside(response, intersection, eig_blocks):
-    rows = eig_blocks[0].shape[0]
-
-    def kernel(response_ref, part_ref, *refs):
-        eigs, (out_ref, share_ref) = refs[:-2], refs[-2:]
+        out_shape=out_shape,
+        in_specs=[pl.BlockSpec(memory_space=pltpu.SMEM)]
+        + [pl.BlockSpec(memory_space=pltpu.VMEM)] * (len(operands) - 1),
+        out_specs=jax.tree.map(lambda _: pl.BlockSpec(memory_space=pltpu.VMEM), out_shape),
+        compiler_params=pltpu.CompilerParams(vmem_limit_bytes=megabytes * 2**20),
+        cost_estimate=pl.CostEstimate(flops=10**9, bytes_accessed=2**22, transcendentals=0),
+    )(*operands)
+
+
+def finish(marks, mine, other):
+    def kernel(marks_ref, mine_ref, other_ref, out_ref):
+        mine, other = mine_ref[...], other_ref[...]
+        first = marks_ref[0] == 0
+        out_ref[...] = jnp.concatenate([jnp.where(first, mine, other), jnp.where(first, other, mine)], axis=0).T
+
+    shape = jax.ShapeDtypeStruct((mine.shape[1], 2 * mine.shape[0]), F32)
+    return with_marks(kernel, shape, [marks, mine, other], 2)
+
+
+def intersect(marks, halves, eig_turned, many):
+    rows = eig_turned[0].shape[1]
+    width = halves[0][0].shape[1]
+    height = sum(near.shape[0] for near, _ in halves)
+    own = halves[0][0].shape[0] // many
+    blocks = height // (own * many)
+
+    def kernel(marks_ref, *refs):
+        eigs, (response_ref, out_ref) = refs[-2 - len(eig_turned) : -2], refs[-2:]
+        mask = marks_ref[1]
+        for q in range(own):
+            for block in range(blocks):
+                near, arrived = refs[0:2] if block == 0 else refs[2:4]
+                top = q * many if block == 0 else (q * (blocks - 1) + block - 1) * many
+                spot = (block ^ mask) * (own * many) + q * many
+                spot = pl.ds(pl.multiple_of(spot, many), many)
+                response_ref[spot, :] = near[top : top + many, :] + arrived[top : top + many, :]
+        total = None
+        for index, eig in enumerate(eigs):
+            low = response_ref[:, index * rows : (index + 1) * rows].astype(BF16)
+            term = contract_last(eig[...], low)
+            total = term if total is None else total + term
+        out_ref[...] = total.T
+
+    shapes = (
+        jax.ShapeDtypeStruct((height, width), F32),
+        jax.ShapeDtypeStruct((height, eig_turned[0].shape[0]), F32),
+    )
+    operands = [marks, *[block for pair in halves for block in pair], *eig_turned]
+    return with_marks(kernel, shapes, operands, 8)
+
+
+def outside(marks, response, intersection, eig_blocks, eig_rows):
+    rows, eig_count = eig_blocks[0].shape
+    count = response.shape[0]
+    pair = 2 * eig_rows
+
+    def kernel(marks_ref, response_ref, part_ref, *refs):
+        eigs, outs = refs[: len(eig_blocks)], refs[len(eig_blocks) :]
         low = part_ref[...].astype(BF16)
-        share = jnp.zeros((low.shape[0], 1), F32)
+        share = jnp.zeros((count, 1), F32)
         for index, eig in enumerate(eigs):
             spot = slice(index * rows, (index + 1) * rows)
             left = response_ref[:, spot] - contract_last(eig[...], low).T
-            out_ref[:, spot] = left
+            outs[index][...] = left
             share = share + jnp.sum(left * left, axis=1, keepdims=True)
-        share_ref[...] = jnp.broadcast_to(share, share_ref.shape)
-
-    shapes = (
-        jax.ShapeDtypeStruct(response.shape, F32),
-        jax.ShapeDtypeStruct((response.shape[0], 128), F32),
-    )
-    return in_vmem(kernel, shapes, [response, intersection, *eig_blocks], 10**9, 12)
+        outs[2][...] = jnp.sum(jnp.where(diagonal(count), share, 0.0), axis=0, keepdims=True)
+        if len(outs) > 3:
+            squares = jnp.sum(part_ref[...] * part_ref[...], axis=1, keepdims=True) / eig_count
+            window = part_ref[:, pl.ds(pl.multiple_of(marks_ref[2] * pair, pair), pair)]
+            window = window / jnp.sqrt(squares + 1e-06)
+            first = marks_ref[0] == 0
+            outs[3][...] = jnp.where(first, window[:, :eig_rows], window[:, eig_rows:])
+            outs[4][...] = jnp.where(first, window[:, eig_rows:], window[:, :eig_rows])
+
+    sizes = [(count, rows), (count, rows), (1, count)] + ([] if pair % 128 else [(count, eig_rows)] * 2)
+    shapes = tuple(jax.ShapeDtypeStruct(size, F32) for size in sizes)
+    return with_marks(kernel, shapes, [marks, response, intersection, *eig_blocks], 12)
+
+
+def diagonal(size):
+    shape = (size, size)
+    return lax.broadcasted_iota(jnp.int32, shape, 0) == lax.broadcasted_iota(jnp.int32, shape, 1)
+
+
+def normalised(marks, sum_mine, sum_other, mine, other, points_total):
+    height, width = mine.shape
+
+    def kernel(marks_ref, sum_mine_ref, sum_other_ref, mine_ref, other_ref, out_ref):
+        core = marks_ref[0]
+        for row_ref, block_ref, half in ((sum_mine_ref, mine_ref, core), (sum_other_ref, other_ref, 1 - core)):
+            column = jnp.sum(jnp.where(diagonal(height), row_ref[...], 0.0), axis=1, keepdims=True)
+            block = block_ref[...] / jnp.sqrt(column / points_total + 1e-06)
+            out_ref[pl.ds(pl.multiple_of(half * height, height), height), :] = block
+
+    shape = jax.ShapeDtypeStruct((2 * height, width), F32)
+    return with_marks(kernel, shape, [marks, sum_mine, sum_other, mine, other], 4)
 
 
 def respond_kernel(places, chunks, *refs):

time: 113 us -> 111 us (0.982)
  waiting for transfers between devices: 45.8 us -> 41.6 us
  Pallas kernels: 17.3 us -> 20.5 us
  other arithmetic: 2.4 us -> 1.22 us
    pallas_call x1 -> x4, Pallas kernels: 0.7 us -> 6.4 us  [with_marks(): pl.pallas_call(kernel, out_shape=out_shape, in_specs=[pl.BlockSpec(memory...]
    ppermute x38, waiting for transfers between devices: 45.8 us -> 41.6 us  [swap(): return lax.ppermute(block, 'grid', [(i, i ^ bit) for i in range(count)])]
    pallas_call x16 -> x15, Pallas kernels: 14 us -> 11.4 us  [in_vmem(): pl.pallas_call(kernel, out_shape=out_shape, in_specs=[pl.BlockSpec(memory...]
    unnamed x12 -> x10, local copies, waits for them, and re-layouts: 2.94 us -> 2.83 us
  transfers between devices with their start and end apart: 38 -> 38, of which waited for: 19 -> 20; matrix products, arithmetic and copies ran while one was open for 6% -> 7% of each run, Pallas kernels for 12% -> 14%
where the time goes in v4:
time: 111 us
  waiting for transfers between devices  41.6 us (37%)
  starting transfers between devices  37.5 us (34%)
  Pallas kernels  20.5 us (18%)
  matrix products  4.63 us (4%)
  local copies, waits for them, and re-layouts  4.49 us (4%)
  other arithmetic  1.22 us (1%)
    ppermute x38, waiting for transfers between devices, swap(): return lax.ppermute(block, 'grid', [(i, i ^ bit) for i in range(count)])  41.6 us
    ppermute x38, starting transfers between devices, swap(): return lax.ppermute(block, 'grid', [(i, i ^ bit) for i in range(count)])  37.5 us
    pallas_call x15, Pallas kernels, in_vmem(): pl.pallas_call(kernel, out_shape=out_shape, in_specs=[pl.BlockSpec(memory...  11.4 us
    pallas_call x4, Pallas kernels, with_marks(): pl.pallas_call(kernel, out_shape=out_shape, in_specs=[pl.BlockSpec(memory...  6.4 us
    dot_general x8, matrix products, contract(): return jnp.dot(left, right, preferred_element_type=F32)  4.63 us
    unnamed x10, local copies, waits for them, and re-layouts  2.83 us
    pallas_call x1, Pallas kernels, body(): pl.pallas_call(functools.partial(own_kernel, CHUNKS), out_shape=[jax.Shap...  2.47 us
  transfers between devices with their start and end apart: 38, of which 20 were waited for; matrix products, arithmetic and copies ran while one was open for 7% of the time, Pallas kernels for 14%

profile of v4, /device:TPU:0, one launch (start us, length us, event | category | flops | bytes accessed | tf_op | source)
XLA Modules:
  0.0 110.9 jit_solution(564449891369699208)
XLA Ops:
  0.6 3.1 %collective-permute-start.5 = (bf16[48,1024]{1,0:T(8,128)(2,1)}, bf16[48,1024]{1,0:T(8,128)(2,1)S(1)}, u32[]{:S(2)}, u32[]{:S(2)}) collective-permute-start(bf16[48,1024]{1,0:T(8,128)(2,1)} %bitcast.32), channel_id=1, source_target_pairs={{0,2},{1,3},{2,0},{3,1},{4,6},{5,7},{6,4},{7,5},{8,10},{9,11},{10,... | collective-permute-start | bytes 294920 | tf_op jit(solution)/shard_map/ppermute | solution.py:19
  4.4 0.8 dynamic_slice.19
  5.1 0.7 subtract_divide_fusion
  5.9 1.2 %copy-done.2 = bf16[1024,512]{1,0:T(8,128)(2,1)S(1)} copy-done((bf16[1024,512]{1,0:T(8,128)(2,1)S(1)}, bf16[1024,512]{1,0:T(8,128)(2,1)}, u32[]{:S(2)}) %copy-start.2) | copy-done | bytes 1048600
  7.4 1.6 %copy-done = bf16[1024,1024]{1,0:T(8,128)(2,1)S(1)} copy-done((bf16[1024,1024]{1,0:T(8,128)(2,1)S(1)}, bf16[1024,1024]{1,0:T(8,128)(2,1)}, u32[]{:S(2)}) %copy-start) | copy-done | bytes 2097176
  9.0 0.6 shard_map.92.refs_4_
  9.9 1.6 %collective-permute-start.6 = (bf16[1024,128]{1,0:T(8,128)(2,1)S(1)}, bf16[1024,128]{1,0:T(8,128)(2,1)S(1)}, u32[]{:S(2)}, u32[]{:S(2)}) collective-permute-start(bf16[1024,128]{1,0:T(8,128)(2,1)S(1)} %get-tuple-element.28), channel_id=1, source_target_pairs={{0,2},{1,3},{2,0},{3,1},{4,6},{5,7},{6,4},{7,5},{8,10},{9,11},{10,... | collective-permute-start | bytes 786440 | tf_op jit(solution)/shard_map/ppermute | solution.py:19
  11.6 0.8 constant_dynamic-slice_fusion.1
  12.6 5.6 %collective-permute-done.6.refs_4_ = bf16[1024,128]{1,0:T(8,128)(2,1)S(1)} collective-permute-done((bf16[1024,128]{1,0:T(8,128)(2,1)S(1)}, bf16[1024,128]{1,0:T(8,128)(2,1)S(1)}, u32[]{:S(2)}, u32[]{:S(2)}) %collective-permute-start.6) | collective-permute-done | bytes 262176 | tf_op jit(solution)/shard_map/ppermute | solution.py:19
  18.3 0.6 fusion.6
  18.8 1.0 collective-permute-done.7
  20.0 1.1 %collective-permute-done.8.refs_6_ = bf16[48,1024]{1,0:T(8,128)(2,1)S(1)} collective-permute-done((bf16[48,1024]{1,0:T(8,128)(2,1)S(1)}, bf16[48,1024]{1,0:T(8,128)(2,1)S(1)}, u32[]{:S(2)}, u32[]{:S(2)}) %collective-permute-start.8) | collective-permute-done | bytes 98336 | tf_op jit(solution)/shard_map/ppermute | solution.py:19
  21.1 1.7 %collective-permute-start.12 = (bf16[1024,128]{1,0:T(8,128)(2,1)S(1)}, bf16[1024,128]{1,0:T(8,128)(2,1)S(1)}, u32[]{:S(2)}, u32[]{:S(2)}) collective-permute-start(bf16[1024,128]{1,0:T(8,128)(2,1)S(1)} %get-tuple-element.33), channel_id=1, source_target_pairs={{0,2},{1,3},{2,0},{3,1},{4,6},{5,7},{6,4},{7,5},{8,10},{9,11},{10,... | collective-permute-start | bytes 786440 | tf_op jit(solution)/shard_map/ppermute | solution.py:19
  23.1 0.6 fusion.7
  23.7 5.8 %collective-permute-done.12.refs_5_ = bf16[1024,128]{1,0:T(8,128)(2,1)S(1)} collective-permute-done((bf16[1024,128]{1,0:T(8,128)(2,1)S(1)}, bf16[1024,128]{1,0:T(8,128)(2,1)S(1)}, u32[]{:S(2)}, u32[]{:S(2)}) %collective-permute-start.12) | collective-permute-done | bytes 262176 | tf_op jit(solution)/shard_map/ppermute | solution.py:19
  29.5 0.6 fusion.8
  30.1 0.6 collective-permute-start.9
  31.0 2.5 %shard_map.78 = (f32[768,128]{1,0:T(8,128)S(1)}, f32[768,128]{1,0:T(8,128)S(1)}, f32[768,128]{1,0:T(8,128)S(1)}, f32[768,128]{1,0:T(8,128)S(1)}) custom-call(s32[5]{0:T(128)S(1)} %stack.23.marks_ref, bf16[48,1024]{1,0:T(8,128)(2,1)S(1)} %bitcast.34, bf16[48,1024]{1,0:T(8,128)(2,1)S(1)} %collective-permute-done.val1.refs_6_, bf16[64,1024]{1,0:T(8,128)(2,1)S(1)} %bitcast.31, ...), custom_call_target="tpu_custom_call" | custom-call | flops 1610612736 | bytes 4194304 | tf_op jit(solution)/shard_map/pallas_call | solution.py:93
  33.5 0.6 fusion.9
  34.1 0.6 fusion
  34.7 1.9 %collective-permute-start.10 = (bf16[384,128]{1,0:T(8,128)(2,1)S(1)}, bf16[384,128]{1,0:T(8,128)(2,1)S(1)}, u32[]{:S(2)}, u32[]{:S(2)}) collective-permute-start(bf16[384,128]{1,0:T(8,128)(2,1)S(1)} %get-tuple-element.53), channel_id=1, source_target_pairs={{0,4},{1,5},{2,6},{3,7},{4,0},{5,1},{6,2},{7,3},{8,12},{9,13},{10,... | collective-permute-start | bytes 294920 | tf_op jit(solution)/shard_map/ppermute | solution.py:19
  36.6 0.6 fusion.1
  37.5 1.8 %collective-permute-start.16 = (bf16[384,128]{1,0:T(8,128)(2,1)S(1)}, bf16[384,128]{1,0:T(8,128)(2,1)S(1)}, u32[]{:S(2)}, u32[]{:S(2)}) collective-permute-start(bf16[384,128]{1,0:T(8,128)(2,1)S(1)} %get-tuple-element.52), channel_id=1, source_target_pairs={{0,4},{1,5},{2,6},{3,7},{4,0},{5,1},{6,2},{7,3},{8,12},{9,13},{10,... | collective-permute-start | bytes 294920 | tf_op jit(solution)/shard_map/ppermute | solution.py:19
  39.5 0.6 convolution_add_fusion.3.block_ref
  40.1 0.6 convolution_add_fusion.1.block_ref
  40.8 2.9 %collective-permute-start.11 = (bf16[384,128]{1,0:T(8,128)(2,1)S(1)}, bf16[384,128]{1,0:T(8,128)(2,1)S(1)}, u32[]{:S(2)}, u32[]{:S(2)}) collective-permute-start(bf16[384,128]{1,0:T(8,128)(2,1)S(1)} %get-tuple-element.31), channel_id=1, source_target_pairs={{0,8},{1,9},{2,10},{3,11},{4,12},{5,13},{6,14},{7,15},{8,0},{9,1},... | collective-permute-start | bytes 294920 | tf_op jit(solution)/shard_map/ppermute | solution.py:19
  43.7 1.9 %collective-permute-start.15 = (bf16[384,128]{1,0:T(8,128)(2,1)S(1)}, bf16[384,128]{1,0:T(8,128)(2,1)S(1)}, u32[]{:S(2)}, u32[]{:S(2)}) collective-permute-start(bf16[384,128]{1,0:T(8,128)(2,1)S(1)} %get-tuple-element.36), channel_id=1, source_target_pairs={{0,8},{1,9},{2,10},{3,11},{4,12},{5,13},{6,14},{7,15},{8,0},{9,1},... | collective-permute-start | bytes 294920 | tf_op jit(solution)/shard_map/ppermute | solution.py:19
  45.6 3.1 %collective-permute-done.16.refs_0_ = bf16[384,128]{1,0:T(8,128)(2,1)S(1)} collective-permute-done((bf16[384,128]{1,0:T(8,128)(2,1)S(1)}, bf16[384,128]{1,0:T(8,128)(2,1)S(1)}, u32[]{:S(2)}, u32[]{:S(2)}) %collective-permute-start.16) | collective-permute-done | bytes 98336 | tf_op jit(solution)/shard_map/ppermute | solution.py:19
  48.8 1.3 %collective-permute-done.18.refs_0_ = bf16[384,128]{1,0:T(8,128)(2,1)S(1)} collective-permute-done((bf16[384,128]{1,0:T(8,128)(2,1)S(1)}, bf16[384,128]{1,0:T(8,128)(2,1)S(1)}, u32[]{:S(2)}, u32[]{:S(2)}) %collective-permute-start.18) | collective-permute-done | bytes 98336 | tf_op jit(solution)/shard_map/ppermute | solution.py:19
  50.1 1.7 %collective-permute-start.19 = (bf16[384,128]{1,0:T(8,128)(2,1)S(1)}, bf16[384,128]{1,0:T(8,128)(2,1)S(1)}, u32[]{:S(2)}, u32[]{:S(2)}) collective-permute-start(bf16[384,128]{1,0:T(8,128)(2,1)S(1)} %get-tuple-element.40), channel_id=1, source_target_pairs={{0,8},{1,9},{2,10},{3,11},{4,12},{5,13},{6,14},{7,15},{8,0},{9,1},... | collective-permute-start | bytes 294920 | tf_op jit(solution)/shard_map/ppermute | solution.py:19
  51.8 0.6 shard_map.87.refs_4_
  52.4 4.1 %collective-permute-start.21 = (bf16[384,128]{1,0:T(8,128)(2,1)S(1)}, bf16[384,128]{1,0:T(8,128)(2,1)S(1)}, u32[]{:S(2)}, u32[]{:S(2)}) collective-permute-start(bf16[384,128]{1,0:T(8,128)(2,1)S(1)} %shard_map.80.refs_0_), channel_id=1, source_target_pairs={{0,4},{1,5},{2,6},{3,7},{4,0},{5,1},{6,2},{7,3},{8,12},{9,13},{10,... | collective-permute-start | bytes 294920 | tf_op jit(solution)/shard_map/ppermute | solution.py:19
  56.6 1.7 %collective-permute-done.15.other_ref = bf16[384,128]{1,0:T(8,128)(2,1)S(1)} collective-permute-done((bf16[384,128]{1,0:T(8,128)(2,1)S(1)}, bf16[384,128]{1,0:T(8,128)(2,1)S(1)}, u32[]{:S(2)}, u32[]{:S(2)}) %collective-permute-start.15) | collective-permute-done | bytes 98336 | tf_op jit(solution)/shard_map/ppermute | solution.py:19
  58.3 0.5 collective-permute-start.22
  58.8 1.3 %collective-permute-done.17.other_ref = bf16[384,128]{1,0:T(8,128)(2,1)S(1)} collective-permute-done((bf16[384,128]{1,0:T(8,128)(2,1)S(1)}, bf16[384,128]{1,0:T(8,128)(2,1)S(1)}, u32[]{:S(2)}, u32[]{:S(2)}) %collective-permute-start.17) | collective-permute-done | bytes 98336 | tf_op jit(solution)/shard_map/ppermute | solution.py:19
  60.5 0.7 collective-permute-done.19.other_ref
  61.3 1.1 %collective-permute-start.24 = (bf16[384,128]{1,0:T(8,128)(2,1)S(1)}, bf16[384,128]{1,0:T(8,128)(2,1)S(1)}, u32[]{:S(2)}, u32[]{:S(2)}) collective-permute-start(bf16[384,128]{1,0:T(8,128)(2,1)S(1)} %shard_map.86.refs_3_), channel_id=1, source_target_pairs={{0,4},{1,5},{2,6},{3,7},{4,0},{5,1},{6,2},{7,3},{8,12},{9,13},{10,... | collective-permute-start | bytes 294920 | tf_op jit(solution)/shard_map/ppermute | solution.py:19
  62.4 2.4 %shard_map.88.refs_0_ = f32[16,2048]{1,0:T(8,128)S(1)} custom-call(bf16[384,128]{1,0:T(8,128)(2,1)S(1)} %shard_map.80.refs_0_, bf16[384,128]{1,0:T(8,128)(2,1)S(1)} %shard_map.82.refs_1_, bf16[384,128]{1,0:T(8,128)(2,1)S(1)} %shard_map.84.refs_2_, bf16[384,128]{1,0:T(8,128)(2,1)S(1)} %shard_map.86.refs_3_, bf16[256,4096]{1,0:T(8,128)(2,1)S(1)} %shard_map.87.refs_4_, ...), custom_call_target="tpu_custom_call" | custom-call | flops 1000000000 | bytes 4194304 | tf_op jit(solution)/shard_map/pallas_call | solution.py:235
  64.9 2.3 %shard_map.89 = f32[16,2048]{1,0:T(8,128)S(1)} custom-call(bf16[384,128]{1,0:T(8,128)(2,1)S(1)} %shard_map.80.refs_0_, bf16[384,128]{1,0:T(8,128)(2,1)S(1)} %shard_map.82.refs_1_, bf16[384,128]{1,0:T(8,128)(2,1)S(1)} %shard_map.84.refs_2_, bf16[384,128]{1,0:T(8,128)(2,1)S(1)} %shard_map.86.refs_3_, bf16[256,4096]{1,0:T(8,128)(2,1)S(1)} %shard_map.87.refs_4_, ...), custom_call_target="tpu_custom_call" | custom-call | flops 1000000000 | bytes 4194304 | tf_op jit(solution)/shard_map/pallas_call | solution.py:235
  67.2 1.8 %collective-permute-start.20 = (f32[16,2048]{1,0:T(8,128)S(1)}, f32[16,2048]{1,0:T(8,128)S(1)}, u32[]{:S(2)}, u32[]{:S(2)}) collective-permute-start(f32[16,2048]{1,0:T(8,128)S(1)} %shard_map.89), channel_id=1, source_target_pairs={{0,2},{1,3},{2,0},{3,1},{4,6},{5,7},{6,4},{7,5},{8,10},{9,11},{10,... | collective-permute-start | bytes 393224 | tf_op jit(solution)/shard_map/ppermute | solution.py:19
  69.0 2.3 %shard_map.91 = f32[16,2048]{1,0:T(8,128)S(1)} custom-call(bf16[384,128]{1,0:T(8,128)(2,1)S(1)} %collective-permute-done.21.refs_0_, bf16[384,128]{1,0:T(8,128)(2,1)S(1)} %collective-permute-done.22.refs_1_, bf16[384,128]{1,0:T(8,128)(2,1)S(1)} %collective-permute-done.23.refs_2_, bf16[384,128]{1,0:T(8,128)(2,1)S(1)} %collective-permute-done.24.refs_3_, ...), custom_call_target="tpu_custom_call" | custom-call | flops 1000000000 | bytes 4194304 | tf_op jit(solution)/shard_map/pallas_call | solution.py:235
  71.3 0.5 collective-permute-start.25
  71.8 2.3 %shard_map.90.refs_2_ = f32[16,2048]{1,0:T(8,128)S(1)} custom-call(bf16[384,128]{1,0:T(8,128)(2,1)S(1)} %collective-permute-done.21.refs_0_, bf16[384,128]{1,0:T(8,128)(2,1)S(1)} %collective-permute-done.22.refs_1_, bf16[384,128]{1,0:T(8,128)(2,1)S(1)} %collective-permute-done.23.refs_2_, bf16[384,128]{1,0:T(8,128)(2,1)S(1)} %collective-permute-done.24.refs_3_, ...), custom_call_target="tpu_custom_call" | custom-call | flops 1000000000 | bytes 4194304 | tf_op jit(solution)/shard_map/pallas_call | solution.py:235
  74.1 0.6 shard_map.93.refs_5_
  74.8 1.6 %collective-permute-done.25.refs_3_ = f32[16,2048]{1,0:T(8,128)S(1)} collective-permute-done((f32[16,2048]{1,0:T(8,128)S(1)}, f32[16,2048]{1,0:T(8,128)S(1)}, u32[]{:S(2)}, u32[]{:S(2)}) %collective-permute-start.25) | collective-permute-done | bytes 131104 | tf_op jit(solution)/shard_map/ppermute | solution.py:19
  76.3 1.8 %shard_map.94 = (f32[32,2048]{1,0:T(8,128)S(1)}, f32[32,1024]{1,0:T(8,128)S(1)}) custom-call(s32[5]{0:T(128)S(1)} %stack.23.marks_ref, f32[16,2048]{1,0:T(8,128)S(1)} %shard_map.88.refs_0_, f32[16,2048]{1,0:T(8,128)S(1)} %collective-permute-done.20.refs_1_, f32[16,2048]{1,0:T(8,128)S(1)} %shard_map.90.refs_2_, ...), custom_call_target="tpu_custom_call" | custom-call | flops 1000000000 | bytes 4194304 | tf_op jit(solution)/shard_map/pallas_call | solution.py:288
  78.6 4.6 %collective-permute-done.27 = f32[32,1024]{1,0:T(8,128)S(1)} collective-permute-done((f32[32,1024]{1,0:T(8,128)S(1)}, f32[32,1024]{1,0:T(8,128)S(1)}, u32[]{:S(2)}, u32[]{:S(2)}) %collective-permute-start.27) | collective-permute-done | bytes 131104 | tf_op jit(solution)/shard_map/ppermute | solution.py:19
  83.2 1.0 collective-permute-start.28
  84.2 4.7 %collective-permute-done.28 = f32[32,1024]{1,0:T(8,128)S(1)} collective-permute-done((f32[32,1024]{1,0:T(8,128)S(1)}, f32[32,1024]{1,0:T(8,128)S(1)}, u32[]{:S(2)}, u32[]{:S(2)}) %collective-permute-start.28) | collective-permute-done | bytes 131104 | tf_op jit(solution)/shard_map/ppermute | solution.py:19
  89.0 1.7 %collective-permute-start.29 = (bf16[32,1024]{1,0:T(8,128)(2,1)S(1)}, bf16[32,1024]{1,0:T(8,128)(2,1)S(1)}, u32[]{:S(2)}, u32[]{:S(2)}) collective-permute-start(bf16[32,1024]{1,0:T(8,128)(2,1)S(1)} %get-tuple-element.48), channel_id=1, source_target_pairs={{0,8},{1,9},{2,10},{3,11},{4,12},{5,13},{6,14},{7,15},{8,0},{9,1},... | collective-permute-start | bytes 196616 | tf_op jit(solution)/shard_map/ppermute | solution.py:19
  90.7 4.2 %collective-permute-done.29 = bf16[32,1024]{1,0:T(8,128)(2,1)S(1)} collective-permute-done((bf16[32,1024]{1,0:T(8,128)(2,1)S(1)}, bf16[32,1024]{1,0:T(8,128)(2,1)S(1)}, u32[]{:S(2)}, u32[]{:S(2)}) %collective-permute-start.29) | collective-permute-done | bytes 65568 | tf_op jit(solution)/shard_map/ppermute | solution.py:19
  94.9 2.0 %shard_map.95 = (f32[32,1024]{1,0:T(8,128)S(1)}, f32[32,1024]{1,0:T(8,128)S(1)}, f32[1,32]{1,0:T(1,128)S(1)}, f32[32,64]{1,0:T(8,128)S(1)}, f32[32,64]{1,0:T(8,128)S(1)}) custom-call(s32[5]{0:T(128)S(1)} %stack.23.marks_ref, f32[32,2048]{1,0:T(8,128)S(1)} %get-tuple-element.41.response_ref, f32[32,1024]{1,0:T(8,128)S(1)} %convert_add_fusion.part_ref, ...), custom_call_target="tpu_custom_call" | custom-call | flops 1000000000 | bytes 4194304 | tf_op jit(solution)/shard_map/pallas_call | solution.py:288
  96.9 2.6 %collective-permute-start.33 = (f32[1,32]{1,0:T(1,128)S(1)}, f32[1,32]{1,0:T(1,128)S(1)}, u32[]{:S(2)}, u32[]{:S(2)}) collective-permute-start(f32[1,32]{1,0:T(1,128)S(1)} %get-tuple-element.45), channel_id=1, source_target_pairs={{0,12},{1,13},{2,14},{3,15},{4,8},{5,9},{6,10},{7,11},{8,4},{9,5},... | collective-permute-start | bytes 392 | tf_op jit(solution)/shard_map/ppermute | solution.py:19
  99.5 1.8 %collective-permute-start.32 = (f32[1,32]{1,0:T(1,128)S(1)}, f32[1,32]{1,0:T(1,128)S(1)}, u32[]{:S(2)}, u32[]{:S(2)}) collective-permute-start(f32[1,32]{1,0:T(1,128)S(1)} %get-tuple-element.45), channel_id=1, source_target_pairs={{0,8},{1,9},{2,10},{3,11},{4,12},{5,13},{6,14},{7,15},{8,0},{9,1},... | collective-permute-start | bytes 392 | tf_op jit(solution)/shard_map/ppermute | solution.py:19
  101.4 0.5 collective-permute-start.37
  101.9 0.5 collective-permute-done.33
  102.3 0.7 collective-permute-done.31
  103.1 0.9 collective-permute-done.32
  104.0 1.2 %collective-permute-start.34 = (f32[1,32]{1,0:T(1,128)S(1)}, f32[1,32]{1,0:T(1,128)S(1)}, u32[]{:S(2)}, u32[]{:S(2)}) collective-permute-start(f32[1,32]{1,0:T(1,128)S(1)} %add_add_fusion), channel_id=1, source_target_pairs={{0,2},{1,3},{2,0},{3,1},{4,6},{5,7},{6,4},{7,5},{8,10},{9,11},{10,... | collective-permute-start | bytes 392 | tf_op jit(solution)/shard_map/ppermute | solution.py:19
  105.2 0.9 collective-permute-start.36
  106.1 1.4 %collective-permute-done.34 = f32[1,32]{1,0:T(1,128)S(1)} collective-permute-done((f32[1,32]{1,0:T(1,128)S(1)}, f32[1,32]{1,0:T(1,128)S(1)}, u32[]{:S(2)}, u32[]{:S(2)}) %collective-permute-start.34) | collective-permute-done | bytes 160 | tf_op jit(solution)/shard_map/ppermute | solution.py:19
  107.6 0.7 collective-permute-done.36
  108.2 1.2 %shard_map.96 = f32[64,64]{1,0:T(8,128)} custom-call(s32[5]{0:T(128)S(1)} %stack.23.marks_ref, f32[32,64]{1,0:T(8,128)S(1)} %get-tuple-element.43.mine_ref, f32[32,64]{1,0:T(8,128)S(1)} %collective-permute-done.30.other_ref), custom_call_target="tpu_custom_call" | custom-call | flops 1000000000 | bytes 4194304 | tf_op jit(solution)/shard_map/pallas_call | solution.py:288
  109.5 1.4 %shard_map.97 = f32[64,1024]{1,0:T(8,128)} custom-call(s32[5]{0:T(128)S(1)} %stack.23.marks_ref, f32[1,32]{1,0:T(1,128)S(1)} %add.85.sum_mine_ref, f32[1,32]{1,0:T(1,128)S(1)} %add.86.sum_other_ref, f32[32,1024]{1,0:T(8,128)S(1)} %get-tuple-element.46.mine_ref, f32[32,1024]{1,0:T(8,128)S(1)} %collective-permute-done.37.other_ref), custom_call_target="tpu_custom_call" | custom-call | flops 1000000000 | bytes 4194304 | tf_op jit(solution)/shard_map/pallas_call | solution.py:288
  (67 shorter events, 4.0 us)
Async XLA Ops:
  0.6 11.7 %collective-permute-start.5 = (bf16[48,1024]{1,0:T(8,128)(2,1)}, bf16[48,1024]{1,0:T(8,128)(2,1)S(1)}, u32[]{:S(2)}, u32[]{:S(2)}) collective-permute-start(bf16[48,1024]{1,0:T(8,128)(2,1)} %bitcast.32), channel_id=1, source_target_pairs={{0,2},{1,3},{2,0},{3,1},{4,6},{5,7},{6,4},{7,5},{8,10},{9,11},{10,... | collective-permute-start | bytes 294920 | tf_op jit(solution)/shard_map/ppermute | solution.py:19
  3.7 26.4 %collective-permute-start = (bf16[48,1024]{1,0:T(8,128)(2,1)}, bf16[48,1024]{1,0:T(8,128)(2,1)S(1)}, u32[]{:S(2)}, u32[]{:S(2)}) collective-permute-start(bf16[48,1024]{1,0:T(8,128)(2,1)} %bitcast.33), channel_id=1, source_target_pairs={{0,1},{1,0},{2,3},{3,2},{4,5},{5,4},{6,7},{7,6},{8,9},{9,8},{10,11... | collective-permute-start | bytes 294920 | tf_op jit(solution)/shard_map/ppermute | solution.py:19
  3.7 6.2 %collective-permute-start.4 = (bf16[64,1024]{1,0:T(8,128)(2,1)}, bf16[64,1024]{1,0:T(8,128)(2,1)}, u32[]{:S(2)}, u32[]{:S(2)}) collective-permute-start(bf16[64,1024]{1,0:T(8,128)(2,1)} %bitcast.29), channel_id=1, source_target_pairs={{0,2},{1,3},{2,0},{3,1},{4,6},{5,7},{6,4},{7,5},{8,10},{9,11},{10,... | collective-permute-start | bytes 393224 | tf_op jit(solution)/shard_map/ppermute | solution.py:19
  3.9 26.8 %collective-permute-start.1 = (bf16[64,1024]{1,0:T(8,128)(2,1)}, bf16[64,1024]{1,0:T(8,128)(2,1)S(1)}, u32[]{:S(2)}, u32[]{:S(2)}) collective-permute-start(bf16[64,1024]{1,0:T(8,128)(2,1)} %bitcast.30), channel_id=1, source_target_pairs={{0,1},{1,0},{2,3},{3,2},{4,5},{5,4},{6,7},{7,6},{8,9},{9,8},{10,11... | collective-permute-start | bytes 393224 | tf_op jit(solution)/shard_map/ppermute | solution.py:19
  4.2 69.9 %collective-permute-start.26 = (bf16[1024,1024]{1,0:T(8,128)(2,1)}, bf16[1024,1024]{1,0:T(8,128)(2,1)S(1)}, u32[]{:S(2)}, u32[]{:S(2)}) collective-permute-start(bf16[1024,1024]{1,0:T(8,128)(2,1)} %refs_0_.3), channel_id=1, source_target_pairs={{0,1},{1,0},{2,3},{3,2},{4,5},{5,4},{6,7},{7,6},{8,9},{9,8},{10,11... | collective-permute-start | bytes 6291464 | tf_op jit(solution)/shard_map/ppermute | solution.py:19
  5.9 1.2 %copy-start.2 = (bf16[1024,512]{1,0:T(8,128)(2,1)S(1)}, bf16[1024,512]{1,0:T(8,128)(2,1)}, u32[]{:S(2)}) copy-start(bf16[1024,512]{1,0:T(8,128)(2,1)} %cond_ref.1) | copy-start | bytes 3145732
  7.4 1.6 %copy-start = (bf16[1024,1024]{1,0:T(8,128)(2,1)S(1)}, bf16[1024,1024]{1,0:T(8,128)(2,1)}, u32[]{:S(2)}) copy-start(bf16[1024,1024]{1,0:T(8,128)(2,1)} %refs_0_.3) | copy-start | bytes 6291460
  9.9 8.3 %collective-permute-start.6 = (bf16[1024,128]{1,0:T(8,128)(2,1)S(1)}, bf16[1024,128]{1,0:T(8,128)(2,1)S(1)}, u32[]{:S(2)}, u32[]{:S(2)}) collective-permute-start(bf16[1024,128]{1,0:T(8,128)(2,1)S(1)} %get-tuple-element.28), channel_id=1, source_target_pairs={{0,2},{1,3},{2,0},{3,1},{4,6},{5,7},{6,4},{7,5},{8,10},{9,11},{10,... | collective-permute-start | bytes 786440 | tf_op jit(solution)/shard_map/ppermute | solution.py:19
  12.3 18.4 %collective-permute-start.2 = (bf16[1024,128]{1,0:T(8,128)(2,1)S(1)}, bf16[1024,128]{1,0:T(8,128)(2,1)S(1)}, u32[]{:S(2)}, u32[]{:S(2)}) collective-permute-start(bf16[1024,128]{1,0:T(8,128)(2,1)S(1)} %get-tuple-element.25.refs_0_), channel_id=1, source_target_pairs={{0,1},{1,0},{2,3},{3,2},{4,5},{5,4},{6,7},{7,6},{8,9},{9,8},{10,11... | collective-permute-start | bytes 786440 | tf_op jit(solution)/shard_map/ppermute | solution.py:19
  18.3 1.6 %collective-permute-start.7 = (bf16[64,1024]{1,0:T(8,128)(2,1)}, bf16[64,1024]{1,0:T(8,128)(2,1)S(1)}, u32[]{:S(2)}, u32[]{:S(2)}) collective-permute-start(bf16[64,1024]{1,0:T(8,128)(2,1)} %collective-permute-done.4), channel_id=1, source_target_pairs={{0,1},{1,0},{2,3},{3,2},{4,5},{5,4},{6,7},{7,6},{8,9},{9,8},{10,11... | collective-permute-start | bytes 393224 | tf_op jit(solution)/shard_map/ppermute | solution.py:19
  19.8 1.3 %collective-permute-start.8 = (bf16[48,1024]{1,0:T(8,128)(2,1)S(1)}, bf16[48,1024]{1,0:T(8,128)(2,1)S(1)}, u32[]{:S(2)}, u32[]{:S(2)}) collective-permute-start(bf16[48,1024]{1,0:T(8,128)(2,1)S(1)} %collective-permute-done.5.refs_5_), channel_id=1, source_target_pairs={{0,1},{1,0},{2,3},{3,2},{4,5},{5,4},{6,7},{7,6},{8,9},{9,8},{10,11... | collective-permute-start | bytes 294920 | tf_op jit(solution)/shard_map/ppermute | solution.py:19
  21.1 8.4 %collective-permute-start.12 = (bf16[1024,128]{1,0:T(8,128)(2,1)S(1)}, bf16[1024,128]{1,0:T(8,128)(2,1)S(1)}, u32[]{:S(2)}, u32[]{:S(2)}) collective-permute-start(bf16[1024,128]{1,0:T(8,128)(2,1)S(1)} %get-tuple-element.33), channel_id=1, source_target_pairs={{0,2},{1,3},{2,0},{3,1},{4,6},{5,7},{6,4},{7,5},{8,10},{9,11},{10,... | collective-permute-start | bytes 786440 | tf_op jit(solution)/shard_map/ppermute | solution.py:19
  23.6 7.4 %copy-start.3 = (bf16[1024,64]{0,1:T(8,128)(2,1)S(1)}, bf16[1024,64]{0,1:T(8,128)(2,1)}, u32[]{:S(2)}) copy-start(bf16[1024,64]{0,1:T(8,128)(2,1)} %param.8) | copy-start | bytes 393220
  23.7 7.4 %copy-start.4 = (bf16[1024,48]{0,1:T(8,128)(2,1)S(1)}, bf16[1024,48]{0,1:T(8,128)(2,1)}, u32[]{:S(2)}) copy-start(bf16[1024,48]{0,1:T(8,128)(2,1)} %param.6) | copy-start | bytes 294916
  29.5 1.5 %collective-permute-start.3 = (bf16[1024,128]{1,0:T(8,128)(2,1)S(1)}, bf16[1024,128]{1,0:T(8,128)(2,1)S(1)}, u32[]{:S(2)}, u32[]{:S(2)}) collective-permute-start(bf16[1024,128]{1,0:T(8,128)(2,1)S(1)} %get-tuple-element.26.refs_1_), channel_id=1, source_target_pairs={{0,1},{1,0},{2,3},{3,2},{4,5},{5,4},{6,7},{7,6},{8,9},{9,8},{10,11... | collective-permute-start | bytes 786440 | tf_op jit(solution)/shard_map/ppermute | solution.py:19
  30.1 4.0 %collective-permute-start.9 = (bf16[1024,128]{1,0:T(8,128)(2,1)S(1)}, bf16[1024,128]{1,0:T(8,128)(2,1)S(1)}, u32[]{:S(2)}, u32[]{:S(2)}) collective-permute-start(bf16[1024,128]{1,0:T(8,128)(2,1)S(1)} %collective-permute-done.6.refs_4_), channel_id=1, source_target_pairs={{0,1},{1,0},{2,3},{3,2},{4,5},{5,4},{6,7},{7,6},{8,9},{9,8},{10,11... | collective-permute-start | bytes 786440 | tf_op jit(solution)/shard_map/ppermute | solution.py:19
  30.6 5.9 %collective-permute-start.13 = (bf16[1024,128]{1,0:T(8,128)(2,1)S(1)}, bf16[1024,128]{1,0:T(8,128)(2,1)S(1)}, u32[]{:S(2)}, u32[]{:S(2)}) collective-permute-start(bf16[1024,128]{1,0:T(8,128)(2,1)S(1)} %collective-permute-done.12.refs_5_), channel_id=1, source_target_pairs={{0,1},{1,0},{2,3},{3,2},{4,5},{5,4},{6,7},{7,6},{8,9},{9,8},{10,11... | collective-permute-start | bytes 786440 | tf_op jit(solution)/shard_map/ppermute | solution.py:19
  34.7 6.0 %collective-permute-start.10 = (bf16[384,128]{1,0:T(8,128)(2,1)S(1)}, bf16[384,128]{1,0:T(8,128)(2,1)S(1)}, u32[]{:S(2)}, u32[]{:S(2)}) collective-permute-start(bf16[384,128]{1,0:T(8,128)(2,1)S(1)} %get-tuple-element.53), channel_id=1, source_target_pairs={{0,4},{1,5},{2,6},{3,7},{4,0},{5,1},{6,2},{7,3},{8,12},{9,13},{10,... | collective-permute-start | bytes 294920 | tf_op jit(solution)/shard_map/ppermute | solution.py:19
  37.2 6.4 %collective-permute-start.14 = (bf16[384,128]{1,0:T(8,128)(2,1)S(1)}, bf16[384,128]{1,0:T(8,128)(2,1)S(1)}, u32[]{:S(2)}, u32[]{:S(2)}) collective-permute-start(bf16[384,128]{1,0:T(8,128)(2,1)S(1)} %get-tuple-element.51), channel_id=1, source_target_pairs={{0,4},{1,5},{2,6},{3,7},{4,0},{5,1},{6,2},{7,3},{8,12},{9,13},{10,... | collective-permute-start | bytes 294920 | tf_op jit(solution)/shard_map/ppermute | solution.py:19
  37.5 11.2 %collective-permute-start.16 = (bf16[384,128]{1,0:T(8,128)(2,1)S(1)}, bf16[384,128]{1,0:T(8,128)(2,1)S(1)}, u32[]{:S(2)}, u32[]{:S(2)}) collective-permute-start(bf16[384,128]{1,0:T(8,128)(2,1)S(1)} %get-tuple-element.52), channel_id=1, source_target_pairs={{0,4},{1,5},{2,6},{3,7},{4,0},{5,1},{6,2},{7,3},{8,12},{9,13},{10,... | collective-permute-start | bytes 294920 | tf_op jit(solution)/shard_map/ppermute | solution.py:19
  39.3 10.8 %collective-permute-start.18 = (bf16[384,128]{1,0:T(8,128)(2,1)S(1)}, bf16[384,128]{1,0:T(8,128)(2,1)S(1)}, u32[]{:S(2)}, u32[]{:S(2)}) collective-permute-start(bf16[384,128]{1,0:T(8,128)(2,1)S(1)} %get-tuple-element.50), channel_id=1, source_target_pairs={{0,4},{1,5},{2,6},{3,7},{4,0},{5,1},{6,2},{7,3},{8,12},{9,13},{10,... | collective-permute-start | bytes 294920 | tf_op jit(solution)/shard_map/ppermute | solution.py:19
  40.8 11.7 %collective-permute-start.11 = (bf16[384,128]{1,0:T(8,128)(2,1)S(1)}, bf16[384,128]{1,0:T(8,128)(2,1)S(1)}, u32[]{:S(2)}, u32[]{:S(2)}) collective-permute-start(bf16[384,128]{1,0:T(8,128)(2,1)S(1)} %get-tuple-element.31), channel_id=1, source_target_pairs={{0,8},{1,9},{2,10},{3,11},{4,12},{5,13},{6,14},{7,15},{8,0},{9,1},... | collective-permute-start | bytes 294920 | tf_op jit(solution)/shard_map/ppermute | solution.py:19
  43.7 14.6 %collective-permute-start.15 = (bf16[384,128]{1,0:T(8,128)(2,1)S(1)}, bf16[384,128]{1,0:T(8,128)(2,1)S(1)}, u32[]{:S(2)}, u32[]{:S(2)}) collective-permute-start(bf16[384,128]{1,0:T(8,128)(2,1)S(1)} %get-tuple-element.36), channel_id=1, source_target_pairs={{0,8},{1,9},{2,10},{3,11},{4,12},{5,13},{6,14},{7,15},{8,0},{9,1},... | collective-permute-start | bytes 294920 | tf_op jit(solution)/shard_map/ppermute | solution.py:19
  48.7 11.5 %collective-permute-start.17 = (bf16[384,128]{1,0:T(8,128)(2,1)S(1)}, bf16[384,128]{1,0:T(8,128)(2,1)S(1)}, u32[]{:S(2)}, u32[]{:S(2)}) collective-permute-start(bf16[384,128]{1,0:T(8,128)(2,1)S(1)} %get-tuple-element.38), channel_id=1, source_target_pairs={{0,8},{1,9},{2,10},{3,11},{4,12},{5,13},{6,14},{7,15},{8,0},{9,1},... | collective-permute-start | bytes 294920 | tf_op jit(solution)/shard_map/ppermute | solution.py:19
  50.1 11.1 %collective-permute-start.19 = (bf16[384,128]{1,0:T(8,128)(2,1)S(1)}, bf16[384,128]{1,0:T(8,128)(2,1)S(1)}, u32[]{:S(2)}, u32[]{:S(2)}) collective-permute-start(bf16[384,128]{1,0:T(8,128)(2,1)S(1)} %get-tuple-element.40), channel_id=1, source_target_pairs={{0,8},{1,9},{2,10},{3,11},{4,12},{5,13},{6,14},{7,15},{8,0},{9,1},... | collective-permute-start | bytes 294920 | tf_op jit(solution)/shard_map/ppermute | solution.py:19
  52.4 14.7 %collective-permute-start.21 = (bf16[384,128]{1,0:T(8,128)(2,1)S(1)}, bf16[384,128]{1,0:T(8,128)(2,1)S(1)}, u32[]{:S(2)}, u32[]{:S(2)}) collective-permute-start(bf16[384,128]{1,0:T(8,128)(2,1)S(1)} %shard_map.80.refs_0_), channel_id=1, source_target_pairs={{0,4},{1,5},{2,6},{3,7},{4,0},{5,1},{6,2},{7,3},{8,12},{9,13},{10,... | collective-permute-start | bytes 294920 | tf_op jit(solution)/shard_map/ppermute | solution.py:19
  58.3 10.7 %collective-permute-start.22 = (bf16[384,128]{1,0:T(8,128)(2,1)S(1)}, bf16[384,128]{1,0:T(8,128)(2,1)S(1)}, u32[]{:S(2)}, u32[]{:S(2)}) collective-permute-start(bf16[384,128]{1,0:T(8,128)(2,1)S(1)} %shard_map.82.refs_1_), channel_id=1, source_target_pairs={{0,4},{1,5},{2,6},{3,7},{4,0},{5,1},{6,2},{7,3},{8,12},{9,13},{10,... | collective-permute-start | bytes 294920 | tf_op jit(solution)/shard_map/ppermute | solution.py:19
  60.2 8.8 %collective-permute-start.23 = (bf16[384,128]{1,0:T(8,128)(2,1)S(1)}, bf16[384,128]{1,0:T(8,128)(2,1)S(1)}, u32[]{:S(2)}, u32[]{:S(2)}) collective-permute-start(bf16[384,128]{1,0:T(8,128)(2,1)S(1)} %shard_map.84.refs_2_), channel_id=1, source_target_pairs={{0,4},{1,5},{2,6},{3,7},{4,0},{5,1},{6,2},{7,3},{8,12},{9,13},{10,... | collective-permute-start | bytes 294920 | tf_op jit(solution)/shard_map/ppermute | solution.py:19
  61.3 7.7 %collective-permute-start.24 = (bf16[384,128]{1,0:T(8,128)(2,1)S(1)}, bf16[384,128]{1,0:T(8,128)(2,1)S(1)}, u32[]{:S(2)}, u32[]{:S(2)}) collective-permute-start(bf16[384,128]{1,0:T(8,128)(2,1)S(1)} %shard_map.86.refs_3_), channel_id=1, source_target_pairs={{0,4},{1,5},{2,6},{3,7},{4,0},{5,1},{6,2},{7,3},{8,12},{9,13},{10,... | collective-permute-start | bytes 294920 | tf_op jit(solution)/shard_map/ppermute | solution.py:19
  67.2 7.6 %collective-permute-start.20 = (f32[16,2048]{1,0:T(8,128)S(1)}, f32[16,2048]{1,0:T(8,128)S(1)}, u32[]{:S(2)}, u32[]{:S(2)}) collective-permute-start(f32[16,2048]{1,0:T(8,128)S(1)} %shard_map.89), channel_id=1, source_target_pairs={{0,2},{1,3},{2,0},{3,1},{4,6},{5,7},{6,4},{7,5},{8,10},{9,11},{10,... | collective-permute-start | bytes 393224 | tf_op jit(solution)/shard_map/ppermute | solution.py:19
  71.3 5.0 %collective-permute-start.25 = (f32[16,2048]{1,0:T(8,128)S(1)}, f32[16,2048]{1,0:T(8,128)S(1)}, u32[]{:S(2)}, u32[]{:S(2)}) collective-permute-start(f32[16,2048]{1,0:T(8,128)S(1)} %shard_map.91), channel_id=1, source_target_pairs={{0,2},{1,3},{2,0},{3,1},{4,6},{5,7},{6,4},{7,5},{8,10},{9,11},{10,... | collective-permute-start | bytes 393224 | tf_op jit(solution)/shard_map/ppermute | solution.py:19
  76.3 18.6 %copy-start.1 = (bf16[1024,1024]{1,0:T(8,128)(2,1)S(1)}, bf16[1024,1024]{1,0:T(8,128)(2,1)}, u32[]{:S(2)}) copy-start(bf16[1024,1024]{1,0:T(8,128)(2,1)} %refs_0_.3) | copy-start | bytes 6291460
  78.2 5.0 %collective-permute-start.27 = (f32[32,1024]{1,0:T(8,128)S(1)}, f32[32,1024]{1,0:T(8,128)S(1)}, u32[]{:S(2)}, u32[]{:S(2)}) collective-permute-start(f32[32,1024]{1,0:T(8,128)S(1)} %get-tuple-element.42), channel_id=1, source_target_pairs={{0,2},{1,3},{2,0},{3,1},{4,6},{5,7},{6,4},{7,5},{8,10},{9,11},{10,... | collective-permute-start | bytes 393224 | tf_op jit(solution)/shard_map/ppermute | solution.py:19
  83.2 5.7 %collective-permute-start.28 = (f32[32,1024]{1,0:T(8,128)S(1)}, f32[32,1024]{1,0:T(8,128)S(1)}, u32[]{:S(2)}, u32[]{:S(2)}) collective-permute-start(f32[32,1024]{1,0:T(8,128)S(1)} %add.79), channel_id=1, source_target_pairs={{0,4},{1,5},{2,6},{3,7},{4,0},{5,1},{6,2},{7,3},{8,12},{9,13},{10,... | collective-permute-start | bytes 393224 | tf_op jit(solution)/shard_map/ppermute | solution.py:19
  89.0 5.9 %collective-permute-start.29 = (bf16[32,1024]{1,0:T(8,128)(2,1)S(1)}, bf16[32,1024]{1,0:T(8,128)(2,1)S(1)}, u32[]{:S(2)}, u32[]{:S(2)}) collective-permute-start(bf16[32,1024]{1,0:T(8,128)(2,1)S(1)} %get-tuple-element.48), channel_id=1, source_target_pairs={{0,8},{1,9},{2,10},{3,11},{4,12},{5,13},{6,14},{7,15},{8,0},{9,1},... | collective-permute-start | bytes 196616 | tf_op jit(solution)/shard_map/ppermute | solution.py:19
  96.9 5.4 %collective-permute-start.33 = (f32[1,32]{1,0:T(1,128)S(1)}, f32[1,32]{1,0:T(1,128)S(1)}, u32[]{:S(2)}, u32[]{:S(2)}) collective-permute-start(f32[1,32]{1,0:T(1,128)S(1)} %get-tuple-element.45), channel_id=1, source_target_pairs={{0,12},{1,13},{2,14},{3,15},{4,8},{5,9},{6,10},{7,11},{8,4},{9,5},... | collective-permute-start | bytes 392 | tf_op jit(solution)/shard_map/ppermute | solution.py:19
  99.5 3.6 %collective-permute-start.31 = (f32[1,32]{1,0:T(1,128)S(1)}, f32[1,32]{1,0:T(1,128)S(1)}, u32[]{:S(2)}, u32[]{:S(2)}) collective-permute-start(f32[1,32]{1,0:T(1,128)S(1)} %get-tuple-element.45), channel_id=1, source_target_pairs={{0,4},{1,5},{2,6},{3,7},{4,0},{5,1},{6,2},{7,3},{8,12},{9,13},{10,... | collective-permute-start | bytes 392 | tf_op jit(solution)/shard_map/ppermute | solution.py:19
  99.5 4.5 %collective-permute-start.32 = (f32[1,32]{1,0:T(1,128)S(1)}, f32[1,32]{1,0:T(1,128)S(1)}, u32[]{:S(2)}, u32[]{:S(2)}) collective-permute-start(f32[1,32]{1,0:T(1,128)S(1)} %get-tuple-element.45), channel_id=1, source_target_pairs={{0,8},{1,9},{2,10},{3,11},{4,12},{5,13},{6,14},{7,15},{8,0},{9,1},... | collective-permute-start | bytes 392 | tf_op jit(solution)/shard_map/ppermute | solution.py:19
  101.4 6.9 %collective-permute-start.30 = (f32[32,64]{1,0:T(8,128)S(1)}, f32[32,64]{1,0:T(8,128)S(1)}, u32[]{:S(2)}, u32[]{:S(2)}) collective-permute-start(f32[32,64]{1,0:T(8,128)S(1)} %get-tuple-element.44), channel_id=1, source_target_pairs={{0,1},{1,0},{2,3},{3,2},{4,5},{5,4},{6,7},{7,6},{8,9},{9,8},{10,11... | collective-permute-start | bytes 24584 | tf_op jit(solution)/shard_map/ppermute | solution.py:19
  101.4 8.1 %collective-permute-start.37 = (f32[32,1024]{1,0:T(8,128)S(1)}, f32[32,1024]{1,0:T(8,128)S(1)}, u32[]{:S(2)}, u32[]{:S(2)}) collective-permute-start(f32[32,1024]{1,0:T(8,128)S(1)} %get-tuple-element.47), channel_id=1, source_target_pairs={{0,1},{1,0},{2,3},{3,2},{4,5},{5,4},{6,7},{7,6},{8,9},{9,8},{10,11... | collective-permute-start | bytes 393224 | tf_op jit(solution)/shard_map/ppermute | solution.py:19
  104.0 3.6 %collective-permute-start.34 = (f32[1,32]{1,0:T(1,128)S(1)}, f32[1,32]{1,0:T(1,128)S(1)}, u32[]{:S(2)}, u32[]{:S(2)}) collective-permute-start(f32[1,32]{1,0:T(1,128)S(1)} %add_add_fusion), channel_id=1, source_target_pairs={{0,2},{1,3},{2,0},{3,1},{4,6},{5,7},{6,4},{7,5},{8,10},{9,11},{10,... | collective-permute-start | bytes 392 | tf_op jit(solution)/shard_map/ppermute | solution.py:19
  105.2 2.3 %collective-permute-start.35 = (f32[1,32]{1,0:T(1,128)S(1)}, f32[1,32]{1,0:T(1,128)S(1)}, u32[]{:S(2)}, u32[]{:S(2)}) collective-permute-start(f32[1,32]{1,0:T(1,128)S(1)} %add_add_fusion), channel_id=1, source_target_pairs={{0,1},{1,0},{2,3},{3,2},{4,5},{5,4},{6,7},{7,6},{8,9},{9,8},{10,11... | collective-permute-start | bytes 392 | tf_op jit(solution)/shard_map/ppermute | solution.py:19
  105.2 3.0 %collective-permute-start.36 = (f32[1,32]{1,0:T(1,128)S(1)}, f32[1,32]{1,0:T(1,128)S(1)}, u32[]{:S(2)}, u32[]{:S(2)}) collective-permute-start(f32[1,32]{1,0:T(1,128)S(1)} %add_add_fusion), channel_id=1, source_target_pairs={{0,3},{1,2},{2,1},{3,0},{4,7},{5,6},{6,5},{7,4},{8,11},{9,10},{10,... | collective-permute-start | bytes 392 | tf_op jit(solution)/shard_map/ppermute | solution.py:19

commit v5 on v4

--- a/solution.py
+++ b/solution.py
@@ -90,13 +90,14 @@
     mask = sum((me & bit) // bit << (len(spread) - 1 - level) for level, bit in enumerate(spread))
     marks = jnp.stack([jnp.int32(core), jnp.int32(mask), jnp.int32(me >> 1)] + [group[0] for group in groups])
     own = [cond_all[place][part] for place in (0, 1) for part in parts]
-    own_terms = pl.pallas_call(
+    *own_terms, vals[0], vals[1] = pl.pallas_call(
         functools.partial(own_kernel, CHUNKS),
         out_shape=[
             jax.ShapeDtypeStruct((group[1] * val_count, c_part), F32) for group in groups for part in parts
-        ],
+        ]
+        + [jax.ShapeDtypeStruct(vals[0].shape, BF16)] * 2,
         in_specs=[pl.BlockSpec(memory_space=pltpu.SMEM)] + [pl.BlockSpec(memory_space=pltpu.VMEM)] * (4 + len(own)),
-        out_specs=[pl.BlockSpec(memory_space=pltpu.VMEM)] * (len(groups) * CHUNKS),
+        out_specs=[pl.BlockSpec(memory_space=pltpu.VMEM)] * (len(groups) * CHUNKS + 2),
         scratch_shapes=[
             pltpu.VMEM((groups[0][1] * val_count, 2 * rows), BF16),
             pltpu.VMEM((2 * rows, c_half), BF16),
@@ -209,7 +210,8 @@
 
 
 def own_kernel(chunks, marks_ref, val0, val1, pot0, pot1, *refs):
-    conds, outs = refs[: 2 * chunks], refs[2 * chunks : -3]
+    conds, outs, kept = refs[: 2 * chunks], refs[2 * chunks : -5], refs[-5:-3]
+    kept[0][...], kept[1][...] = val0[...], val1[...]
     pairs, right, wide = refs[-3:]
     val_count, rows = val0.shape
     width = conds[0].shape[1]

time: 111 us -> 111 us (level)
  no operation moved by 1% of the time
where the time goes in v5:
time: 111 us
  waiting for transfers between devices  41.7 us (38%)
  starting transfers between devices  37.3 us (34%)
  Pallas kernels  20.6 us (19%)
  matrix products  4.63 us (4%)
  local copies, waits for them, and re-layouts  4.49 us (4%)
  other arithmetic  1.22 us (1%)
    ppermute x38, waiting for transfers between devices, swap(): return lax.ppermute(block, 'grid', [(i, i ^ bit) for i in range(count)])  41.7 us
    ppermute x38, starting transfers between devices, swap(): return lax.ppermute(block, 'grid', [(i, i ^ bit) for i in range(count)])  37.3 us
    pallas_call x15, Pallas kernels, in_vmem(): pl.pallas_call(kernel, out_shape=out_shape, in_specs=[pl.BlockSpec(memory...  11.5 us
    pallas_call x4, Pallas kernels, with_marks(): pl.pallas_call(kernel, out_shape=out_shape, in_specs=[pl.BlockSpec(memory...  6.4 us
    dot_general x8, matrix products, contract(): return jnp.dot(left, right, preferred_element_type=F32)  4.63 us
    unnamed x10, local copies, waits for them, and re-layouts  2.83 us
    pallas_call x1, Pallas kernels, body(): pl.pallas_call(functools.partial(own_kernel, CHUNKS), out_shape=[jax.Shap...  2.49 us
  transfers between devices with their start and end apart: 38, of which 20 were waited for; matrix products, arithmetic and copies ran while one was open for 7% of the time, Pallas kernels for 14%

profile of v5, /device:TPU:0, one launch (start us, length us, event | category | flops | bytes accessed | tf_op | source)
XLA Modules:
  0.0 110.8 jit_solution(12160569416540817257)
XLA Ops:
  0.6 3.1 %collective-permute-start.5 = (bf16[48,1024]{1,0:T(8,128)(2,1)}, bf16[48,1024]{1,0:T(8,128)(2,1)S(1)}, u32[]{:S(2)}, u32[]{:S(2)}) collective-permute-start(bf16[48,1024]{1,0:T(8,128)(2,1)} %bitcast.32), channel_id=1, source_target_pairs={{0,2},{1,3},{2,0},{3,1},{4,6},{5,7},{6,4},{7,5},{8,10},{9,11},{10,... | collective-permute-start | bytes 294920 | tf_op jit(solution)/shard_map/ppermute | solution.py:19
  4.4 0.8 dynamic_slice.19
  5.1 0.7 subtract_divide_fusion
  5.9 1.2 %copy-done.2 = bf16[1024,512]{1,0:T(8,128)(2,1)S(1)} copy-done((bf16[1024,512]{1,0:T(8,128)(2,1)S(1)}, bf16[1024,512]{1,0:T(8,128)(2,1)}, u32[]{:S(2)}) %copy-start.2) | copy-done | bytes 1048600
  7.4 1.6 %copy-done = bf16[1024,1024]{1,0:T(8,128)(2,1)S(1)} copy-done((bf16[1024,1024]{1,0:T(8,128)(2,1)S(1)}, bf16[1024,1024]{1,0:T(8,128)(2,1)}, u32[]{:S(2)}) %copy-start) | copy-done | bytes 2097176
  9.0 0.6 shard_map.92.refs_4_
  9.9 1.6 %collective-permute-start.6 = (bf16[1024,128]{1,0:T(8,128)(2,1)S(1)}, bf16[1024,128]{1,0:T(8,128)(2,1)S(1)}, u32[]{:S(2)}, u32[]{:S(2)}) collective-permute-start(bf16[1024,128]{1,0:T(8,128)(2,1)S(1)} %get-tuple-element.30), channel_id=1, source_target_pairs={{0,2},{1,3},{2,0},{3,1},{4,6},{5,7},{6,4},{7,5},{8,10},{9,11},{10,... | collective-permute-start | bytes 786440 | tf_op jit(solution)/shard_map/ppermute | solution.py:19
  11.6 0.8 constant_dynamic-slice_fusion.1
  12.6 5.6 %collective-permute-done.6.refs_4_ = bf16[1024,128]{1,0:T(8,128)(2,1)S(1)} collective-permute-done((bf16[1024,128]{1,0:T(8,128)(2,1)S(1)}, bf16[1024,128]{1,0:T(8,128)(2,1)S(1)}, u32[]{:S(2)}, u32[]{:S(2)}) %collective-permute-start.6) | collective-permute-done | bytes 262176 | tf_op jit(solution)/shard_map/ppermute | solution.py:19
  18.3 0.6 fusion.6
  18.8 1.0 collective-permute-done.7
  20.0 1.1 %collective-permute-done.8.refs_6_ = bf16[48,1024]{1,0:T(8,128)(2,1)S(1)} collective-permute-done((bf16[48,1024]{1,0:T(8,128)(2,1)S(1)}, bf16[48,1024]{1,0:T(8,128)(2,1)S(1)}, u32[]{:S(2)}, u32[]{:S(2)}) %collective-permute-start.8) | collective-permute-done | bytes 98336 | tf_op jit(solution)/shard_map/ppermute | solution.py:19
  21.1 1.7 %collective-permute-start.12 = (bf16[1024,128]{1,0:T(8,128)(2,1)S(1)}, bf16[1024,128]{1,0:T(8,128)(2,1)S(1)}, u32[]{:S(2)}, u32[]{:S(2)}) collective-permute-start(bf16[1024,128]{1,0:T(8,128)(2,1)S(1)} %get-tuple-element.35), channel_id=1, source_target_pairs={{0,2},{1,3},{2,0},{3,1},{4,6},{5,7},{6,4},{7,5},{8,10},{9,11},{10,... | collective-permute-start | bytes 786440 | tf_op jit(solution)/shard_map/ppermute | solution.py:19
  23.1 0.6 fusion.7
  23.7 5.8 %collective-permute-done.12.refs_5_ = bf16[1024,128]{1,0:T(8,128)(2,1)S(1)} collective-permute-done((bf16[1024,128]{1,0:T(8,128)(2,1)S(1)}, bf16[1024,128]{1,0:T(8,128)(2,1)S(1)}, u32[]{:S(2)}, u32[]{:S(2)}) %collective-permute-start.12) | collective-permute-done | bytes 262176 | tf_op jit(solution)/shard_map/ppermute | solution.py:19
  29.5 0.6 fusion.8
  30.1 0.6 collective-permute-start.9
  31.0 2.5 %shard_map.78 = (f32[768,128]{1,0:T(8,128)S(1)}, f32[768,128]{1,0:T(8,128)S(1)}, f32[768,128]{1,0:T(8,128)S(1)}, f32[768,128]{1,0:T(8,128)S(1)}, bf16[48,1024]{1...) custom-call(s32[5]{0:T(128)S(1)} %stack.23.marks_ref, bf16[48,1024]{1,0:T(8,128)(2,1)S(1)} %bitcast.34, ...), custom_call_target="tpu_custom_call" | custom-call | flops 1610612736 | bytes 4194304 | tf_op jit(solution)/shard_map/pallas_call | solution.py:93
  33.5 0.6 fusion.9
  34.1 0.6 fusion
  34.7 1.9 %collective-permute-start.10 = (bf16[384,128]{1,0:T(8,128)(2,1)S(1)}, bf16[384,128]{1,0:T(8,128)(2,1)S(1)}, u32[]{:S(2)}, u32[]{:S(2)}) collective-permute-start(bf16[384,128]{1,0:T(8,128)(2,1)S(1)} %get-tuple-element.57), channel_id=1, source_target_pairs={{0,4},{1,5},{2,6},{3,7},{4,0},{5,1},{6,2},{7,3},{8,12},{9,13},{10,... | collective-permute-start | bytes 294920 | tf_op jit(solution)/shard_map/ppermute | solution.py:19
  36.6 0.6 fusion.1
  37.5 1.8 %collective-permute-start.16 = (bf16[384,128]{1,0:T(8,128)(2,1)S(1)}, bf16[384,128]{1,0:T(8,128)(2,1)S(1)}, u32[]{:S(2)}, u32[]{:S(2)}) collective-permute-start(bf16[384,128]{1,0:T(8,128)(2,1)S(1)} %get-tuple-element.56), channel_id=1, source_target_pairs={{0,4},{1,5},{2,6},{3,7},{4,0},{5,1},{6,2},{7,3},{8,12},{9,13},{10,... | collective-permute-start | bytes 294920 | tf_op jit(solution)/shard_map/ppermute | solution.py:19
  39.5 0.6 convolution_add_fusion.3.block_ref
  40.1 0.6 convolution_add_fusion.1.block_ref
  40.8 2.9 %collective-permute-start.11 = (bf16[384,128]{1,0:T(8,128)(2,1)S(1)}, bf16[384,128]{1,0:T(8,128)(2,1)S(1)}, u32[]{:S(2)}, u32[]{:S(2)}) collective-permute-start(bf16[384,128]{1,0:T(8,128)(2,1)S(1)} %get-tuple-element.33), channel_id=1, source_target_pairs={{0,8},{1,9},{2,10},{3,11},{4,12},{5,13},{6,14},{7,15},{8,0},{9,1},... | collective-permute-start | bytes 294920 | tf_op jit(solution)/shard_map/ppermute | solution.py:19
  43.7 2.0 %collective-permute-start.15 = (bf16[384,128]{1,0:T(8,128)(2,1)S(1)}, bf16[384,128]{1,0:T(8,128)(2,1)S(1)}, u32[]{:S(2)}, u32[]{:S(2)}) collective-permute-start(bf16[384,128]{1,0:T(8,128)(2,1)S(1)} %get-tuple-element.38), channel_id=1, source_target_pairs={{0,8},{1,9},{2,10},{3,11},{4,12},{5,13},{6,14},{7,15},{8,0},{9,1},... | collective-permute-start | bytes 294920 | tf_op jit(solution)/shard_map/ppermute | solution.py:19
  45.6 3.1 %collective-permute-done.16.refs_0_ = bf16[384,128]{1,0:T(8,128)(2,1)S(1)} collective-permute-done((bf16[384,128]{1,0:T(8,128)(2,1)S(1)}, bf16[384,128]{1,0:T(8,128)(2,1)S(1)}, u32[]{:S(2)}, u32[]{:S(2)}) %collective-permute-start.16) | collective-permute-done | bytes 98336 | tf_op jit(solution)/shard_map/ppermute | solution.py:19
  48.8 1.3 %collective-permute-done.18.refs_0_ = bf16[384,128]{1,0:T(8,128)(2,1)S(1)} collective-permute-done((bf16[384,128]{1,0:T(8,128)(2,1)S(1)}, bf16[384,128]{1,0:T(8,128)(2,1)S(1)}, u32[]{:S(2)}, u32[]{:S(2)}) %collective-permute-start.18) | collective-permute-done | bytes 98336 | tf_op jit(solution)/shard_map/ppermute | solution.py:19
  50.1 1.7 %collective-permute-start.19 = (bf16[384,128]{1,0:T(8,128)(2,1)S(1)}, bf16[384,128]{1,0:T(8,128)(2,1)S(1)}, u32[]{:S(2)}, u32[]{:S(2)}) collective-permute-start(bf16[384,128]{1,0:T(8,128)(2,1)S(1)} %get-tuple-element.42), channel_id=1, source_target_pairs={{0,8},{1,9},{2,10},{3,11},{4,12},{5,13},{6,14},{7,15},{8,0},{9,1},... | collective-permute-start | bytes 294920 | tf_op jit(solution)/shard_map/ppermute | solution.py:19
  51.8 0.6 shard_map.87.refs_4_
  52.5 4.1 %collective-permute-start.21 = (bf16[384,128]{1,0:T(8,128)(2,1)S(1)}, bf16[384,128]{1,0:T(8,128)(2,1)S(1)}, u32[]{:S(2)}, u32[]{:S(2)}) collective-permute-start(bf16[384,128]{1,0:T(8,128)(2,1)S(1)} %shard_map.80.refs_0_), channel_id=1, source_target_pairs={{0,4},{1,5},{2,6},{3,7},{4,0},{5,1},{6,2},{7,3},{8,12},{9,13},{10,... | collective-permute-start | bytes 294920 | tf_op jit(solution)/shard_map/ppermute | solution.py:19
  56.6 1.7 %collective-permute-done.15.other_ref = bf16[384,128]{1,0:T(8,128)(2,1)S(1)} collective-permute-done((bf16[384,128]{1,0:T(8,128)(2,1)S(1)}, bf16[384,128]{1,0:T(8,128)(2,1)S(1)}, u32[]{:S(2)}, u32[]{:S(2)}) %collective-permute-start.15) | collective-permute-done | bytes 98336 | tf_op jit(solution)/shard_map/ppermute | solution.py:19
  58.3 0.6 collective-permute-start.22
  58.8 1.3 %collective-permute-done.17.other_ref = bf16[384,128]{1,0:T(8,128)(2,1)S(1)} collective-permute-done((bf16[384,128]{1,0:T(8,128)(2,1)S(1)}, bf16[384,128]{1,0:T(8,128)(2,1)S(1)}, u32[]{:S(2)}, u32[]{:S(2)}) %collective-permute-start.17) | collective-permute-done | bytes 98336 | tf_op jit(solution)/shard_map/ppermute | solution.py:19
  60.5 0.7 collective-permute-done.19.other_ref
  61.3 1.1 %collective-permute-start.24 = (bf16[384,128]{1,0:T(8,128)(2,1)S(1)}, bf16[384,128]{1,0:T(8,128)(2,1)S(1)}, u32[]{:S(2)}, u32[]{:S(2)}) collective-permute-start(bf16[384,128]{1,0:T(8,128)(2,1)S(1)} %shard_map.86.refs_3_), channel_id=1, source_target_pairs={{0,4},{1,5},{2,6},{3,7},{4,0},{5,1},{6,2},{7,3},{8,12},{9,13},{10,... | collective-permute-start | bytes 294920 | tf_op jit(solution)/shard_map/ppermute | solution.py:19
  62.4 2.5 %shard_map.88.refs_0_ = f32[16,2048]{1,0:T(8,128)S(1)} custom-call(bf16[384,128]{1,0:T(8,128)(2,1)S(1)} %shard_map.80.refs_0_, bf16[384,128]{1,0:T(8,128)(2,1)S(1)} %shard_map.82.refs_1_, bf16[384,128]{1,0:T(8,128)(2,1)S(1)} %shard_map.84.refs_2_, bf16[384,128]{1,0:T(8,128)(2,1)S(1)} %shard_map.86.refs_3_, bf16[256,4096]{1,0:T(8,128)(2,1)S(1)} %shard_map.87.refs_4_, ...), custom_call_target="tpu_custom_call" | custom-call | flops 1000000000 | bytes 4194304 | tf_op jit(solution)/shard_map/pallas_call | solution.py:237
  64.9 2.3 %shard_map.89 = f32[16,2048]{1,0:T(8,128)S(1)} custom-call(bf16[384,128]{1,0:T(8,128)(2,1)S(1)} %shard_map.80.refs_0_, bf16[384,128]{1,0:T(8,128)(2,1)S(1)} %shard_map.82.refs_1_, bf16[384,128]{1,0:T(8,128)(2,1)S(1)} %shard_map.84.refs_2_, bf16[384,128]{1,0:T(8,128)(2,1)S(1)} %shard_map.86.refs_3_, bf16[256,4096]{1,0:T(8,128)(2,1)S(1)} %shard_map.87.refs_4_, ...), custom_call_target="tpu_custom_call" | custom-call | flops 1000000000 | bytes 4194304 | tf_op jit(solution)/shard_map/pallas_call | solution.py:237
  67.2 1.8 %collective-permute-start.20 = (f32[16,2048]{1,0:T(8,128)S(1)}, f32[16,2048]{1,0:T(8,128)S(1)}, u32[]{:S(2)}, u32[]{:S(2)}) collective-permute-start(f32[16,2048]{1,0:T(8,128)S(1)} %shard_map.89), channel_id=1, source_target_pairs={{0,2},{1,3},{2,0},{3,1},{4,6},{5,7},{6,4},{7,5},{8,10},{9,11},{10,... | collective-permute-start | bytes 393224 | tf_op jit(solution)/shard_map/ppermute | solution.py:19
  69.0 2.3 %shard_map.91 = f32[16,2048]{1,0:T(8,128)S(1)} custom-call(bf16[384,128]{1,0:T(8,128)(2,1)S(1)} %collective-permute-done.21.refs_0_, bf16[384,128]{1,0:T(8,128)(2,1)S(1)} %collective-permute-done.22.refs_1_, bf16[384,128]{1,0:T(8,128)(2,1)S(1)} %collective-permute-done.23.refs_2_, bf16[384,128]{1,0:T(8,128)(2,1)S(1)} %collective-permute-done.24.refs_3_, ...), custom_call_target="tpu_custom_call" | custom-call | flops 1000000000 | bytes 4194304 | tf_op jit(solution)/shard_map/pallas_call | solution.py:237
  71.3 0.4 collective-permute-start.25
  71.7 2.3 %shard_map.90.refs_2_ = f32[16,2048]{1,0:T(8,128)S(1)} custom-call(bf16[384,128]{1,0:T(8,128)(2,1)S(1)} %collective-permute-done.21.refs_0_, bf16[384,128]{1,0:T(8,128)(2,1)S(1)} %collective-permute-done.22.refs_1_, bf16[384,128]{1,0:T(8,128)(2,1)S(1)} %collective-permute-done.23.refs_2_, bf16[384,128]{1,0:T(8,128)(2,1)S(1)} %collective-permute-done.24.refs_3_, ...), custom_call_target="tpu_custom_call" | custom-call | flops 1000000000 | bytes 4194304 | tf_op jit(solution)/shard_map/pallas_call | solution.py:237
  74.0 0.6 shard_map.93.refs_5_
  74.7 1.6 %collective-permute-done.25.refs_3_ = f32[16,2048]{1,0:T(8,128)S(1)} collective-permute-done((f32[16,2048]{1,0:T(8,128)S(1)}, f32[16,2048]{1,0:T(8,128)S(1)}, u32[]{:S(2)}, u32[]{:S(2)}) %collective-permute-start.25) | collective-permute-done | bytes 131104 | tf_op jit(solution)/shard_map/ppermute | solution.py:19
  76.3 1.8 %shard_map.94 = (f32[32,2048]{1,0:T(8,128)S(1)}, f32[32,1024]{1,0:T(8,128)S(1)}) custom-call(s32[5]{0:T(128)S(1)} %stack.23.marks_ref, f32[16,2048]{1,0:T(8,128)S(1)} %shard_map.88.refs_0_, f32[16,2048]{1,0:T(8,128)S(1)} %collective-permute-done.20.refs_1_, f32[16,2048]{1,0:T(8,128)S(1)} %shard_map.90.refs_2_, ...), custom_call_target="tpu_custom_call" | custom-call | flops 1000000000 | bytes 4194304 | tf_op jit(solution)/shard_map/pallas_call | solution.py:290
  78.6 4.6 %collective-permute-done.27 = f32[32,1024]{1,0:T(8,128)S(1)} collective-permute-done((f32[32,1024]{1,0:T(8,128)S(1)}, f32[32,1024]{1,0:T(8,128)S(1)}, u32[]{:S(2)}, u32[]{:S(2)}) %collective-permute-start.27) | collective-permute-done | bytes 131104 | tf_op jit(solution)/shard_map/ppermute | solution.py:19
  83.2 1.0 collective-permute-start.28
  84.2 4.7 %collective-permute-done.28 = f32[32,1024]{1,0:T(8,128)S(1)} collective-permute-done((f32[32,1024]{1,0:T(8,128)S(1)}, f32[32,1024]{1,0:T(8,128)S(1)}, u32[]{:S(2)}, u32[]{:S(2)}) %collective-permute-start.28) | collective-permute-done | bytes 131104 | tf_op jit(solution)/shard_map/ppermute | solution.py:19
  89.0 1.7 %collective-permute-start.29 = (bf16[32,1024]{1,0:T(8,128)(2,1)S(1)}, bf16[32,1024]{1,0:T(8,128)(2,1)S(1)}, u32[]{:S(2)}, u32[]{:S(2)}) collective-permute-start(bf16[32,1024]{1,0:T(8,128)(2,1)S(1)} %get-tuple-element.52), channel_id=1, source_target_pairs={{0,8},{1,9},{2,10},{3,11},{4,12},{5,13},{6,14},{7,15},{8,0},{9,1},... | collective-permute-start | bytes 196616 | tf_op jit(solution)/shard_map/ppermute | solution.py:19
  90.7 4.2 %collective-permute-done.29 = bf16[32,1024]{1,0:T(8,128)(2,1)S(1)} collective-permute-done((bf16[32,1024]{1,0:T(8,128)(2,1)S(1)}, bf16[32,1024]{1,0:T(8,128)(2,1)S(1)}, u32[]{:S(2)}, u32[]{:S(2)}) %collective-permute-start.29) | collective-permute-done | bytes 65568 | tf_op jit(solution)/shard_map/ppermute | solution.py:19
  94.9 2.0 %shard_map.95 = (f32[32,1024]{1,0:T(8,128)S(1)}, f32[32,1024]{1,0:T(8,128)S(1)}, f32[1,32]{1,0:T(1,128)S(1)}, f32[32,64]{1,0:T(8,128)S(1)}, f32[32,64]{1,0:T(8,128)S(1)}) custom-call(s32[5]{0:T(128)S(1)} %stack.23.marks_ref, f32[32,2048]{1,0:T(8,128)S(1)} %get-tuple-element.45.response_ref, f32[32,1024]{1,0:T(8,128)S(1)} %convert_add_fusion.part_ref, ...), custom_call_target="tpu_custom_call" | custom-call | flops 1000000000 | bytes 4194304 | tf_op jit(solution)/shard_map/pallas_call | solution.py:290
  96.9 2.6 %collective-permute-start.33 = (f32[1,32]{1,0:T(1,128)S(1)}, f32[1,32]{1,0:T(1,128)S(1)}, u32[]{:S(2)}, u32[]{:S(2)}) collective-permute-start(f32[1,32]{1,0:T(1,128)S(1)} %get-tuple-element.49), channel_id=1, source_target_pairs={{0,12},{1,13},{2,14},{3,15},{4,8},{5,9},{6,10},{7,11},{8,4},{9,5},... | collective-permute-start | bytes 392 | tf_op jit(solution)/shard_map/ppermute | solution.py:19
  99.5 1.8 %collective-permute-start.32 = (f32[1,32]{1,0:T(1,128)S(1)}, f32[1,32]{1,0:T(1,128)S(1)}, u32[]{:S(2)}, u32[]{:S(2)}) collective-permute-start(f32[1,32]{1,0:T(1,128)S(1)} %get-tuple-element.49), channel_id=1, source_target_pairs={{0,8},{1,9},{2,10},{3,11},{4,12},{5,13},{6,14},{7,15},{8,0},{9,1},... | collective-permute-start | bytes 392 | tf_op jit(solution)/shard_map/ppermute | solution.py:19
  101.4 0.5 collective-permute-start.37
  101.9 0.5 collective-permute-done.33
  102.3 0.7 collective-permute-done.31
  103.1 0.9 collective-permute-done.32
  104.0 1.2 %collective-permute-start.34 = (f32[1,32]{1,0:T(1,128)S(1)}, f32[1,32]{1,0:T(1,128)S(1)}, u32[]{:S(2)}, u32[]{:S(2)}) collective-permute-start(f32[1,32]{1,0:T(1,128)S(1)} %add_add_fusion), channel_id=1, source_target_pairs={{0,2},{1,3},{2,0},{3,1},{4,6},{5,7},{6,4},{7,5},{8,10},{9,11},{10,... | collective-permute-start | bytes 392 | tf_op jit(solution)/shard_map/ppermute | solution.py:19
  105.2 0.9 collective-permute-start.36
  106.1 1.4 %collective-permute-done.34 = f32[1,32]{1,0:T(1,128)S(1)} collective-permute-done((f32[1,32]{1,0:T(1,128)S(1)}, f32[1,32]{1,0:T(1,128)S(1)}, u32[]{:S(2)}, u32[]{:S(2)}) %collective-permute-start.34) | collective-permute-done | bytes 160 | tf_op jit(solution)/shard_map/ppermute | solution.py:19
  107.6 0.7 collective-permute-done.36
  108.2 1.2 %shard_map.96 = f32[64,64]{1,0:T(8,128)} custom-call(s32[5]{0:T(128)S(1)} %stack.23.marks_ref, f32[32,64]{1,0:T(8,128)S(1)} %get-tuple-element.47.mine_ref, f32[32,64]{1,0:T(8,128)S(1)} %collective-permute-done.30.other_ref), custom_call_target="tpu_custom_call" | custom-call | flops 1000000000 | bytes 4194304 | tf_op jit(solution)/shard_map/pallas_call | solution.py:290
  109.5 1.4 %shard_map.97 = f32[64,1024]{1,0:T(8,128)} custom-call(s32[5]{0:T(128)S(1)} %stack.23.marks_ref, f32[1,32]{1,0:T(1,128)S(1)} %add.85.sum_mine_ref, f32[1,32]{1,0:T(1,128)S(1)} %add.86.sum_other_ref, f32[32,1024]{1,0:T(8,128)S(1)} %get-tuple-element.50.mine_ref, f32[32,1024]{1,0:T(8,128)S(1)} %collective-permute-done.37.other_ref), custom_call_target="tpu_custom_call" | custom-call | flops 1000000000 | bytes 4194304 | tf_op jit(solution)/shard_map/pallas_call | solution.py:290
  (67 shorter events, 3.9 us)
Async XLA Ops:
  0.6 11.7 %collective-permute-start.5 = (bf16[48,1024]{1,0:T(8,128)(2,1)}, bf16[48,1024]{1,0:T(8,128)(2,1)S(1)}, u32[]{:S(2)}, u32[]{:S(2)}) collective-permute-start(bf16[48,1024]{1,0:T(8,128)(2,1)} %bitcast.32), channel_id=1, source_target_pairs={{0,2},{1,3},{2,0},{3,1},{4,6},{5,7},{6,4},{7,5},{8,10},{9,11},{10,... | collective-permute-start | bytes 294920 | tf_op jit(solution)/shard_map/ppermute | solution.py:19
  3.7 26.4 %collective-permute-start = (bf16[48,1024]{1,0:T(8,128)(2,1)}, bf16[48,1024]{1,0:T(8,128)(2,1)S(1)}, u32[]{:S(2)}, u32[]{:S(2)}) collective-permute-start(bf16[48,1024]{1,0:T(8,128)(2,1)} %bitcast.33), channel_id=1, source_target_pairs={{0,1},{1,0},{2,3},{3,2},{4,5},{5,4},{6,7},{7,6},{8,9},{9,8},{10,11... | collective-permute-start | bytes 294920 | tf_op jit(solution)/shard_map/ppermute | solution.py:19
  3.7 6.2 %collective-permute-start.4 = (bf16[64,1024]{1,0:T(8,128)(2,1)}, bf16[64,1024]{1,0:T(8,128)(2,1)}, u32[]{:S(2)}, u32[]{:S(2)}) collective-permute-start(bf16[64,1024]{1,0:T(8,128)(2,1)} %bitcast.29), channel_id=1, source_target_pairs={{0,2},{1,3},{2,0},{3,1},{4,6},{5,7},{6,4},{7,5},{8,10},{9,11},{10,... | collective-permute-start | bytes 393224 | tf_op jit(solution)/shard_map/ppermute | solution.py:19
  3.9 26.8 %collective-permute-start.1 = (bf16[64,1024]{1,0:T(8,128)(2,1)}, bf16[64,1024]{1,0:T(8,128)(2,1)S(1)}, u32[]{:S(2)}, u32[]{:S(2)}) collective-permute-start(bf16[64,1024]{1,0:T(8,128)(2,1)} %bitcast.30), channel_id=1, source_target_pairs={{0,1},{1,0},{2,3},{3,2},{4,5},{5,4},{6,7},{7,6},{8,9},{9,8},{10,11... | collective-permute-start | bytes 393224 | tf_op jit(solution)/shard_map/ppermute | solution.py:19
  4.2 69.8 %collective-permute-start.26 = (bf16[1024,1024]{1,0:T(8,128)(2,1)}, bf16[1024,1024]{1,0:T(8,128)(2,1)S(1)}, u32[]{:S(2)}, u32[]{:S(2)}) collective-permute-start(bf16[1024,1024]{1,0:T(8,128)(2,1)} %refs_0_.3), channel_id=1, source_target_pairs={{0,1},{1,0},{2,3},{3,2},{4,5},{5,4},{6,7},{7,6},{8,9},{9,8},{10,11... | collective-permute-start | bytes 6291464 | tf_op jit(solution)/shard_map/ppermute | solution.py:19
  5.9 1.2 %copy-start.2 = (bf16[1024,512]{1,0:T(8,128)(2,1)S(1)}, bf16[1024,512]{1,0:T(8,128)(2,1)}, u32[]{:S(2)}) copy-start(bf16[1024,512]{1,0:T(8,128)(2,1)} %cond_ref.1) | copy-start | bytes 3145732
  7.4 1.6 %copy-start = (bf16[1024,1024]{1,0:T(8,128)(2,1)S(1)}, bf16[1024,1024]{1,0:T(8,128)(2,1)}, u32[]{:S(2)}) copy-start(bf16[1024,1024]{1,0:T(8,128)(2,1)} %refs_0_.3) | copy-start | bytes 6291460
  9.9 8.3 %collective-permute-start.6 = (bf16[1024,128]{1,0:T(8,128)(2,1)S(1)}, bf16[1024,128]{1,0:T(8,128)(2,1)S(1)}, u32[]{:S(2)}, u32[]{:S(2)}) collective-permute-start(bf16[1024,128]{1,0:T(8,128)(2,1)S(1)} %get-tuple-element.30), channel_id=1, source_target_pairs={{0,2},{1,3},{2,0},{3,1},{4,6},{5,7},{6,4},{7,5},{8,10},{9,11},{10,... | collective-permute-start | bytes 786440 | tf_op jit(solution)/shard_map/ppermute | solution.py:19
  12.3 18.4 %collective-permute-start.2 = (bf16[1024,128]{1,0:T(8,128)(2,1)S(1)}, bf16[1024,128]{1,0:T(8,128)(2,1)S(1)}, u32[]{:S(2)}, u32[]{:S(2)}) collective-permute-start(bf16[1024,128]{1,0:T(8,128)(2,1)S(1)} %get-tuple-element.27.refs_0_), channel_id=1, source_target_pairs={{0,1},{1,0},{2,3},{3,2},{4,5},{5,4},{6,7},{7,6},{8,9},{9,8},{10,11... | collective-permute-start | bytes 786440 | tf_op jit(solution)/shard_map/ppermute | solution.py:19
  18.3 1.6 %collective-permute-start.7 = (bf16[64,1024]{1,0:T(8,128)(2,1)}, bf16[64,1024]{1,0:T(8,128)(2,1)S(1)}, u32[]{:S(2)}, u32[]{:S(2)}) collective-permute-start(bf16[64,1024]{1,0:T(8,128)(2,1)} %collective-permute-done.4), channel_id=1, source_target_pairs={{0,1},{1,0},{2,3},{3,2},{4,5},{5,4},{6,7},{7,6},{8,9},{9,8},{10,11... | collective-permute-start | bytes 393224 | tf_op jit(solution)/shard_map/ppermute | solution.py:19
  19.8 1.3 %collective-permute-start.8 = (bf16[48,1024]{1,0:T(8,128)(2,1)S(1)}, bf16[48,1024]{1,0:T(8,128)(2,1)S(1)}, u32[]{:S(2)}, u32[]{:S(2)}) collective-permute-start(bf16[48,1024]{1,0:T(8,128)(2,1)S(1)} %collective-permute-done.5.refs_5_), channel_id=1, source_target_pairs={{0,1},{1,0},{2,3},{3,2},{4,5},{5,4},{6,7},{7,6},{8,9},{9,8},{10,11... | collective-permute-start | bytes 294920 | tf_op jit(solution)/shard_map/ppermute | solution.py:19
  21.1 8.4 %collective-permute-start.12 = (bf16[1024,128]{1,0:T(8,128)(2,1)S(1)}, bf16[1024,128]{1,0:T(8,128)(2,1)S(1)}, u32[]{:S(2)}, u32[]{:S(2)}) collective-permute-start(bf16[1024,128]{1,0:T(8,128)(2,1)S(1)} %get-tuple-element.35), channel_id=1, source_target_pairs={{0,2},{1,3},{2,0},{3,1},{4,6},{5,7},{6,4},{7,5},{8,10},{9,11},{10,... | collective-permute-start | bytes 786440 | tf_op jit(solution)/shard_map/ppermute | solution.py:19
  23.6 7.4 %copy-start.3 = (bf16[1024,64]{0,1:T(8,128)(2,1)S(1)}, bf16[1024,64]{0,1:T(8,128)(2,1)}, u32[]{:S(2)}) copy-start(bf16[1024,64]{0,1:T(8,128)(2,1)} %param.8) | copy-start | bytes 393220
  23.7 7.4 %copy-start.4 = (bf16[1024,48]{0,1:T(8,128)(2,1)S(1)}, bf16[1024,48]{0,1:T(8,128)(2,1)}, u32[]{:S(2)}) copy-start(bf16[1024,48]{0,1:T(8,128)(2,1)} %param.6) | copy-start | bytes 294916
  29.5 1.5 %collective-permute-start.3 = (bf16[1024,128]{1,0:T(8,128)(2,1)S(1)}, bf16[1024,128]{1,0:T(8,128)(2,1)S(1)}, u32[]{:S(2)}, u32[]{:S(2)}) collective-permute-start(bf16[1024,128]{1,0:T(8,128)(2,1)S(1)} %get-tuple-element.28.refs_1_), channel_id=1, source_target_pairs={{0,1},{1,0},{2,3},{3,2},{4,5},{5,4},{6,7},{7,6},{8,9},{9,8},{10,11... | collective-permute-start | bytes 786440 | tf_op jit(solution)/shard_map/ppermute | solution.py:19
  30.1 4.0 %collective-permute-start.9 = (bf16[1024,128]{1,0:T(8,128)(2,1)S(1)}, bf16[1024,128]{1,0:T(8,128)(2,1)S(1)}, u32[]{:S(2)}, u32[]{:S(2)}) collective-permute-start(bf16[1024,128]{1,0:T(8,128)(2,1)S(1)} %collective-permute-done.6.refs_4_), channel_id=1, source_target_pairs={{0,1},{1,0},{2,3},{3,2},{4,5},{5,4},{6,7},{7,6},{8,9},{9,8},{10,11... | collective-permute-start | bytes 786440 | tf_op jit(solution)/shard_map/ppermute | solution.py:19
  30.6 5.9 %collective-permute-start.13 = (bf16[1024,128]{1,0:T(8,128)(2,1)S(1)}, bf16[1024,128]{1,0:T(8,128)(2,1)S(1)}, u32[]{:S(2)}, u32[]{:S(2)}) collective-permute-start(bf16[1024,128]{1,0:T(8,128)(2,1)S(1)} %collective-permute-done.12.refs_5_), channel_id=1, source_target_pairs={{0,1},{1,0},{2,3},{3,2},{4,5},{5,4},{6,7},{7,6},{8,9},{9,8},{10,11... | collective-permute-start | bytes 786440 | tf_op jit(solution)/shard_map/ppermute | solution.py:19
  34.7 6.0 %collective-permute-start.10 = (bf16[384,128]{1,0:T(8,128)(2,1)S(1)}, bf16[384,128]{1,0:T(8,128)(2,1)S(1)}, u32[]{:S(2)}, u32[]{:S(2)}) collective-permute-start(bf16[384,128]{1,0:T(8,128)(2,1)S(1)} %get-tuple-element.57), channel_id=1, source_target_pairs={{0,4},{1,5},{2,6},{3,7},{4,0},{5,1},{6,2},{7,3},{8,12},{9,13},{10,... | collective-permute-start | bytes 294920 | tf_op jit(solution)/shard_map/ppermute | solution.py:19
  37.2 6.4 %collective-permute-start.14 = (bf16[384,128]{1,0:T(8,128)(2,1)S(1)}, bf16[384,128]{1,0:T(8,128)(2,1)S(1)}, u32[]{:S(2)}, u32[]{:S(2)}) collective-permute-start(bf16[384,128]{1,0:T(8,128)(2,1)S(1)} %get-tuple-element.55), channel_id=1, source_target_pairs={{0,4},{1,5},{2,6},{3,7},{4,0},{5,1},{6,2},{7,3},{8,12},{9,13},{10,... | collective-permute-start | bytes 294920 | tf_op jit(solution)/shard_map/ppermute | solution.py:19
  37.5 11.2 %collective-permute-start.16 = (bf16[384,128]{1,0:T(8,128)(2,1)S(1)}, bf16[384,128]{1,0:T(8,128)(2,1)S(1)}, u32[]{:S(2)}, u32[]{:S(2)}) collective-permute-start(bf16[384,128]{1,0:T(8,128)(2,1)S(1)} %get-tuple-element.56), channel_id=1, source_target_pairs={{0,4},{1,5},{2,6},{3,7},{4,0},{5,1},{6,2},{7,3},{8,12},{9,13},{10,... | collective-permute-start | bytes 294920 | tf_op jit(solution)/shard_map/ppermute | solution.py:19
  39.3 10.8 %collective-permute-start.18 = (bf16[384,128]{1,0:T(8,128)(2,1)S(1)}, bf16[384,128]{1,0:T(8,128)(2,1)S(1)}, u32[]{:S(2)}, u32[]{:S(2)}) collective-permute-start(bf16[384,128]{1,0:T(8,128)(2,1)S(1)} %get-tuple-element.54), channel_id=1, source_target_pairs={{0,4},{1,5},{2,6},{3,7},{4,0},{5,1},{6,2},{7,3},{8,12},{9,13},{10,... | collective-permute-start | bytes 294920 | tf_op jit(solution)/shard_map/ppermute | solution.py:19
  40.8 11.6 %collective-permute-start.11 = (bf16[384,128]{1,0:T(8,128)(2,1)S(1)}, bf16[384,128]{1,0:T(8,128)(2,1)S(1)}, u32[]{:S(2)}, u32[]{:S(2)}) collective-permute-start(bf16[384,128]{1,0:T(8,128)(2,1)S(1)} %get-tuple-element.33), channel_id=1, source_target_pairs={{0,8},{1,9},{2,10},{3,11},{4,12},{5,13},{6,14},{7,15},{8,0},{9,1},... | collective-permute-start | bytes 294920 | tf_op jit(solution)/shard_map/ppermute | solution.py:19
  43.7 14.6 %collective-permute-start.15 = (bf16[384,128]{1,0:T(8,128)(2,1)S(1)}, bf16[384,128]{1,0:T(8,128)(2,1)S(1)}, u32[]{:S(2)}, u32[]{:S(2)}) collective-permute-start(bf16[384,128]{1,0:T(8,128)(2,1)S(1)} %get-tuple-element.38), channel_id=1, source_target_pairs={{0,8},{1,9},{2,10},{3,11},{4,12},{5,13},{6,14},{7,15},{8,0},{9,1},... | collective-permute-start | bytes 294920 | tf_op jit(solution)/shard_map/ppermute | solution.py:19
  48.7 11.5 %collective-permute-start.17 = (bf16[384,128]{1,0:T(8,128)(2,1)S(1)}, bf16[384,128]{1,0:T(8,128)(2,1)S(1)}, u32[]{:S(2)}, u32[]{:S(2)}) collective-permute-start(bf16[384,128]{1,0:T(8,128)(2,1)S(1)} %get-tuple-element.40), channel_id=1, source_target_pairs={{0,8},{1,9},{2,10},{3,11},{4,12},{5,13},{6,14},{7,15},{8,0},{9,1},... | collective-permute-start | bytes 294920 | tf_op jit(solution)/shard_map/ppermute | solution.py:19
  50.1 11.1 %collective-permute-start.19 = (bf16[384,128]{1,0:T(8,128)(2,1)S(1)}, bf16[384,128]{1,0:T(8,128)(2,1)S(1)}, u32[]{:S(2)}, u32[]{:S(2)}) collective-permute-start(bf16[384,128]{1,0:T(8,128)(2,1)S(1)} %get-tuple-element.42), channel_id=1, source_target_pairs={{0,8},{1,9},{2,10},{3,11},{4,12},{5,13},{6,14},{7,15},{8,0},{9,1},... | collective-permute-start | bytes 294920 | tf_op jit(solution)/shard_map/ppermute | solution.py:19
  52.5 14.7 %collective-permute-start.21 = (bf16[384,128]{1,0:T(8,128)(2,1)S(1)}, bf16[384,128]{1,0:T(8,128)(2,1)S(1)}, u32[]{:S(2)}, u32[]{:S(2)}) collective-permute-start(bf16[384,128]{1,0:T(8,128)(2,1)S(1)} %shard_map.80.refs_0_), channel_id=1, source_target_pairs={{0,4},{1,5},{2,6},{3,7},{4,0},{5,1},{6,2},{7,3},{8,12},{9,13},{10,... | collective-permute-start | bytes 294920 | tf_op jit(solution)/shard_map/ppermute | solution.py:19
  58.3 10.7 %collective-permute-start.22 = (bf16[384,128]{1,0:T(8,128)(2,1)S(1)}, bf16[384,128]{1,0:T(8,128)(2,1)S(1)}, u32[]{:S(2)}, u32[]{:S(2)}) collective-permute-start(bf16[384,128]{1,0:T(8,128)(2,1)S(1)} %shard_map.82.refs_1_), channel_id=1, source_target_pairs={{0,4},{1,5},{2,6},{3,7},{4,0},{5,1},{6,2},{7,3},{8,12},{9,13},{10,... | collective-permute-start | bytes 294920 | tf_op jit(solution)/shard_map/ppermute | solution.py:19
  60.2 8.8 %collective-permute-start.23 = (bf16[384,128]{1,0:T(8,128)(2,1)S(1)}, bf16[384,128]{1,0:T(8,128)(2,1)S(1)}, u32[]{:S(2)}, u32[]{:S(2)}) collective-permute-start(bf16[384,128]{1,0:T(8,128)(2,1)S(1)} %shard_map.84.refs_2_), channel_id=1, source_target_pairs={{0,4},{1,5},{2,6},{3,7},{4,0},{5,1},{6,2},{7,3},{8,12},{9,13},{10,... | collective-permute-start | bytes 294920 | tf_op jit(solution)/shard_map/ppermute | solution.py:19
  61.3 7.7 %collective-permute-start.24 = (bf16[384,128]{1,0:T(8,128)(2,1)S(1)}, bf16[384,128]{1,0:T(8,128)(2,1)S(1)}, u32[]{:S(2)}, u32[]{:S(2)}) collective-permute-start(bf16[384,128]{1,0:T(8,128)(2,1)S(1)} %shard_map.86.refs_3_), channel_id=1, source_target_pairs={{0,4},{1,5},{2,6},{3,7},{4,0},{5,1},{6,2},{7,3},{8,12},{9,13},{10,... | collective-permute-start | bytes 294920 | tf_op jit(solution)/shard_map/ppermute | solution.py:19
  67.2 7.5 %collective-permute-start.20 = (f32[16,2048]{1,0:T(8,128)S(1)}, f32[16,2048]{1,0:T(8,128)S(1)}, u32[]{:S(2)}, u32[]{:S(2)}) collective-permute-start(f32[16,2048]{1,0:T(8,128)S(1)} %shard_map.89), channel_id=1, source_target_pairs={{0,2},{1,3},{2,0},{3,1},{4,6},{5,7},{6,4},{7,5},{8,10},{9,11},{10,... | collective-permute-start | bytes 393224 | tf_op jit(solution)/shard_map/ppermute | solution.py:19
  71.3 5.0 %collective-permute-start.25 = (f32[16,2048]{1,0:T(8,128)S(1)}, f32[16,2048]{1,0:T(8,128)S(1)}, u32[]{:S(2)}, u32[]{:S(2)}) collective-permute-start(f32[16,2048]{1,0:T(8,128)S(1)} %shard_map.91), channel_id=1, source_target_pairs={{0,2},{1,3},{2,0},{3,1},{4,6},{5,7},{6,4},{7,5},{8,10},{9,11},{10,... | collective-permute-start | bytes 393224 | tf_op jit(solution)/shard_map/ppermute | solution.py:19
  76.3 18.6 %copy-start.1 = (bf16[1024,1024]{1,0:T(8,128)(2,1)S(1)}, bf16[1024,1024]{1,0:T(8,128)(2,1)}, u32[]{:S(2)}) copy-start(bf16[1024,1024]{1,0:T(8,128)(2,1)} %refs_0_.3) | copy-start | bytes 6291460
  78.2 5.0 %collective-permute-start.27 = (f32[32,1024]{1,0:T(8,128)S(1)}, f32[32,1024]{1,0:T(8,128)S(1)}, u32[]{:S(2)}, u32[]{:S(2)}) collective-permute-start(f32[32,1024]{1,0:T(8,128)S(1)} %get-tuple-element.46), channel_id=1, source_target_pairs={{0,2},{1,3},{2,0},{3,1},{4,6},{5,7},{6,4},{7,5},{8,10},{9,11},{10,... | collective-permute-start | bytes 393224 | tf_op jit(solution)/shard_map/ppermute | solution.py:19
  83.2 5.7 %collective-permute-start.28 = (f32[32,1024]{1,0:T(8,128)S(1)}, f32[32,1024]{1,0:T(8,128)S(1)}, u32[]{:S(2)}, u32[]{:S(2)}) collective-permute-start(f32[32,1024]{1,0:T(8,128)S(1)} %add.79), channel_id=1, source_target_pairs={{0,4},{1,5},{2,6},{3,7},{4,0},{5,1},{6,2},{7,3},{8,12},{9,13},{10,... | collective-permute-start | bytes 393224 | tf_op jit(solution)/shard_map/ppermute | solution.py:19
  89.0 5.9 %collective-permute-start.29 = (bf16[32,1024]{1,0:T(8,128)(2,1)S(1)}, bf16[32,1024]{1,0:T(8,128)(2,1)S(1)}, u32[]{:S(2)}, u32[]{:S(2)}) collective-permute-start(bf16[32,1024]{1,0:T(8,128)(2,1)S(1)} %get-tuple-element.52), channel_id=1, source_target_pairs={{0,8},{1,9},{2,10},{3,11},{4,12},{5,13},{6,14},{7,15},{8,0},{9,1},... | collective-permute-start | bytes 196616 | tf_op jit(solution)/shard_map/ppermute | solution.py:19
  96.9 5.4 %collective-permute-start.33 = (f32[1,32]{1,0:T(1,128)S(1)}, f32[1,32]{1,0:T(1,128)S(1)}, u32[]{:S(2)}, u32[]{:S(2)}) collective-permute-start(f32[1,32]{1,0:T(1,128)S(1)} %get-tuple-element.49), channel_id=1, source_target_pairs={{0,12},{1,13},{2,14},{3,15},{4,8},{5,9},{6,10},{7,11},{8,4},{9,5},... | collective-permute-start | bytes 392 | tf_op jit(solution)/shard_map/ppermute | solution.py:19
  99.5 3.6 %collective-permute-start.31 = (f32[1,32]{1,0:T(1,128)S(1)}, f32[1,32]{1,0:T(1,128)S(1)}, u32[]{:S(2)}, u32[]{:S(2)}) collective-permute-start(f32[1,32]{1,0:T(1,128)S(1)} %get-tuple-element.49), channel_id=1, source_target_pairs={{0,4},{1,5},{2,6},{3,7},{4,0},{5,1},{6,2},{7,3},{8,12},{9,13},{10,... | collective-permute-start | bytes 392 | tf_op jit(solution)/shard_map/ppermute | solution.py:19
  99.5 4.5 %collective-permute-start.32 = (f32[1,32]{1,0:T(1,128)S(1)}, f32[1,32]{1,0:T(1,128)S(1)}, u32[]{:S(2)}, u32[]{:S(2)}) collective-permute-start(f32[1,32]{1,0:T(1,128)S(1)} %get-tuple-element.49), channel_id=1, source_target_pairs={{0,8},{1,9},{2,10},{3,11},{4,12},{5,13},{6,14},{7,15},{8,0},{9,1},... | collective-permute-start | bytes 392 | tf_op jit(solution)/shard_map/ppermute | solution.py:19
  101.4 6.9 %collective-permute-start.30 = (f32[32,64]{1,0:T(8,128)S(1)}, f32[32,64]{1,0:T(8,128)S(1)}, u32[]{:S(2)}, u32[]{:S(2)}) collective-permute-start(f32[32,64]{1,0:T(8,128)S(1)} %get-tuple-element.48), channel_id=1, source_target_pairs={{0,1},{1,0},{2,3},{3,2},{4,5},{5,4},{6,7},{7,6},{8,9},{9,8},{10,11... | collective-permute-start | bytes 24584 | tf_op jit(solution)/shard_map/ppermute | solution.py:19
  101.4 8.1 %collective-permute-start.37 = (f32[32,1024]{1,0:T(8,128)S(1)}, f32[32,1024]{1,0:T(8,128)S(1)}, u32[]{:S(2)}, u32[]{:S(2)}) collective-permute-start(f32[32,1024]{1,0:T(8,128)S(1)} %get-tuple-element.51), channel_id=1, source_target_pairs={{0,1},{1,0},{2,3},{3,2},{4,5},{5,4},{6,7},{7,6},{8,9},{9,8},{10,11... | collective-permute-start | bytes 393224 | tf_op jit(solution)/shard_map/ppermute | solution.py:19
  104.0 3.6 %collective-permute-start.34 = (f32[1,32]{1,0:T(1,128)S(1)}, f32[1,32]{1,0:T(1,128)S(1)}, u32[]{:S(2)}, u32[]{:S(2)}) collective-permute-start(f32[1,32]{1,0:T(1,128)S(1)} %add_add_fusion), channel_id=1, source_target_pairs={{0,2},{1,3},{2,0},{3,1},{4,6},{5,7},{6,4},{7,5},{8,10},{9,11},{10,... | collective-permute-start | bytes 392 | tf_op jit(solution)/shard_map/ppermute | solution.py:19
  105.2 2.3 %collective-permute-start.35 = (f32[1,32]{1,0:T(1,128)S(1)}, f32[1,32]{1,0:T(1,128)S(1)}, u32[]{:S(2)}, u32[]{:S(2)}) collective-permute-start(f32[1,32]{1,0:T(1,128)S(1)} %add_add_fusion), channel_id=1, source_target_pairs={{0,1},{1,0},{2,3},{3,2},{4,5},{5,4},{6,7},{7,6},{8,9},{9,8},{10,11... | collective-permute-start | bytes 392 | tf_op jit(solution)/shard_map/ppermute | solution.py:19
  105.2 3.0 %collective-permute-start.36 = (f32[1,32]{1,0:T(1,128)S(1)}, f32[1,32]{1,0:T(1,128)S(1)}, u32[]{:S(2)}, u32[]{:S(2)}) collective-permute-start(f32[1,32]{1,0:T(1,128)S(1)} %add_add_fusion), channel_id=1, source_target_pairs={{0,3},{1,2},{2,1},{3,0},{4,7},{5,6},{6,5},{7,4},{8,11},{9,10},{10,... | collective-permute-start | bytes 392 | tf_op jit(solution)/shard_map/ppermute | solution.py:19
